TPU v7x, 8 devices: a whole 2x2x1 slice. The times are simulated.
8 devices in a mesh: rep: 1 (over z), yz: 2 (over y), x: 4 (over x, core).
Axes of the slice: x: 2, y: 2, z: 1, core: 2. Of those that a mesh axis runs over, the one named last changes fastest.
Arguments:
- hidden: bfloat16 [256, 1536], P('rep', ('x', 'yz'))
- norm_gain: bfloat16 [2, 1536], P(None, 'x')
- w_attn: bfloat16 [2, 1536, 2048], P(None, 'x', 'yz')
- w_mlp: bfloat16 [2, 1536, 2, 8960], P(None, 'x', None, 'yz')
- w_out: bfloat16 [2, 1536, 1536], P(None, 'yz', 'x')
- w_down: bfloat16 [2, 8960, 1536], P(None, 'yz', 'x')
- k_cache: bfloat16 [2, 256, 2, 1024, 128], P(None, ('rep', 'x', 'yz'))
- v_cache: bfloat16 [2, 256, 2, 1024, 128], P(None, ('rep', 'x', 'yz'))
- lengths: int32 [256], P(('rep', 'x', 'yz'))
Outputs:
- output 1: bfloat16 [256, 1536], P('rep', ('x', 'yz'))
- output 2: bfloat16 [2, 256, 2, 1024, 128], P(None, ('rep', 'x', 'yz'))
- output 3: bfloat16 [2, 256, 2, 1024, 128], P(None, ('rep', 'x', 'yz'))
All inputs are finite; a program needn't handle non-finite values.
Results may differ from a plain program's by a relative error of at most 0.0192237.
Values are sent between devices in bfloat16 or wider.
A program may use at most 1 GiB of HBM per device.

v0:
```python
import jax
import jax.numpy as jnp
from jax import lax
from jax.sharding import PartitionSpec as P

NORM_EPS = 1e-5


def attend(attn_z, keys_l, vals_l, lengths, kv_heads, head_dim):
    num_seqs = attn_z.shape[0]
    per_group = attn_z.shape[1] // (kv_heads * head_dim)
    qkv_rows = attn_z.reshape(num_seqs, kv_heads, per_group, head_dim)
    queries = qkv_rows[:, :, :per_group - 2]
    key_new = qkv_rows[:, :, per_group - 2]
    val_new = qkv_rows[:, :, per_group - 1]
    score_scale = head_dim ** -0.5
    positions = jnp.arange(keys_l.shape[2])
    visible = positions[None, None, None, :] < lengths[:, None, None, None]
    score_old = jnp.einsum('bgqd,bgsd->bgqs', queries, keys_l, preferred_element_type=jnp.float32) * score_scale
    score_old = jnp.where(visible, score_old, -1e30)
    score_new = jnp.einsum('bgqd,bgd->bgq', queries, key_new, preferred_element_type=jnp.float32) * score_scale
    top_score = jnp.maximum(jnp.max(score_old, axis=-1), score_new)
    exp_old = jnp.exp(score_old - top_score[..., None])
    exp_new = jnp.exp(score_new - top_score)
    denominator = jnp.sum(exp_old, axis=-1) + exp_new
    prob_old = (exp_old / denominator[..., None]).astype(jnp.bfloat16)
    prob_new = (exp_new / denominator).astype(jnp.bfloat16)
    attn_out = jnp.einsum('bgqs,bgsd->bgqd', prob_old, vals_l, preferred_element_type=jnp.float32)
    attn_out = attn_out + prob_new.astype(jnp.float32)[..., None] * val_new.astype(jnp.float32)[:, :, None, :]
    return attn_out.astype(jnp.bfloat16).reshape(num_seqs, -1), key_new, val_new


def write_caches(k_cache, v_cache, new_keys, new_vals, lengths):
    positions = jnp.arange(k_cache.shape[3])
    slot_hit = (positions[None, :] == lengths[:, None])[None, :, None, :, None]
    keys_out = jnp.where(slot_hit, jnp.stack(new_keys)[:, :, :, None, :], k_cache)
    vals_out = jnp.where(slot_hit, jnp.stack(new_vals)[:, :, :, None, :], v_cache)
    return keys_out, vals_out


def solution(mesh):
    x_size = mesh.shape['x']
    seq_axes = ('rep', 'x', 'yz')
    hidden_spec = P('rep', ('x', 'yz'))
    cache_spec = P(None, seq_axes, None, None, None)
    in_specs = (hidden_spec, P(None, 'x'), P(None, 'x', 'yz'), P(None, 'x', None, 'yz'), P(None, 'yz', 'x'), P(None, 'yz', 'x'), cache_spec, cache_spec, P(seq_axes))
    out_specs = (hidden_spec, cache_spec, cache_spec)

    def device_step(hidden, norm_gain, w_attn, w_mlp, w_out, w_down, k_cache, v_cache, lengths):
        layers = w_attn.shape[0]
        model_dim = w_attn.shape[1] * x_size
        kv_heads = k_cache.shape[2]
        head_dim = k_cache.shape[4]
        num_seqs = hidden.shape[0]
        current = hidden
        new_keys = []
        new_vals = []
        for layer_idx in range(layers):
            row_block = lax.all_gather(current, 'yz', axis=1, tiled=True)
            row_f = row_block.astype(jnp.float32)
            sq_sum = lax.psum(jnp.sum(row_f * row_f, axis=1, keepdims=True), 'x')
            inv_rms = lax.rsqrt(sq_sum / model_dim + NORM_EPS)
            normed = (row_f * inv_rms * norm_gain[layer_idx].astype(jnp.float32)).astype(jnp.bfloat16)
            attn_part = jnp.dot(normed, w_attn[layer_idx], preferred_element_type=jnp.float32).astype(jnp.bfloat16)
            mlp_part = jnp.einsum('be,etf->btf', normed, w_mlp[layer_idx], preferred_element_type=jnp.float32).astype(jnp.bfloat16)
            merged = jnp.concatenate([attn_part, mlp_part.reshape(num_seqs, -1)], axis=1)
            summed = lax.psum_scatter(merged, 'x', scatter_dimension=0, tiled=True)
            attn_cols = attn_part.shape[1]
            attn_rows = lax.all_to_all(summed[:, :attn_cols], 'yz', 0, 1, tiled=True)
            attn_out, key_new, val_new = attend(attn_rows, k_cache[layer_idx], v_cache[layer_idx], lengths, kv_heads, head_dim)
            new_keys.append(key_new)
            new_vals.append(val_new)
            attn_back = lax.all_to_all(attn_out, 'yz', 1, 0, tiled=True)
            attn_full = lax.all_gather(attn_back, 'x', axis=0, tiled=True)
            gate_up = summed[:, attn_cols:].reshape(summed.shape[0], 2, -1).astype(jnp.float32)
            mixed = (jax.nn.silu(gate_up[:, 0]) * gate_up[:, 1]).astype(jnp.bfloat16)
            mixed_full = lax.all_gather(mixed, 'x', axis=0, tiled=True)
            update = jnp.dot(attn_full, w_out[layer_idx], preferred_element_type=jnp.float32) + jnp.dot(mixed_full, w_down[layer_idx], preferred_element_type=jnp.float32)
            reduced = lax.psum_scatter(update.astype(jnp.bfloat16), 'yz', scatter_dimension=1, tiled=True)
            current = (current.astype(jnp.float32) + reduced.astype(jnp.float32)).astype(jnp.bfloat16)
        keys_out, vals_out = write_caches(k_cache, v_cache, new_keys, new_vals, lengths)
        return current, keys_out, vals_out

    return jax.shard_map(device_step, mesh=mesh, in_specs=in_specs, out_specs=out_specs, check_vma=False)
```

profile of v0, /device:TPU:0, one launch (start us, length us, event | category | flops | bytes accessed | tf_op | source)
XLA Modules:
  0.0 362.3 jit_solution(13059013570256217613)
XLA Ops:
  8.6 6.8 %all_gather.18 = bf16[256,384]{0,1:T(8,128)(2,1)S(1)} all-gather(bf16[256,192]{0,1:T(8,128)(2,1)} %param.9), channel_id=1, replica_groups=mesh['rep'=1,'yz'=2,'x'=4] {'yz'}, dimensions={1}, use_global_device_ids=true | all-gather | bytes 294912 | tf_op jit(solution)/shard_map/all_gather | solution.py:59
  15.4 5.7 %psum.14 = f32[256,1]{0,1:T(1,128)S(1)} all-reduce(f32[256,1]{0,1:T(1,128)S(1)} %bitcast.151), channel_id=1, replica_groups=mesh['rep'=1,'yz'=2,'x'=4] {'x'}, use_global_device_ids=true, to_apply=%region_1.0 | all-reduce | flops 256 | bytes 2048 | tf_op jit(solution)/shard_map/psum | solution.py:61
  23.1 11.9 %fusion.85 = (bf16[1,384,2,4480]{3,2,1,0:T(2,128)(2,1)S(1)}, bf16[1,384,2,4480]{3,2,1,0:T(2,128)(2,1)}) fusion(bf16[2,384,2,4480]{3,2,1,0:T(2,128)(2,1)} %param.12), kind=kLoop, calls=%fused_computation.125 | loop fusion | bytes 27525120 | tf_op jit(solution)/shard_map/slice | solution.py:65
  35.0 4.8 %convolution_convert_fusion.1 = bf16[256,2,4480]{2,0,1:T(8,128)(2,1)} fusion(bf16[1,384,2,4480]{3,2,1,0:T(2,128)(2,1)S(1)} %get-tuple-element.5, bf16[256,384]{0,1:T(8,128)(2,1)S(1)} %all_gather.18, f32[384]{0:T(512)S(1)} %get-tuple-element.4, f32[256]{0:T(256)S(1)} %bitcast.148), kind=kOutput, calls=%fused_computation.15 | convolution fusion | flops 1764294656 | bytes 11667968 | tf_op jit(solution)/shard_map/be,etf->btf/dot_general | solution.py:65
  39.8 6.5 %copy.138 = bf16[256,2,4480]{0,2,1:T(8,128)(2,1)} copy(bf16[256,2,4480]{2,0,1:T(8,128)(2,1)} %convolution_convert_fusion.1) | data formatting | bytes 9175040 | tf_op jit(solution)/shard_map/convert_element_type | solution.py:65
  46.3 6.8 %pad_maximum_fusion = bf16[256,9984]{0,1:T(8,128)(2,1)} fusion(bf16[256,8960]{0,1:T(8,128)(2,1)} %bitcast.128, bf16[256,1024]{0,1:T(8,128)(2,1)S(1)} %copy.139), kind=kLoop, calls=%fused_computation.18 | loop fusion | flops 10223616 | bytes 10223616 | tf_op jit(solution)/shard_map/concatenate | solution.py:66
  53.2 7.7 %copy.172 = bf16[256,9984]{1,0:T(8,128)(2,1)} copy(bf16[256,9984]{0,1:T(8,128)(2,1)} %pad_maximum_fusion) | data formatting | bytes 10223616
  61.7 44.8 %reduce-scatter.13.cloned.1.call-done = bf16[64,9984]{1,0:T(8,128)(2,1)} async-done(((bf16[256,9984]{1,0:T(8,128)(2,1)}), bf16[64,9984]{1,0:T(8,128)(2,1)}) %reduce-scatter.13.cloned.1.call-update) | async-done | bytes 1277968 | tf_op jit(solution)/shard_map/reduce_scatter | solution.py:67
  121.2 8.2 %fusion.18 = (f32[32,2,6]{2,1,0:T(2,128)S(1)}, f32[32,2,6,1024]{3,2,1,0:T(8,128)S(1)}) fusion(pred[32,1024]{1,0:T(8,128)(4,1)S(1)} %get-tuple-element.27, bf16[2,32,2,1024,128]{4,3,2,1,0:T(8,128)(2,1)} %param.15, bf16[32,2,8,128]{3,2,0,1:T(8,128)(2,1)S(1)} %bitcast.131), kind=kOutput, calls=%fused_computation.32 | convolution fusion | flops 101842560 | bytes 18515456 | tf_op jit(solution)/shard_map/bgqd,bgsd->bgqs/dot_general | solution.py:19
  130.2 7.2 %fusion.33 = bf16[32,2,6,128]{3,2,1,0:T(8,128)(2,1)S(1)} fusion(bf16[2,32,2,1024,128]{4,3,2,1,0:T(8,128)(2,1)} %param.16, f32[32,2,6,1024]{3,2,1,0:T(8,128)S(1)} %get-tuple-element.29, f32[32,2,6]{2,1,0:T(2,128)S(1)} %get-tuple-element.19, f32[32,2,6]{2,1,0:T(2,128)S(1)} %multiply_maximum_fusion.1, pred[32,1024]{1,0:T(8,128)(4,1)S(1)} %get-tuple-element.27, ...), kind=kOutput, calls=%fused_computation.45 | convolution fusion | flops 102776832 | bytes 18518528 | tf_op jit(solution)/shard_map/bgqs,bgsd->bgqd/dot_general | solution.py:28
  137.4 7.3 %all_to_all.70 = bf16[32,2,768]{2,0,1:T(8,128)(2,1)S(1)} all-to-all(bf16[32,2,768]{2,0,1:T(8,128)(2,1)S(1)} %copy.169), channel_id=1, replica_groups=mesh['rep'=1,'yz'=2,'x'=4] {'yz'}, dimensions={1} | all-to-all | bytes 196608 | tf_op jit(solution)/shard_map/all_to_all | solution.py:73
  144.8 8.3 %all_gather.19 = bf16[256,768]{1,0:T(8,128)(2,1)S(1)} all-gather(bf16[64,768]{1,0:T(8,128)(2,1)S(1)} %bitcast.137), channel_id=1, replica_groups=mesh['rep'=1,'yz'=2,'x'=4] {'x'}, dimensions={0}, use_global_device_ids=true | all-gather | bytes 491520 | tf_op jit(solution)/shard_map/all_gather | solution.py:74
  158.5 8.5 %reduce-scatter.9.cloned.1.call-done = bf16[256,192]{0,1:T(8,128)(2,1)} async-done(((bf16[256,384]{0,1:T(8,128)(2,1)}), bf16[256,192]{0,1:T(8,128)(2,1)}) %reduce-scatter.9.cloned.1.call-update) | async-done | bytes 98320 | tf_op jit(solution)/shard_map/reduce_scatter | solution.py:79
  168.0 5.3 %all_gather.21 = bf16[256,384]{0,1:T(8,128)(2,1)S(1)} all-gather(bf16[256,192]{0,1:T(8,128)(2,1)S(1)} %add_convert_fusion.1), channel_id=1, replica_groups=mesh['rep'=1,'yz'=2,'x'=4] {'yz'}, dimensions={1}, use_global_device_ids=true | all-gather | bytes 294912 | tf_op jit(solution)/shard_map/all_gather | solution.py:59
  173.3 5.7 %psum.15 = f32[256,1]{0,1:T(1,128)S(1)} all-reduce(f32[256,1]{0,1:T(1,128)S(1)} %bitcast.152), channel_id=1, replica_groups=mesh['rep'=1,'yz'=2,'x'=4] {'x'}, use_global_device_ids=true, to_apply=%region_7.8 | all-reduce | flops 256 | bytes 2048 | tf_op jit(solution)/shard_map/psum | solution.py:61
  180.7 7.8 %convolution_convert_fusion = bf16[256,2,4480]{2,0,1:T(8,128)(2,1)} fusion(bf16[1,384,2,4480]{3,2,1,0:T(2,128)(2,1)} %get-tuple-element.6, bf16[256,384]{0,1:T(8,128)(2,1)S(1)} %all_gather.21, f32[384]{0:T(512)S(1)} %copy-done.9, f32[256]{0:T(256)S(1)} %bitcast.150), kind=kOutput, calls=%fused_computation.14 | convolution fusion | flops 1764294656 | bytes 11667968 | tf_op jit(solution)/shard_map/be,etf->btf/dot_general | solution.py:65
  188.4 6.5 %copy.148 = bf16[256,2,4480]{0,2,1:T(8,128)(2,1)} copy(bf16[256,2,4480]{2,0,1:T(8,128)(2,1)} %convolution_convert_fusion) | data formatting | bytes 9175040 | tf_op jit(solution)/shard_map/convert_element_type | solution.py:65
  195.2 6.8 %pad_maximum_fusion.1 = bf16[256,9984]{0,1:T(8,128)(2,1)} fusion(bf16[256,8960]{0,1:T(8,128)(2,1)} %bitcast.127, bf16[256,1024]{0,1:T(8,128)(2,1)S(1)} %copy.149), kind=kLoop, calls=%fused_computation.19 | loop fusion | flops 10223616 | bytes 10223616 | tf_op jit(solution)/shard_map/concatenate | solution.py:66
  202.0 7.7 %copy.174 = bf16[256,9984]{1,0:T(8,128)(2,1)} copy(bf16[256,9984]{0,1:T(8,128)(2,1)} %pad_maximum_fusion.1) | data formatting | bytes 10223616
  209.8 44.4 %reduce-scatter.15.cloned.1.call-done = bf16[64,9984]{1,0:T(8,128)(2,1)} async-done(((bf16[256,9984]{1,0:T(8,128)(2,1)}), bf16[64,9984]{1,0:T(8,128)(2,1)}) %reduce-scatter.15.cloned.1.call-update) | async-done | bytes 1277968 | tf_op jit(solution)/shard_map/reduce_scatter | solution.py:67
  271.6 8.2 %fusion.19 = (f32[32,2,6]{2,1,0:T(2,128)S(1)}, f32[32,2,6,1024]{3,2,1,0:T(8,128)S(1)}) fusion(pred[32,1024]{1,0:T(8,128)(4,1)S(1)} %get-tuple-element.27, bf16[2,32,2,1024,128]{4,3,2,1,0:T(8,128)(2,1)} %param.15, bf16[32,2,8,128]{3,2,0,1:T(8,128)(2,1)S(1)} %bitcast.134), kind=kOutput, calls=%fused_computation.33 | convolution fusion | flops 101842560 | bytes 18515456 | tf_op jit(solution)/shard_map/bgqd,bgsd->bgqs/dot_general | solution.py:19
  281.4 7.2 %fusion.30 = bf16[32,2,6,128]{3,2,1,0:T(8,128)(2,1)S(1)} fusion(bf16[2,32,2,1024,128]{4,3,2,1,0:T(8,128)(2,1)} %param.16, f32[32,2,6,1024]{3,2,1,0:T(8,128)S(1)} %get-tuple-element.31, f32[32,2,6]{2,1,0:T(2,128)S(1)} %get-tuple-element.17, f32[32,2,6]{2,1,0:T(2,128)S(1)} %multiply_maximum_fusion, pred[32,1024]{1,0:T(8,128)(4,1)S(1)} %get-tuple-element.27, ...), kind=kOutput, calls=%fused_computation.44 | convolution fusion | flops 102776832 | bytes 18518528 | tf_op jit(solution)/shard_map/bgqs,bgsd->bgqd/dot_general | solution.py:28
  296.8 8.3 %all_gather.22 = bf16[256,768]{1,0:T(8,128)(2,1)S(1)} all-gather(bf16[64,768]{1,0:T(8,128)(2,1)S(1)} %bitcast.136), channel_id=1, replica_groups=mesh['rep'=1,'yz'=2,'x'=4] {'x'}, dimensions={0}, use_global_device_ids=true | all-gather | bytes 491520 | tf_op jit(solution)/shard_map/all_gather | solution.py:74
  310.3 43.5 %broadcast_select_fusion = (bf16[2,32,2,1024,128]{4,3,2,1,0:T(8,128)(2,1)}, bf16[2,32,2,1024,128]{4,3,2,1,0:T(8,128)(2,1)}) fusion(bf16[2,32,2,1024,128]{4,3,2,1,0:T(8,128)(2,1)} %param.16, pred[32,1024]{1,0:T(8,128)(4,1)S(1)} %get-tuple-element.26, bf16[2,32,2,128]{3,2,1,0:T(2,128)(2,1)S(1)} %copy.160, bf16[2,32,2,1024,128]{4,3,2,1,0:T(8,128)(2,1)} %param.15, ...), kind=kLoop, calls=%fused_computation | loop fusion | flops 33554432 | bytes 134316032 | tf_op jit(solution)/shard_map/jit(_where)/select_n | solution.py:37
  (94 shorter events, 61.7 us)
Async XLA Ops:
  7.2 99.4 %reduce-scatter.13.cloned.1.call-start = ((), (), s32[]{:S(2)}) async-start(), calls=%async_computation.12 | async-start | bytes 6389760 | tf_op jit(solution)/shard_map/reduce_scatter | solution.py:67
  60.9 0.7 copy-start.10
  108.1 12.1 %all-to-all-start = ((bf16[2,32,1024]{2,1,0:T(8,128)(2,1)}), bf16[2,32,1024]{2,1,0:T(8,128)(2,1)S(1)}, u32[]{:S(2)}, u32[]{:S(2)}) async-start(bf16[2,32,1024]{2,1,0:T(8,128)(2,1)} %bitcast.6), calls=%async_computation | async-start | bytes 262144 | tf_op jit(solution)/shard_map/all_to_all | solution.py:69
  111.5 41.7 %all-gather.3.cloned.1.call-start = ((), (), s32[]{:S(2)}) async-start(), calls=%async_computation.8 | async-start | bytes 2867200 | tf_op jit(solution)/shard_map/all_gather | solution.py:77
  120.0 47.0 %reduce-scatter.9.cloned.1.call-start = ((), (), s32[]{:S(2)}) async-start(), calls=%async_computation.9 | async-start | bytes 294912 | tf_op jit(solution)/shard_map/reduce_scatter | solution.py:79
  153.1 4.3 %copy-start = (bf16[2,768,384]{2,1,0:T(8,128)(2,1)S(1)}, bf16[2,768,384]{2,1,0:T(8,128)(2,1)}, u32[]{:S(2)}) copy-start(bf16[2,768,384]{2,1,0:T(8,128)(2,1)} %param.13) | copy-start | bytes 3538948
  153.1 13.9 %copy-start.3 = (bf16[256,192]{0,1:T(8,128)(2,1)S(1)}, bf16[256,192]{0,1:T(8,128)(2,1)}, u32[]{:S(2)}) copy-start(bf16[256,192]{0,1:T(8,128)(2,1)} %param.9) | copy-start | bytes 294916
  157.4 21.6 %copy-start.9 = (f32[384]{0:T(512)S(1)}, f32[384]{0:T(512)}, u32[]{:S(2)}) copy-start(f32[384]{0:T(512)} %get-tuple-element.3) | copy-start | bytes 4612
  158.5 95.7 %reduce-scatter.15.cloned.1.call-start = ((), (), s32[]{:S(2)}) async-start(), calls=%async_computation.13 | async-start | bytes 6389760 | tf_op jit(solution)/shard_map/reduce_scatter | solution.py:67
  167.9 20.5 %copy-start.1 = (bf16[256,192]{0,1:T(8,128)(2,1)}, bf16[256,192]{0,1:T(8,128)(2,1)S(1)}, u32[]{:S(2)}) copy-start(bf16[256,192]{0,1:T(8,128)(2,1)S(1)} %add_convert_fusion.1) | copy-start | bytes 294916
  255.7 12.7 %all-to-all-start.2 = ((bf16[2,32,1024]{2,1,0:T(8,128)(2,1)}), bf16[2,32,1024]{2,1,0:T(8,128)(2,1)}, u32[]{:S(2)}, u32[]{:S(2)}) async-start(bf16[2,32,1024]{2,1,0:T(8,128)(2,1)} %bitcast.26), calls=%async_computation.3 | async-start | bytes 262144 | tf_op jit(solution)/shard_map/all_to_all | solution.py:69
  259.8 45.3 %all-gather.5.cloned.1.call-start = ((), (), s32[]{:S(2)}) async-start(), calls=%async_computation.10 | async-start | bytes 2867200 | tf_op jit(solution)/shard_map/all_gather | solution.py:77
  270.7 9.0 %copy-start.7 = (bf16[32,2,1,128]{3,0,2,1:T(8,128)(2,1)}, bf16[32,2,1,128]{3,0,2,1:T(8,128)(2,1)S(1)}, u32[]{:S(2)}) copy-start(bf16[32,2,1,128]{3,0,2,1:T(8,128)(2,1)S(1)} %copy.233) | copy-start | bytes 49156
  279.7 1.6 copy-start.4
  279.8 1.7 copy-start.8
  281.4 11.3 %copy-start.5 = (bf16[1,32,2,128]{3,1,2,0:T(8,128)(2,1)S(1)}, bf16[1,32,2,128]{3,1,2,0:T(8,128)(2,1)}, u32[]{:S(2)}) copy-start(bf16[1,32,2,128]{3,1,2,0:T(8,128)(2,1)} %get-tuple-element.32) | copy-start | bytes 49156
  281.4 11.3 %copy-start.6 = (bf16[32,2,1,128]{3,0,2,1:T(8,128)(2,1)S(1)}, bf16[32,2,1,128]{3,0,2,1:T(8,128)(2,1)}, u32[]{:S(2)}) copy-start(bf16[32,2,1,128]{3,0,2,1:T(8,128)(2,1)} %copy.232) | copy-start | bytes 49156
  289.3 7.4 %all-to-all-start.3 = ((bf16[32,2,768]{2,0,1:T(8,128)(2,1)}), bf16[32,2,768]{2,0,1:T(8,128)(2,1)S(1)}, u32[]{:S(2)}, u32[]{:S(2)}) async-start(bf16[32,2,768]{2,0,1:T(8,128)(2,1)} %copy.171), calls=%async_computation.4 | async-start | bytes 196608 | tf_op jit(solution)/shard_map/all_to_all | solution.py:73
  292.7 61.2 %reduce-scatter.11.cloned.1.call-start = ((), (), s32[]{:S(2)}) async-start(), calls=%async_computation.11 | async-start | bytes 294912 | tf_op jit(solution)/shard_map/reduce_scatter | solution.py:79
  310.3 43.6 %copy-start.2 = (bf16[256,192]{0,1:T(8,128)(2,1)S(1)}, bf16[256,192]{0,1:T(8,128)(2,1)}, u32[]{:S(2)}) copy-start(bf16[256,192]{0,1:T(8,128)(2,1)} %copy-done.1) | copy-start | bytes 294916
Sparse Core Ops, SparseCore 0:
  61.1 45.4 reduce-scatter.12
  120.1 21.0 all-gather.2
  158.6 8.3 reduce-scatter.8
  209.9 44.2 reduce-scatter.14
  268.6 20.8 all-gather.4
  310.4 8.3 reduce-scatter.10
where the time goes:
time: 364 us; the launch traced here: 362 us
  waiting for transfers between devices  101 us (28%)
  other arithmetic  72.4 us (20%)
  matrix products  58.2 us (16%)
  local copies, waits for them, and re-layouts  57.3 us (16%)
  blocking collectives  47.5 us (13%)
  between operations  14.5 us (4%)
  starting transfers between devices  11.4 us (3%)
    reduce_scatter x2, waiting for transfers between devices, device_step(): summed = lax.psum_scatter(merged, 'x', scatter_dimension=0, tiled=True)  89.3 us
    select_n x1, other arithmetic, write_caches(): jnp.where(slot_hit, jnp.stack(new_vals)[:, :, :, None, :], v_cache)  43.5 us
    unnamed x28, local copies, waits for them, and re-layouts  17.7 us
    all_gather x2, blocking collectives, device_step(): attn_full = lax.all_gather(attn_back, 'x', axis=0, tiled=True)  16.7 us
    dot_general x2, matrix products, attend(): jnp.einsum('bgqd,bgsd->bgqs', queries, keys_l, preferred_element_type=jnp...  16.3 us
    dot_general x2, matrix products, attend(): jnp.einsum('bgqs,bgsd->bgqd', prob_old, vals_l, preferred_element_type=jn...  14.4 us
    concatenate x2, other arithmetic, device_step(): jnp.concatenate([attn_part, mlp_part.reshape(num_seqs, -1)], axis=1)  13.7 us
    convert_element_type x2, local copies, waits for them, and re-layouts, device_step(): jnp.einsum('be,etf->btf', normed, w_mlp[layer_idx], preferred_element_typ...  13.1 us
  transfers between devices with their start and end apart: 9, of which 4 were waited for; matrix products, arithmetic and copies ran while one was open for 27% of the time, Pallas kernels for 0%

commit v1 on v0

v1 whole, which is shorter than its diff:
```python
import functools

import jax
import jax.numpy as jnp
from jax import lax
from jax.experimental import pallas as pl
from jax.experimental.pallas import tpu as pltpu
from jax.sharding import PartitionSpec as P

NORM_EPS = 1e-5
MESH = pl.DeviceIdType.MESH
BF16 = jnp.bfloat16
F32 = jnp.float32

CHUNKS = 5
EARLY = 1
VMEM_LIMITS = (62 * 2 ** 20, 58 * 2 ** 20, 58 * 2 ** 20)


def dot(a, b):
    return jnp.dot(a, b, preferred_element_type=F32)


class Links:
    def __init__(self, send_sems, recv_sems, local_sems):
        self.send_sems, self.recv_sems, self.local_sems = send_sems, recv_sems, local_sems
        self.sent, self.used, self.local_used = [], 0, 0
        x, y = lax.axis_index('x'), lax.axis_index('yz')
        self.x, self.y = x, y
        core = lax.rem(x, 2)
        self.along_x = (3 - x, x + 1 - 2 * core, lax.rem(x + 2, 4))
        self.blocks = self.along_x + (x,)
        self.targets = tuple({'x': p, 'yz': y} for p in self.along_x) + ({'x': x, 'yz': 1 - y},)

    def barrier(self):
        sem = pltpu.get_barrier_semaphore()
        for target in self.targets:
            pl.semaphore_signal(sem, inc=1, device_id=target, device_id_type=MESH)
        pl.semaphore_wait(sem, len(self.targets))

    def push(self, src, dst, to):
        k = self.used
        self.used += 1
        copy = pltpu.make_async_remote_copy(
            src_ref=src, dst_ref=dst, send_sem=self.send_sems.at[k], recv_sem=self.recv_sems.at[k],
            device_id=self.targets[to], device_id_type=MESH)
        copy.start()
        self.sent.append(copy)
        return copy

    def copy(self, src, dst):
        k = self.local_used
        self.local_used += 1
        copy = pltpu.make_async_copy(src, dst, self.local_sems.at[k])
        copy.start()
        return copy

    def drain(self):
        for copy in self.sent:
            copy.wait_send()


DIAG, PARTNER, ACROSS, YZ = 0, 1, 2, 3


def spread_matrices(depth):
    row = lax.broadcasted_iota(jnp.int32, (depth, 2 * depth), 0)
    col = lax.broadcasted_iota(jnp.int32, (depth, 2 * depth), 1)
    one, zero = jnp.ones((), F32), jnp.zeros((), F32)
    return (jnp.where(col == 2 * row, one, zero).astype(BF16), jnp.where(col == 2 * row + 1, one, zero).astype(BF16))


def front(links, layer, h_t, model_dim, gain_ref, wa, wm, qkv_out, zsend_out, zmine_out, s):
    depth, rows = h_t.shape
    shard = rows // 4
    chunks, _, cols = s['z_recv'].shape
    x, y = links.x, links.y
    s['sq_send'][...] = jnp.broadcast_to(jnp.sum(h_t * h_t, axis=0, keepdims=True), s['sq_send'].shape)
    sq_copies = [links.push(s['sq_send'], s['sq_recv'].at[k], k) for k in (DIAG, ACROSS, PARTNER)]
    gain = jnp.broadcast_to(gain_ref[layer:layer + 1, :].astype(F32), (128, depth)).T
    gain = jnp.concatenate([gain] * (rows // 128), axis=1)
    even, odd = spread_matrices(depth)
    for c in sq_copies:
        c.wait_recv()
    total = s['sq_send'][...] + s['sq_recv'][PARTNER] + (s['sq_recv'][ACROSS] + s['sq_recv'][DIAG])
    inv_rms = lax.rsqrt(total[:1] / model_dim + NORM_EPS)
    s['u'][...] = (h_t * inv_rms * gain).T.astype(BF16)
    u = jnp.concatenate([s['u'][pl.ds(pl.multiple_of(b * shard, shard), shard), :] for b in links.blocks], axis=0)
    wa.wait()
    s['a_part'][...] = dot(u, s['wa'][...]).astype(BF16)
    half = rows // 2
    a_core = links.push(s['a_part'].at[pl.ds(0, half)], s['a_core'], PARTNER)
    u_gate, u_up = dot(u, even).astype(BF16), dot(u, odd).astype(BF16)
    for k in range(4):
        s['u2'][pl.ds(2 * k * shard, shard), :] = u_gate[k * shard:(k + 1) * shard]
        s['u2'][pl.ds((2 * k + 1) * shard, shard), :] = u_up[k * shard:(k + 1) * shard]

    z_copies, early, outs = {}, {}, []

    def project(j):
        wm[j].wait()
        s['z_part'][j] = dot(s['u2'][...], s['wm'][j].reshape(2 * depth, cols)).astype(BF16)
        z_copies[j] = links.push(s['z_part'].at[j, pl.ds(0, rows)], s['z_recv'].at[j], PARTNER)

    def combine(j):
        z_copies[j].wait_recv()
        half_z = 2 * shard
        s['z_x'][j] = (s['z_part'][j, rows:rows + half_z].astype(F32) + s['z_recv'][j, :half_z].astype(F32)).astype(BF16)
        if j < EARLY:
            early[j] = links.push(s['z_x'].at[j], s['z_early'].at[j], ACROSS)
        else:
            outs.append(links.copy(s['z_x'].at[j], zsend_out.at[j - EARLY]))
        s['z_mine'][j] = (s['z_part'][j, rows + half_z:].astype(F32) + s['z_recv'][j, half_z:].astype(F32)).astype(BF16)
        if j >= EARLY:
            outs.append(links.copy(s['z_mine'].at[j], zmine_out.at[j]))

    project(0)
    a_core.wait_recv()
    s['a_sum'][...] = (s['a_part'][half:].astype(F32) + s['a_core'][...].astype(F32)).astype(BF16)
    a_across = links.push(s['a_sum'].at[pl.ds(0, shard)], s['a_across'], ACROSS)
    project(1)
    combine(0)
    project(2)
    a_across.wait_recv()
    s['a_full'][...] = (s['a_sum'][shard:].astype(F32) + s['a_across'][...].astype(F32)).astype(BF16)
    seqs = shard // 2
    a_yz = links.push(s['a_full'].at[pl.ds(pl.multiple_of((1 - y) * seqs, seqs), seqs)], s['a_yz'], YZ)
    qkv_out[y] = s['a_full'][pl.ds(pl.multiple_of(y * seqs, seqs), seqs), :]
    combine(1)
    for j in range(3, chunks):
        project(j)
        combine(j - 1)
    combine(chunks - 1)
    for j in range(EARLY):
        early[j].wait_recv()
        s['z_mine'][j] = (s['z_mine'][j].astype(F32) + s['z_early'][j].astype(F32)).astype(BF16)
        outs.append(links.copy(s['z_mine'].at[j], zmine_out.at[j]))
    a_yz.wait_recv()
    qkv_out[1 - y] = s['a_yz'][...]
    for c in outs:
        c.wait()


def back(links, o_ref, zgot_ref, z_loads, wd, wo, s, whole):
    chunks, rows, cols = s['m'].shape
    shard = rows // 4
    seqs = shard // 2
    x, y = links.x, links.y
    own_rows = pl.ds(pl.multiple_of(y * seqs, seqs), seqs)
    o_yz = links.push(o_ref.at[1 - y], s['o'].at[pl.ds(3 * shard + pl.multiple_of(y * seqs, seqs), seqs)], YZ)
    s['o'][pl.ds(3 * shard + pl.multiple_of(y * seqs, seqs), seqs), :] = o_ref[y]
    across, partner, diag = {}, {}, {}

    def block(j, k):
        return s['m'].at[j, pl.ds(k * shard, shard)]

    def mix(j):
        z_loads[j].wait()
        z = s['z_in'][j].astype(F32)
        if j >= EARLY:
            z = (z + zgot_ref[j - EARLY].astype(F32)).astype(BF16).astype(F32)
        gate, up = z[:shard], z[shard:]
        s['m'][j, 3 * shard:] = (gate * jax.nn.sigmoid(gate) * up).astype(BF16)
        across[j] = links.push(block(j, 3), block(j, 2), ACROSS)
        partner[j] = links.push(block(j, 3), block(j, 1), PARTNER)

    def forward(j):
        across[j].wait_recv()
        diag[j] = links.push(block(j, 2), block(j, 0), PARTNER)

    def o_block(k):
        return s['o'].at[pl.ds(k * shard, shard)]

    mix(0)
    mix(1)
    o_yz.wait_recv()
    o_across = links.push(o_block(3), o_block(2), ACROSS)
    o_partner = links.push(o_block(3), o_block(1), PARTNER)
    for j in range(2, chunks):
        mix(j)
    acc = None
    o_diag = None
    for j in range(chunks):
        forward(j)
        if j == 1:
            o_across.wait_recv()
            o_diag = links.push(o_block(2), o_block(0), PARTNER)
        if j >= 1:
            acc = down(links, j - 1, partner, diag, wd, s, acc)
        if j == 2:
            o_partner.wait_recv()
            o_diag.wait_recv()
            wo.wait()
            s['acc'][...] += dot(s['o'][...], s['wo'][...])
    down(links, chunks - 1, partner, diag, wd, s, acc)
    for k in range(4):
        s['update'][pl.ds(pl.multiple_of(links.blocks[k] * shard, shard), shard), :] = s['acc'][k * shard:(k + 1) * shard, :]
    s['up_part'][...] = s['update'][...].T.astype(BF16)
    if whole:
        up = links.push(s['up_part'], s['up_recv'], YZ)
        up.wait_recv()
        return s['up_part'][...].astype(F32) + s['up_recv'][...].astype(F32)
    part = s['up_recv'].shape[0]
    up = links.push(s['up_part'].at[pl.ds(pl.multiple_of((1 - y) * part, part), part)], s['up_recv'], YZ)
    up.wait_recv()
    own = s['up_part'][pl.ds(pl.multiple_of(y * part, part), part), :]
    return own.astype(F32) + s['up_recv'][...].astype(F32)


def down(links, j, partner, diag, wd, s, acc):
    partner[j].wait_recv()
    diag[j].wait_recv()
    wd[j].wait()
    part = dot(s['m'][j], s['wd'][j])
    if acc is None:
        s['acc'][...] = part
    else:
        s['acc'][...] += part
    return True


def load_front(links, layer, wa_hbm, wm_hbm, s):
    cols = s['wm'].shape[-1]
    wa = links.copy(wa_hbm.at[layer], s['wa'])
    wm = [links.copy(wm_hbm.at[layer, :, :, pl.ds(j * cols, cols)], s['wm'].at[j]) for j in range(s['wm'].shape[0])]
    return wa, wm


def load_back(links, layer, zmine_hbm, wd_hbm, wo_hbm, s):
    chunks, cols, _ = s['wd'].shape
    z_loads = [links.copy(zmine_hbm.at[j], s['z_in'].at[j]) for j in range(chunks)]
    wd = [links.copy(wd_hbm.at[layer, pl.ds(j * cols, cols)], s['wd'].at[j]) for j in range(chunks)]
    wo = links.copy(wo_hbm.at[layer], s['wo'])
    return z_loads, wd, wo


def start_kernel(names, model_dim, h_ref, gain_ref, wa_hbm, wm_hbm, qkv_out, zsend_out, zmine_out, h_out, *scratch):
    s = dict(zip(names, scratch))
    links = Links(s['send'], s['recv'], s['local'])
    wa, wm = load_front(links, 0, wa_hbm, wm_hbm, s)
    links.barrier()
    part = h_ref.shape[0]
    mine = pl.ds(pl.multiple_of(links.y * part, part), part)
    h_yz = links.push(h_ref, s['h'].at[mine], YZ)
    s['h'][mine, :] = h_ref[...]
    h_yz.wait_recv()
    h_out[...] = s['h'][...]
    front(links, 0, s['h'][...].astype(F32), model_dim, gain_ref, wa, wm, qkv_out, zsend_out, zmine_out, s)
    links.drain()


def middle_kernel(names, model_dim, h_ref, o_ref, gain_ref, zmine_hbm, zgot_ref, wd_hbm, wo_hbm, wa_hbm, wm_hbm, qkv_out, zsend_out,
                  zmine_out, h_out, *scratch):
    s = dict(zip(names, scratch))
    links = Links(s['send'], s['recv'], s['local'])
    z_loads, wd, wo = load_back(links, 0, zmine_hbm, wd_hbm, wo_hbm, s)
    wa, wm = load_front(links, 1, wa_hbm, wm_hbm, s)
    links.barrier()
    update = back(links, o_ref, zgot_ref, z_loads, wd, wo, s, True)
    h_new = (h_ref[...].astype(F32) + update).astype(BF16)
    h_out[...] = h_new
    front(links, 1, h_new.astype(F32), model_dim, gain_ref, wa, wm, qkv_out, zsend_out, zmine_out, s)
    links.drain()


def end_kernel(names, h_ref, o_ref, zmine_hbm, zgot_ref, wd_hbm, wo_hbm, h_out, *scratch):
    s = dict(zip(names, scratch))
    links = Links(s['send'], s['recv'], s['local'])
    z_loads, wd, wo = load_back(links, 1, zmine_hbm, wd_hbm, wo_hbm, s)
    links.barrier()
    update = back(links, o_ref, zgot_ref, z_loads, wd, wo, s, False)
    part = h_out.shape[0]
    own = h_ref[pl.ds(pl.multiple_of(links.y * part, part), part), :]
    h_out[...] = (own.astype(F32) + update).astype(BF16)
    links.drain()


def attention_kernel(layer, per_step, len_ref, qkv_ref, k_hbm, v_hbm, *rest):
    k_out, v_out, o_ref, kbuf, vbuf, q_scr, o_scr, in_sem, out_sem = rest[-9:]
    num_seqs, kv_heads, cache_len, head_dim = kbuf.shape
    slots = qkv_ref.shape[2] // head_dim
    rows = kv_heads * slots
    scale = head_dim ** -0.5

    def load(i):
        return (pltpu.make_async_copy(k_hbm.at[layer, i], kbuf.at[i], in_sem.at[0, i]),
                pltpu.make_async_copy(v_hbm.at[layer, i], vbuf.at[i], in_sem.at[1, i]))

    def store(i):
        return (pltpu.make_async_copy(kbuf.at[i], k_out.at[layer, i], out_sem.at[0, i]),
                pltpu.make_async_copy(vbuf.at[i], v_out.at[layer, i], out_sem.at[1, i]))

    @pl.loop(0, num_seqs)
    def _(i):
        for c in load(i):
            c.start()

    for head in range(kv_heads):
        for j in range(slots):
            q_scr[pl.ds(head * slots + j, num_seqs, stride=rows), :] = (
                qkv_ref[head, :, j * head_dim:(j + 1) * head_dim].astype(F32))

    tile_row = lax.broadcasted_iota(jnp.int32, (16, head_dim), 0)
    position = lax.broadcasted_iota(jnp.int32, (rows, cache_len), 1)

    @pl.loop(0, num_seqs // per_step)
    def _(step):
        group = [step * per_step + sub for sub in range(per_step)]
        for i in group:
            for c in load(i):
                c.wait()
            length = len_ref[i]
            base = pl.multiple_of((length // 16) * 16, 16)
            hit = tile_row == length - base
            for head in range(kv_heads):
                for buf, j in ((kbuf, slots - 2), (vbuf, slots - 1)):
                    new = q_scr[pl.ds(i * rows + head * slots + j, 1), :]
                    old = buf[i, head, pl.ds(base, 16), :].astype(F32)
                    buf[i, head, pl.ds(base, 16), :] = jnp.where(hit, new, old).astype(buf.dtype)
            for c in store(i):
                c.start()
        scores, probs = [], []
        for i in group:
            q = q_scr[pl.ds(pl.multiple_of(i * rows, rows), rows), :].astype(BF16)
            by_head = [lax.dot_general(q, kbuf[i, head], (((1,), (1,)), ((), ())), preferred_element_type=F32)
                       for head in range(kv_heads)]
            scores.append(jnp.concatenate([by_head[head][head * slots:(head + 1) * slots] for head in range(kv_heads)], axis=0))
        for i, score in zip(group, scores):
            score = jnp.where(position <= len_ref[i], score * scale, -1e30)
            e = jnp.exp(score - jnp.max(score, axis=1, keepdims=True))
            probs.append((e / jnp.sum(e, axis=1, keepdims=True)).astype(BF16))
        for i, p in zip(group, probs):
            by_head = [dot(p, vbuf[i, head]) for head in range(kv_heads)]
            o_scr[pl.ds(pl.multiple_of(i * rows, rows), rows), :] = jnp.concatenate(
                [by_head[head][head * slots:(head + 1) * slots] for head in range(kv_heads)], axis=0)

    for head in range(kv_heads):
        for j in range(slots - 2):
            o_ref[head, :, j * head_dim:(j + 1) * head_dim] = (
                o_scr[pl.ds(head * slots + j, num_seqs, stride=rows), :].astype(o_ref.dtype))

    @pl.loop(0, num_seqs)
    def _(i):
        for c in store(i):
            c.wait()


ANY = pl.BlockSpec(memory_space=pl.ANY)
VMEM = pl.BlockSpec(memory_space=pltpu.VMEM)


def attention(layer, lengths, qkv, k_cache, v_cache, outs):
    layers, num_seqs, kv_heads, cache_len, head_dim = k_cache.shape
    slots = qkv.shape[2] // head_dim
    rows = kv_heads * slots
    return pl.pallas_call(
        functools.partial(attention_kernel, layer, 2),
        out_shape=(jax.ShapeDtypeStruct(k_cache.shape, k_cache.dtype), jax.ShapeDtypeStruct(v_cache.shape, v_cache.dtype),
                   jax.ShapeDtypeStruct((kv_heads, num_seqs, (slots - 2) * head_dim), BF16)),
        in_specs=[pl.BlockSpec(memory_space=pltpu.SMEM), VMEM, ANY, ANY] + [ANY] * len(outs),
        out_specs=(ANY, ANY, VMEM),
        scratch_shapes=[pltpu.VMEM((num_seqs, kv_heads, cache_len, head_dim), BF16)] * 2
        + [pltpu.VMEM((num_seqs * rows, head_dim), F32)] * 2 + [pltpu.SemaphoreType.DMA((2, num_seqs))] * 2,
        input_output_aliases={4: 0, 5: 1} if outs else {},
        compiler_params=pltpu.CompilerParams(vmem_limit_bytes=44 * 2 ** 20),
        cost_estimate=pl.CostEstimate(flops=10 ** 10, bytes_accessed=8 * num_seqs * kv_heads * cache_len * head_dim, transcendentals=0),
        name=f'attention_{layer}',
    )(lengths, qkv, k_cache, v_cache, *outs)


def solution(mesh):
    seq_axes = ('rep', 'x', 'yz')
    hidden_spec = P('rep', ('x', 'yz'))
    cache_spec = P(None, seq_axes, None, None, None)
    in_specs = (hidden_spec, P(None, 'x'), P(None, 'x', 'yz'), P(None, 'x', None, 'yz'), P(None, 'yz', 'x'), P(None, 'yz', 'x'), cache_spec, cache_spec, P(seq_axes))
    out_specs = (hidden_spec, cache_spec, cache_spec)
    swap = [(0, 2), (2, 0), (1, 3), (3, 1)]

    def device_step(hidden, norm_gain, w_attn, w_mlp, w_out, w_down, k_cache, v_cache, lengths):
        rows, part = hidden.shape
        depth, attn_cols = w_attn.shape[1:]
        model_dim = depth * mesh.shape['x']
        mlp_cols = w_mlp.shape[3]
        out_depth = w_out.shape[1]
        shard, half = rows // 4, rows // 2
        seqs = shard // 2
        cols = mlp_cols // CHUNKS
        late = CHUNKS - EARLY
        sq = (8, rows)
        common = {
            'send': pltpu.SemaphoreType.DMA((40,)), 'recv': pltpu.SemaphoreType.DMA((40,)), 'local': pltpu.SemaphoreType.DMA((40,)),
        }
        front_scratch = {
            'sq_send': pltpu.VMEM(sq, F32), 'sq_recv': pltpu.VMEM((3,) + sq, F32), 'u': pltpu.VMEM((rows, depth), BF16),
            'wa': pltpu.VMEM((depth, attn_cols), BF16), 'wm': pltpu.VMEM((CHUNKS, depth, 2, cols), BF16),
            'a_part': pltpu.VMEM((rows, attn_cols), BF16), 'a_core': pltpu.VMEM((half, attn_cols), BF16),
            'a_sum': pltpu.VMEM((half, attn_cols), BF16), 'a_across': pltpu.VMEM((shard, attn_cols), BF16),
            'a_full': pltpu.VMEM((shard, attn_cols), BF16), 'a_yz': pltpu.VMEM((seqs, attn_cols), BF16),
            'u2': pltpu.VMEM((2 * rows, 2 * depth), BF16), 'z_part': pltpu.VMEM((CHUNKS, 2 * rows, cols), BF16),
            'z_recv': pltpu.VMEM((CHUNKS, rows, cols), BF16), 'z_x': pltpu.VMEM((CHUNKS, half, cols), BF16),
            'z_mine': pltpu.VMEM((CHUNKS, half, cols), BF16), 'z_early': pltpu.VMEM((EARLY, half, cols), BF16),
        }

        def back_scratch(whole):
            return {
                'o': pltpu.VMEM((rows, out_depth), BF16), 'm': pltpu.VMEM((CHUNKS, rows, cols), BF16),
                'z_in': pltpu.VMEM((CHUNKS, half, cols), BF16),
                'wd': pltpu.VMEM((CHUNKS, cols, depth), BF16), 'wo': pltpu.VMEM((out_depth, depth), BF16),
                'acc': pltpu.VMEM((rows, depth), F32), 'update': pltpu.VMEM((rows, depth), F32),
                'up_part': pltpu.VMEM((depth, rows), BF16), 'up_recv': pltpu.VMEM((depth if whole else part, rows), BF16),
            }

        front_shapes = (
            jax.ShapeDtypeStruct((2, seqs, attn_cols), BF16), jax.ShapeDtypeStruct((late, half, cols), BF16),
            jax.ShapeDtypeStruct((CHUNKS, half, cols), BF16), jax.ShapeDtypeStruct((depth, rows), BF16))
        front_specs = (VMEM, ANY, ANY, VMEM)

        def call(kernel, name, collective_id, scratch, in_specs, out_shape, out_specs, *args):
            return pl.pallas_call(
                functools.partial(kernel, tuple(scratch)), out_shape=out_shape, in_specs=list(in_specs), out_specs=out_specs,
                scratch_shapes=list(scratch.values()), name=name,
                compiler_params=pltpu.CompilerParams(collective_id=collective_id, has_side_effects=True, vmem_limit_bytes=VMEM_LIMITS[collective_id]),
            )(*args)

        def start(names, *refs):
            start_kernel(names, model_dim, *refs)

        def middle(names, *refs):
            middle_kernel(names, model_dim, *refs)

        qkv, zsend, zmine, h_block = call(
            start, 'start', 0, {**common, **front_scratch, 'h': pltpu.VMEM((depth, rows), BF16)}, (VMEM, VMEM, ANY, ANY),
            front_shapes, front_specs, hidden.T, norm_gain, w_attn, w_mlp)
        zgot = lax.ppermute(zsend, 'x', swap)
        k_new, v_new, o = attention(0, lengths, qkv, k_cache, v_cache, ())
        qkv, zsend, zmine, h_block = call(
            middle, 'middle', 1, {**common, **front_scratch, **back_scratch(True)}, (VMEM, VMEM, VMEM, ANY, VMEM) + (ANY,) * 4,
            front_shapes, front_specs, h_block, o, norm_gain, zmine, zgot, w_down, w_out, w_attn, w_mlp)
        zgot = lax.ppermute(zsend, 'x', swap)
        k_new, v_new, o = attention(1, lengths, qkv, k_cache, v_cache, (k_new, v_new))
        h_out = call(
            end_kernel, 'end', 2, {**common, **back_scratch(False)}, (VMEM, VMEM, ANY, VMEM) + (ANY,) * 2,
            jax.ShapeDtypeStruct((part, rows), BF16), VMEM, h_block, o, zmine, zgot, w_down, w_out)
        return h_out.T, k_new, v_new

    return jax.shard_map(device_step, mesh=mesh, in_specs=in_specs, out_specs=out_specs, check_vma=False)
```

time: 364 us -> 155 us (0.43)
  Pallas kernels: 0 us -> 146 us
  waiting for transfers between devices: 101 us -> 0.01 us
  other arithmetic: 72.4 us -> 0 us
  matrix products: 58.2 us -> 0 us
  local copies, waits for them, and re-layouts: 57.3 us -> 7.12 us
  blocking collectives: 47.5 us -> 0 us
  between operations: 14.5 us -> 0.69 us
  starting transfers between devices: 11.4 us -> 1.56 us
    pallas_call x0 -> x5, Pallas kernels: none -> 146 us  [the longest x3 96.6 us: call(): pl.pallas_call(functools.partial(kernel, tuple(scratch)), out_shape=out_s...]
    reduce_scatter x4 -> x0, waiting for transfers between devices: 97.8 us -> none  [the longest x2 89.3 us: device_step(): summed = lax.psum_scatter(merged, 'x', scatter_dimension=0, tiled=True)]
    dot_general x14 -> x0, matrix products: 58.2 us -> none  [the longest x2 16.3 us: attend(): jnp.einsum('bgqd,bgsd->bgqs', queries, keys_l, preferred_element_type=jnp...]
    select_n x1 -> x0, other arithmetic: 43.5 us -> none  [write_caches(): jnp.where(slot_hit, jnp.stack(new_vals)[:, :, :, None, :], v_cache)]
    all_gather x4 -> x0, blocking collectives: 28.8 us -> none  [the longest x2 16.7 us: device_step(): attn_full = lax.all_gather(attn_back, 'x', axis=0, tiled=True)]
    convert_element_type x6 -> x0, local copies, waits for them, and re-layouts: 18.9 us -> none  [the longest x2 13.1 us: device_step(): jnp.einsum('be,etf->btf', normed, w_mlp[layer_idx], preferred_element_typ...]
    slice x6 -> x0, local copies, waits for them, and re-layouts: 18.6 us -> none  [the longest x1 11.9 us: device_step(): w_mlp[layer_idx]]
    concatenate x2 -> x0, other arithmetic: 13.7 us -> none  [device_step(): jnp.concatenate([attn_part, mlp_part.reshape(num_seqs, -1)], axis=1)]
  transfers between devices with their start and end apart: 9 -> 2, of which waited for: 4 -> 0; matrix products, arithmetic and copies ran while one was open for 27% -> 0% of each run, Pallas kernels for 0% -> 32%
where the time goes in v1:
time: 155 us
  Pallas kernels  146 us (94%)
  local copies, waits for them, and re-layouts  7.12 us (5%)
  starting transfers between devices  1.56 us (1%)
    pallas_call x3, Pallas kernels, call(): pl.pallas_call(functools.partial(kernel, tuple(scratch)), out_shape=out_s...  96.6 us
    pallas_call x2, Pallas kernels, attention(): pl.pallas_call(functools.partial(attention_kernel, layer, 2), out_shape=(...  49.2 us
    unnamed x17, local copies, waits for them, and re-layouts  7.12 us
  transfers between devices with their start and end apart: 2, of which 0 were waited for; matrix products, arithmetic and copies ran while one was open for 0% of the time, Pallas kernels for 32%

profile of v1, /device:TPU:0, one launch (start us, length us, event | category | flops | bytes accessed | tf_op | source)
XLA Modules:
  0.0 155.1 jit_solution(416906870006910834)
XLA Ops:
  0.6 26.3 %start.1 = (bf16[2,32,1024]{2,1,0:T(8,128)(2,1)}, bf16[4,128,896]{2,1,0:T(8,128)(2,1)}, bf16[5,128,896]{2,1,0:T(8,128)(2,1)}, bf16[384,256]{1,0:T(8,128)(2,1)}) custom-call(bf16[192,256]{1,0:T(8,128)(2,1)} %bitcast.3, bf16[2,384]{1,0:T(2,128)(2,1)} %refs_2_.3, bf16[2,384,1024]{2,1,0:T(8,128)(2,1)} %refs_7_.1, bf16[2,384,2,4480]{3,2,1,0:T(2,128)(2,1)} %refs_8_.1), custom_call_target="tpu_custom_call" | custom-call | tf_op jit(solution)/shard_map/start/pallas_call | solution.py:419
  26.9 0.6 collective-permute-start
  27.4 0.0 copy-start.1
  27.4 0.9 copy-done.1
  28.3 0.0 copy-start.4
  28.4 0.7 copy-done.4
  29.0 0.0 copy-start.5
  29.0 24.7 %attention_0.1 = (bf16[2,32,2,1024,128]{4,3,2,1,0:T(8,128)(2,1)}, bf16[2,32,2,1024,128]{4,3,2,1,0:T(8,128)(2,1)}, bf16[2,32,768]{2,1,0:T(8,128)(2,1)S(1)}) custom-call(s32[32]{0:T(128)S(1)} %copy-done.4, bf16[2,32,1024]{2,1,0:T(8,128)(2,1)S(1)} %copy-done.1, bf16[2,32,2,1024,128]{4,3,2,1,0:T(8,128)(2,1)} %k_hbm.3, bf16[2,32,2,1024,128]{4,3,2,1,0:T(8,128)(2,1)} %v_hbm.3), custom_call_target="tpu_custom_call" | custom-call | flops 10000000000 | bytes 67108864 | tf_op jit(solution)/shard_map/attention_0/pallas_call | solution.py:356
  53.7 0.0 copy-start.2
  53.7 0.6 copy-done.2
  54.3 0.0 collective-permute-done.refs_4_
  54.3 0.0 copy-start.7
  54.3 0.9 copy-done.7
  55.3 43.9 %middle.1 = (bf16[2,32,1024]{2,1,0:T(8,128)(2,1)}, bf16[4,128,896]{2,1,0:T(8,128)(2,1)}, bf16[5,128,896]{2,1,0:T(8,128)(2,1)}, bf16[384,256]{1,0:T(8,128)(2,1)}) custom-call(bf16[384,256]{1,0:T(8,128)(2,1)} %get-tuple-element.17.refs_0_, bf16[2,32,768]{2,1,0:T(8,128)(2,1)} %copy-done.2, bf16[2,384]{1,0:T(2,128)(2,1)} %refs_2_.3, ...), custom_call_target="tpu_custom_call" | custom-call | tf_op jit(solution)/shard_map/middle/pallas_call | solution.py:419
  99.2 1.0 collective-permute-start.1
  100.2 0.0 copy-done.5
  100.2 0.9 copy-done
  101.1 24.5 %attention_1.1 = (bf16[2,32,2,1024,128]{4,3,2,1,0:T(8,128)(2,1)}, bf16[2,32,2,1024,128]{4,3,2,1,0:T(8,128)(2,1)}, bf16[2,32,768]{2,1,0:T(8,128)(2,1)S(1)}) custom-call(s32[32]{0:T(128)S(1)} %copy-done.5, bf16[2,32,1024]{2,1,0:T(8,128)(2,1)S(1)} %copy-done, bf16[2,32,2,1024,128]{4,3,2,1,0:T(8,128)(2,1)} %k_hbm.3, ...), custom_call_target="tpu_custom_call", output_to_operand_aliasing={{0}: (4, {}), {1}: (5, {})} | custom-call | flops 10000000000 | bytes 67108864 | tf_op jit(solution)/shard_map/attention_1/pallas_call | solution.py:356
  125.6 0.0 copy-start.3
  125.6 0.6 copy-done.3
  126.3 0.0 collective-permute-done.1.zgot_ref
  126.3 0.9 copy-done.6
  127.2 26.4 %end.1 = bf16[192,256]{1,0:T(8,128)(2,1)} custom-call(bf16[384,256]{1,0:T(8,128)(2,1)} %get-tuple-element.22.h_ref, bf16[2,32,768]{2,1,0:T(8,128)(2,1)} %copy-done.3, bf16[5,128,896]{2,1,0:T(8,128)(2,1)} %get-tuple-element.27.zmine_hbm, bf16[4,128,896]{2,1,0:T(8,128)(2,1)} %copy-done.6, bf16[2,4480,384]{2,1,0:T(8,128)(2,1)} %wd_hbm.1, ...), custom_call_target="tpu_custom_call" | custom-call | tf_op jit(solution)/shard_map/end/pallas_call | solution.py:419
  153.6 1.5 copy.17
  (2 shorter events, 0.0 us)
Async XLA Ops:
  26.9 27.4 %collective-permute-start = (bf16[4,128,896]{2,1,0:T(8,128)(2,1)}, bf16[4,128,896]{2,1,0:T(8,128)(2,1)S(1)}, u32[]{:S(2)}, u32[]{:S(2)}) collective-permute-start(bf16[4,128,896]{2,1,0:T(8,128)(2,1)} %get-tuple-element.21), channel_id=1, source_target_pairs={{0,2},{2,0},{1,3},{3,1},{4,6},{6,4},{5,7},{7,5}} | collective-permute-start | bytes 2752520 | tf_op jit(solution)/shard_map/ppermute | solution.py:434
  27.4 0.9 copy-start.1
  28.3 0.7 copy-start.4
  29.0 71.2 %copy-start.5 = (s32[32]{0:T(128)S(1)}, s32[32]{0:T(128)}, u32[]{:S(2)}) copy-start(s32[32]{0:T(128)} %len_ref.3) | copy-start | bytes 388
  53.7 0.6 copy-start.2
  54.3 0.9 copy-start.7
  99.2 27.1 %collective-permute-start.1 = (bf16[4,128,896]{2,1,0:T(8,128)(2,1)}, bf16[4,128,896]{2,1,0:T(8,128)(2,1)S(1)}, u32[]{:S(2)}, u32[]{:S(2)}) collective-permute-start(bf16[4,128,896]{2,1,0:T(8,128)(2,1)} %get-tuple-element.28), channel_id=1, source_target_pairs={{0,2},{2,0},{1,3},{3,1},{4,6},{6,4},{5,7},{7,5}} | collective-permute-start | bytes 2752520 | tf_op jit(solution)/shard_map/ppermute | solution.py:439
  100.2 0.9 copy-start
  125.6 0.6 copy-start.3
  126.3 0.9 copy-start.6

commit v2 on v1

v2 whole, which is shorter than its diff:
```python
import functools

import jax
import jax.numpy as jnp
from jax import lax
from jax.experimental import pallas as pl
from jax.experimental.pallas import tpu as pltpu
from jax.sharding import PartitionSpec as P

NORM_EPS = 1e-5
MESH = pl.DeviceIdType.MESH
BF16 = jnp.bfloat16
F32 = jnp.float32

CHUNKS = 5
EARLY = 2
VMEM_LIMIT = 62 * 2 ** 20


def dot(a, b):
    return jnp.dot(a, b, preferred_element_type=F32)


class Links:
    def __init__(self, send_sems, recv_sems, local_sems, everyone):
        self.send_sems, self.recv_sems, self.local_sems = send_sems, recv_sems, local_sems
        self.sent, self.used, self.local_used = [], 0, 0
        x, y = lax.axis_index('x'), lax.axis_index('yz')
        self.x, self.y = x, y
        core = lax.rem(x, 2)
        self.along_x = (3 - x, x + 1 - 2 * core, lax.rem(x + 2, 4))
        self.blocks = self.along_x + (x,)
        self.targets = tuple({'x': p, 'yz': y} for p in self.blocks) + ({'x': x, 'yz': 1 - y},) + tuple(
            {'x': p, 'yz': 1 - y} for p in self.along_x)
        self.peers = [k for k in range(8 if everyone else 5) if k != OWN]
        self.barrier = pltpu.get_barrier_semaphore()
        for k in self.peers:
            pl.semaphore_signal(self.barrier, inc=1, device_id=self.targets[k], device_id_type=MESH)

    def meet(self):
        pl.semaphore_wait(self.barrier, len(self.peers))

    def push(self, src, dst, to):
        k = self.used
        self.used += 1
        copy = pltpu.make_async_remote_copy(
            src_ref=src, dst_ref=dst, send_sem=self.send_sems.at[k], recv_sem=self.recv_sems.at[k],
            device_id=self.targets[to], device_id_type=MESH)
        copy.start()
        self.sent.append(copy)
        return copy

    def copy(self, src, dst):
        k = self.local_used
        self.local_used += 1
        copy = pltpu.make_async_copy(src, dst, self.local_sems.at[k])
        copy.start()
        return copy

    def drain(self):
        for copy in self.sent:
            copy.wait_send()


DIAG, PARTNER, ACROSS, OWN, YZ = 0, 1, 2, 3, 4
PARTS = 2


def spread_matrices(depth):
    row = lax.broadcasted_iota(jnp.int32, (depth, 2 * depth), 0)
    col = lax.broadcasted_iota(jnp.int32, (depth, 2 * depth), 1)
    one, zero = jnp.ones((), F32), jnp.zeros((), F32)
    return (jnp.where(col == 2 * row, one, zero).astype(BF16), jnp.where(col == 2 * row + 1, one, zero).astype(BF16))


def part_order(rows, inverse):
    i = lax.broadcasted_iota(jnp.int32, (rows, rows), 0)
    j = lax.broadcasted_iota(jnp.int32, (rows, rows), 1)
    src, dst = (j, i) if inverse else (i, j)
    run = rows // (8 * PARTS)
    piece = src // run
    place = lax.rem(piece, PARTS) * (8 * run) + (piece // PARTS) * run + lax.rem(src, run)
    return jnp.where(dst == place, jnp.ones((), F32), jnp.zeros((), F32)).astype(BF16)


class Front:
    def __init__(self, links, layer, gain_hbm, wa_hbm, wm_hbm, model_dim, outs, s):
        self.links, self.s, self.layer, self.model_dim = links, s, layer, model_dim
        self.gain_copy = links.copy(gain_hbm, s['gain_in'])
        self.qkv_out, self.zsend_out, self.zmine_out = outs
        self.chunks, self.depth, _, self.cols = s['wm'].shape
        self.wa = links.copy(wa_hbm.at[layer], s['wa'])
        self.wm = [links.copy(wm_hbm.at[layer, :, :, pl.ds(j * self.cols, self.cols)], s['wm'].at[j]) for j in range(self.chunks)]
        self.wa_ready, self.wm_ready = False, [False] * self.chunks
        self.a_core, self.a_across, self.a_yz, self.z_core, self.early, self.out_copies = {}, {}, {}, {}, {}, []
        self.sq = {}

    def constants(self):
        lanes = self.s['u'].shape[1]
        self.gain_copy.wait()
        gain = jnp.broadcast_to(self.s['gain_in'][self.layer:self.layer + 1, :].astype(F32), (lanes, self.depth)).T
        self.s['gain'][...] = gain
        self.s['even'][...], self.s['odd'][...] = spread_matrices(self.depth)

    def send_squares(self, p, h_t, to):
        s = self.s
        s['sq_send'][p] = jnp.broadcast_to(jnp.sum(h_t * h_t, axis=0, keepdims=True), s['sq_send'].shape[1:])
        self.sq[p] = [self.links.push(s['sq_send'].at[p], s['sq_recv'].at[p, k], k) for k in to]

    def normalize(self, p, h_t, to):
        s, links = self.s, self.links
        for c in self.sq[p]:
            c.wait_recv()
        total = s['sq_send'][p]
        for k in sorted(to):
            total = total + s['sq_recv'][p, k]
        inv_rms = lax.rsqrt(total[:1] / self.model_dim + NORM_EPS)
        s['u'][p] = (h_t * inv_rms * s['gain'][...]).T.astype(BF16)
        shard = s['u'].shape[1] // 4
        u = jnp.concatenate([s['u'][p, pl.ds(pl.multiple_of(b * shard, shard), shard), :] for b in links.blocks], axis=0)
        s['u_rel'][p] = u
        if not self.wa_ready:
            self.wa.wait()
            self.wa_ready = True
        s['a_part'][p] = dot(u, s['wa'][...]).astype(BF16)
        self.a_core[p] = links.push(s['a_part'].at[p, pl.ds(0, 2 * shard)], s['a_core'].at[p], PARTNER)

    def spread(self, p):
        s = self.s
        u = s['u_rel'][p]
        gate, up = dot(u, s['even'][...]).astype(BF16), dot(u, s['odd'][...]).astype(BF16)
        shard = u.shape[0] // 4
        for k in range(4):
            s['u2'][p, 2 * k * shard:(2 * k + 1) * shard] = gate[k * shard:(k + 1) * shard]
            s['u2'][p, (2 * k + 1) * shard:(2 * k + 2) * shard] = up[k * shard:(k + 1) * shard]

    def attend_core(self, p):
        s = self.s
        half = s['a_core'].shape[1]
        self.a_core[p].wait_recv()
        s['a_sum'][p] = (s['a_part'][p, half:].astype(F32) + s['a_core'][p].astype(F32)).astype(BF16)
        self.a_across[p] = self.links.push(s['a_sum'].at[p, pl.ds(0, half // 2)], s['a_across'].at[p], ACROSS)

    def attend_across(self, p):
        s, y = self.s, self.links.y
        shard, seqs = s['a_across'].shape[1], s['a_yz'].shape[1]
        self.a_across[p].wait_recv()
        s['a_full'][p] = (s['a_sum'][p, shard:].astype(F32) + s['a_across'][p].astype(F32)).astype(BF16)
        self.a_yz[p] = self.links.push(s['a_full'].at[p, pl.ds(pl.multiple_of((1 - y) * seqs, seqs), seqs)], s['a_yz'].at[p], YZ)
        self.out_copies.append(self.links.copy(
            s['a_full'].at[p, pl.ds(pl.multiple_of(y * seqs, seqs), seqs)], self.qkv_out.at[y, pl.ds(p * seqs, seqs)]))

    def attend_yz(self, p):
        s, y = self.s, self.links.y
        seqs = s['a_yz'].shape[1]
        self.a_yz[p].wait_recv()
        self.out_copies.append(self.links.copy(s['a_yz'].at[p], self.qkv_out.at[1 - y, pl.ds(p * seqs, seqs)]))

    def project(self, p, j):
        s = self.s
        if not self.wm_ready[j]:
            self.wm[j].wait()
            self.wm_ready[j] = True
        s['z_part'][p, j] = dot(s['u2'][p], s['wm'][j].reshape(2 * self.depth, self.cols)).astype(BF16)
        half = s['z_recv'].shape[2]
        self.z_core[p, j] = self.links.push(s['z_part'].at[p, j, pl.ds(0, half)], s['z_recv'].at[p, j], PARTNER)

    def combine(self, p, j):
        s, unit = self.s, p * self.chunks + j
        half = s['z_recv'].shape[2]
        shard2 = half // 2
        self.z_core[p, j].wait_recv()
        s['z_x'][unit] = (s['z_part'][p, j, half:half + shard2].astype(F32) + s['z_recv'][p, j, :shard2].astype(F32)).astype(BF16)
        if unit < EARLY:
            self.early[unit] = self.links.push(s['z_x'].at[unit], s['z_early'].at[unit], ACROSS)
        else:
            self.out_copies.append(self.links.copy(s['z_x'].at[unit], self.zsend_out.at[unit - EARLY]))
        s['z_mine'][unit] = (s['z_part'][p, j, half + shard2:].astype(F32) + s['z_recv'][p, j, shard2:].astype(F32)).astype(BF16)
        if unit >= EARLY:
            self.out_copies.append(self.links.copy(s['z_mine'].at[unit], self.zmine_out.at[unit]))

    def finish(self):
        s = self.s
        for unit in range(EARLY):
            self.early[unit].wait_recv()
            s['z_mine'][unit] = (s['z_mine'][unit].astype(F32) + s['z_early'][unit].astype(F32)).astype(BF16)
            self.out_copies.append(self.links.copy(s['z_mine'].at[unit], self.zmine_out.at[unit]))
        for p in range(PARTS):
            self.attend_yz(p)
        for c in self.out_copies:
            c.wait()

    def run(self, steps):
        for name, *args in steps:
            getattr(self, name)(*args)


class Back:
    def __init__(self, links, layer, h_hbm, o_hbm, zgot_hbm, zmine_hbm, wd_hbm, wo_hbm, whole, s):
        self.links, self.s, self.whole = links, s, whole
        self.chunks, cols, _ = s['wd'].shape
        self.z = []
        for unit in range(PARTS * self.chunks):
            self.z.append([links.copy(zmine_hbm.at[unit], s['z_in'].at[unit])])
            if unit >= EARLY:
                self.z[-1].append(links.copy(zgot_hbm.at[unit - EARLY], s['z_got'].at[unit - EARLY]))
            if unit == 0:
                self.o_copy = links.copy(o_hbm, s['o_in'])
                self.h_copy = links.copy(h_hbm, s['h_in'])
        self.wd = [links.copy(wd_hbm.at[layer, pl.ds(j * cols, cols)], s['wd'].at[j]) for j in range(self.chunks)]
        self.wo = links.copy(wo_hbm.at[layer], s['wo'])
        self.wo_ready, self.wd_ready = False, [False] * self.chunks
        self.across, self.partner, self.diag = {}, {}, {}
        self.o_across, self.o_partner, self.o_diag = {}, {}, {}
        self.up = {}

    def mix(self, p, j):
        s, unit = self.s, p * self.chunks + j
        for c in self.z[unit]:
            c.wait()
        z = s['z_in'][unit].astype(F32)
        if unit >= EARLY:
            z = (z + s['z_got'][unit - EARLY].astype(F32)).astype(BF16).astype(F32)
        shard = z.shape[0] // 2
        gate, up = z[:shard], z[shard:]
        s['m'][p, j, OWN * shard:] = (gate * jax.nn.sigmoid(gate) * up).astype(BF16)

    def block(self, p, j, k):
        shard = self.s['m'].shape[2] // 4
        return self.s['m'].at[p, j, pl.ds(k * shard, shard)]

    def send(self, p, j):
        self.across[p, j] = self.links.push(self.block(p, j, OWN), self.block(p, j, ACROSS), ACROSS)
        self.partner[p, j] = self.links.push(self.block(p, j, OWN), self.block(p, j, PARTNER), PARTNER)

    def forward(self, p, j):
        self.across[p, j].wait_recv()
        self.diag[p, j] = self.links.push(self.block(p, j, ACROSS), self.block(p, j, DIAG), PARTNER)

    def send_o_yz(self):
        y, s = self.links.y, self.s
        self.o_copy.wait()
        self.o_yz = self.links.push(s['o_in'].at[1 - y], s['o_yz'], YZ)

    def o_block(self, p, k):
        shard = self.s['o'].shape[1] // 4
        return self.s['o'].at[p, pl.ds(k * shard, shard)]

    def send_o(self):
        y, s = self.links.y, self.s
        self.o_yz.wait_recv()
        shard = s['o'].shape[1] // 4
        seqs = shard // 2
        for p in range(PARTS):
            s['o'][p, pl.ds(OWN * shard + pl.multiple_of(y * seqs, seqs), seqs), :] = s['o_in'][y, p * seqs:(p + 1) * seqs]
            s['o'][p, pl.ds(OWN * shard + pl.multiple_of((1 - y) * seqs, seqs), seqs), :] = s['o_yz'][p * seqs:(p + 1) * seqs]
            self.o_across[p] = self.links.push(self.o_block(p, OWN), self.o_block(p, ACROSS), ACROSS)
            self.o_partner[p] = self.links.push(self.o_block(p, OWN), self.o_block(p, PARTNER), PARTNER)

    def forward_o(self, p):
        self.o_across[p].wait_recv()
        self.o_diag[p] = self.links.push(self.o_block(p, ACROSS), self.o_block(p, DIAG), PARTNER)

    def project_o(self, p):
        s = self.s
        self.o_partner[p].wait_recv()
        self.o_diag[p].wait_recv()
        if not self.wo_ready:
            self.wo.wait()
            self.wo_ready = True
        s['acc'][p] += dot(s['o'][p], s['wo'][...])

    def down(self, p, j):
        s = self.s
        self.partner[p, j].wait_recv()
        self.diag[p, j].wait_recv()
        if not self.wd_ready[j]:
            self.wd[j].wait()
            self.wd_ready[j] = True
        part = dot(s['m'][p, j], s['wd'][j])
        if j == 0:
            s['acc'][p] = part
        else:
            s['acc'][p] += part

    def send_update(self, p):
        s, links = self.s, self.links
        shard = s['acc'].shape[1] // 4
        for k in range(4):
            s['update'][p, pl.ds(pl.multiple_of(links.blocks[k] * shard, shard), shard), :] = s['acc'][p, k * shard:(k + 1) * shard, :]
        s['up_part'][p] = s['update'][p].T.astype(BF16)
        if self.whole:
            src = s['up_part'].at[p]
        else:
            part = s['up_recv'].shape[1]
            src = s['up_part'].at[p, pl.ds(pl.multiple_of((1 - links.y) * part, part), part)]
        self.up[p] = links.push(src, s['up_recv'].at[p], YZ)

    def update(self, p):
        s, links = self.s, self.links
        self.up[p].wait_recv()
        if self.whole:
            own = s['up_part'][p]
        else:
            part = s['up_recv'].shape[1]
            own = s['up_part'][p, pl.ds(pl.multiple_of(links.y * part, part), part), :]
        return own.astype(F32) + s['up_recv'][p].astype(F32)

    def open(self):
        links, chunks = self.links, self.chunks
        self.mix(0, 0)
        links.meet()
        self.send_o_yz()
        self.send(0, 0)
        for j in range(1, chunks):
            self.mix(0, j)
            self.send(0, j)
            if j == 2:
                self.send_o()
        if chunks < 3:
            self.send_o()
        for j in range(chunks):
            self.mix(1, j)
            self.send(1, j)


def start_kernel(names, model_dim, h_hbm, gain_hbm, wa_hbm, wm_hbm, qkv_out, zsend_out, zmine_out, h_out, *scratch):
    s = dict(zip(names, scratch))
    links = Links(s['send'], s['recv'], s['local'], True)
    h_copy = links.copy(h_hbm, s['h_in'])
    f = Front(links, 0, gain_hbm, wa_hbm, wm_hbm, model_dim, (qkv_out, zsend_out, zmine_out), s)
    part, rows = h_hbm.shape
    lanes = rows // PARTS
    mine = pl.ds(pl.multiple_of(links.y * part, part), part)
    order = part_order(rows, False)
    h_copy.wait()
    own = dot(s['h_in'][...], order)
    for p in range(PARTS):
        s['h'][p, mine, :] = own[:, p * lanes:(p + 1) * lanes].astype(BF16)
    links.meet()
    h_yz = [links.push(s['h'].at[p, mine], s['h'].at[p, mine], YZ) for p in range(PARTS)]
    to = [k for k in range(8) if k != OWN]
    for p in range(PARTS):
        f.send_squares(p, own[:, p * lanes:(p + 1) * lanes], to)
    f.constants()
    for p in range(PARTS):
        h_yz[p].wait_recv()
        f.out_copies.append(links.copy(s['h'].at[p], h_out.at[p]))
        f.normalize(p, s['h'][p].astype(F32), to)
    f.spread(0)
    f.project(0, 0)
    f.attend_core(0)
    f.attend_core(1)
    f.spread(1)
    finish_front(f)
    links.drain()


def finish_front(f, begun=1):
    units = [(p, j) for p in range(PARTS) for j in range(f.chunks)]
    for n in range(begun, len(units)):
        f.project(*units[n])
        f.combine(*units[n - 1])
        if n == 5:
            f.attend_across(0)
        if n == 7:
            f.attend_across(1)
    f.combine(*units[-1])
    f.finish()


def middle_kernel(names, model_dim, h_hbm, o_hbm, gain_hbm, zmine_hbm, zgot_hbm, wd_hbm, wo_hbm, wa_hbm, wm_hbm, qkv_out, zsend_out,
                  zmine_out, h_out, *scratch):
    s = dict(zip(names, scratch))
    links = Links(s['send'], s['recv'], s['local'], False)
    b = Back(links, 0, h_hbm, o_hbm, zgot_hbm, zmine_hbm, wd_hbm, wo_hbm, True, s)
    f = Front(links, 1, gain_hbm, wa_hbm, wm_hbm, model_dim, (qkv_out, zsend_out, zmine_out), s)
    to = (DIAG, PARTNER, ACROSS)
    b.open()
    f.constants()
    b.h_copy.wait()

    def new_h(p):
        h = (s['h_in'][p].astype(F32) + b.update(p)).astype(BF16)
        s['h'][p] = h
        f.out_copies.append(links.copy(s['h'].at[p], h_out.at[p]))
        f.send_squares(p, h.astype(F32), to)

    first_part(b)
    second_part(b, lambda: new_h(0), lambda: f.normalize(0, s['h'][0].astype(F32), to))
    f.spread(0)
    f.attend_core(0)
    f.project(0, 0)
    new_h(1)
    f.project(0, 1)
    f.combine(0, 0)
    f.project(0, 2)
    f.combine(0, 1)
    f.normalize(1, s['h'][1].astype(F32), to)
    f.spread(1)
    f.project(0, 3)
    f.combine(0, 2)
    f.attend_core(1)
    finish_front(f, 4)
    links.drain()


def first_part(b):
    for j in range(b.chunks):
        b.forward(0, j)
        if j == 2:
            b.forward_o(0)
            b.forward_o(1)
        if j >= 1:
            b.down(0, j - 1)
    b.forward(1, 0)
    b.down(0, b.chunks - 1)
    b.project_o(0)
    b.send_update(0)


def second_part(b, when_updated, when_squared):
    for j in range(1, b.chunks):
        b.forward(1, j)
        b.down(1, j - 1)
        if j == 1:
            b.project_o(1)
        if j == b.chunks - 2:
            when_updated()
    b.down(1, b.chunks - 1)
    b.send_update(1)
    when_squared()


def end_kernel(names, h_hbm, o_hbm, zmine_hbm, zgot_hbm, wd_hbm, wo_hbm, h_out, *scratch):
    s = dict(zip(names, scratch))
    links = Links(s['send'], s['recv'], s['local'], False)
    b = Back(links, 1, h_hbm, o_hbm, zgot_hbm, zmine_hbm, wd_hbm, wo_hbm, False, s)
    part, rows = h_out.shape
    own_rows = pl.ds(pl.multiple_of(links.y * part, part), part)
    b.open()
    b.h_copy.wait()

    def new_h(p):
        return (s['h_in'][p, own_rows, :].astype(F32) + b.update(p)).astype(BF16)

    first_part(b)
    kept = []
    second_part(b, lambda: kept.append(new_h(0)), lambda: None)
    order = part_order(rows, True)
    h_new = jnp.concatenate(kept + [new_h(1)], axis=1)
    h_out[...] = dot(h_new, order).astype(BF16)
    links.drain()


def attention_kernel(layer, per_step, len_hbm, qkv_hbm, k_hbm, v_hbm, *rest):
    k_out, v_out, o_hbm, kbuf, vbuf, q_scr, o_scr, qkv_ref, o_ref, len_ref, in_sem, out_sem, small_sem = rest[-13:]
    num_seqs, kv_heads, cache_len, head_dim = kbuf.shape
    slots = qkv_ref.shape[2] // head_dim
    rows = kv_heads * slots
    scale = head_dim ** -0.5

    def load(i):
        return (pltpu.make_async_copy(k_hbm.at[layer, i], kbuf.at[i], in_sem.at[0, i]),
                pltpu.make_async_copy(v_hbm.at[layer, i], vbuf.at[i], in_sem.at[1, i]))

    def store(i):
        return (pltpu.make_async_copy(kbuf.at[i], k_out.at[layer, i], out_sem.at[0, i]),
                pltpu.make_async_copy(vbuf.at[i], v_out.at[layer, i], out_sem.at[1, i]))

    qkv_copy = pltpu.make_async_copy(qkv_hbm, qkv_ref, small_sem.at[0])
    len_copy = pltpu.make_async_copy(len_hbm, len_ref, small_sem.at[1])
    qkv_copy.start()
    len_copy.start()

    @pl.loop(0, num_seqs)
    def _(i):
        for c in load(i):
            c.start()

    qkv_copy.wait()
    len_copy.wait()
    for head in range(kv_heads):
        for j in range(slots):
            q_scr[pl.ds(head * slots + j, num_seqs, stride=rows), :] = (
                qkv_ref[head, :, j * head_dim:(j + 1) * head_dim].astype(F32))

    tile_row = lax.broadcasted_iota(jnp.int32, (16, head_dim), 0)
    position = lax.broadcasted_iota(jnp.int32, (rows, cache_len), 1)

    @pl.loop(0, num_seqs // per_step)
    def _(step):
        group = [step * per_step + sub for sub in range(per_step)]
        for i in group:
            for c in load(i):
                c.wait()
            length = len_ref[i]
            base = pl.multiple_of((length // 16) * 16, 16)
            hit = tile_row == length - base
            for head in range(kv_heads):
                for buf, j in ((kbuf, slots - 2), (vbuf, slots - 1)):
                    new = q_scr[pl.ds(i * rows + head * slots + j, 1), :]
                    old = buf[i, head, pl.ds(base, 16), :].astype(F32)
                    buf[i, head, pl.ds(base, 16), :] = jnp.where(hit, new, old).astype(buf.dtype)
            for c in store(i):
                c.start()
        scores, probs = [], []
        for i in group:
            q = q_scr[pl.ds(pl.multiple_of(i * rows, rows), rows), :].astype(BF16)
            by_head = [lax.dot_general(q, kbuf[i, head], (((1,), (1,)), ((), ())), preferred_element_type=F32)
                       for head in range(kv_heads)]
            scores.append(jnp.concatenate([by_head[head][head * slots:(head + 1) * slots] for head in range(kv_heads)], axis=0))
        for i, score in zip(group, scores):
            score = jnp.where(position <= len_ref[i], score * scale, -1e30)
            e = jnp.exp(score - jnp.max(score, axis=1, keepdims=True))
            probs.append((e / jnp.sum(e, axis=1, keepdims=True)).astype(BF16))
        for i, p in zip(group, probs):
            by_head = [dot(p, vbuf[i, head]) for head in range(kv_heads)]
            o_scr[pl.ds(pl.multiple_of(i * rows, rows), rows), :] = jnp.concatenate(
                [by_head[head][head * slots:(head + 1) * slots] for head in range(kv_heads)], axis=0)

    for head in range(kv_heads):
        for j in range(slots - 2):
            o_ref[head, :, j * head_dim:(j + 1) * head_dim] = (
                o_scr[pl.ds(head * slots + j, num_seqs, stride=rows), :].astype(o_ref.dtype))
    o_copy = pltpu.make_async_copy(o_ref, o_hbm, small_sem.at[2])
    o_copy.start()

    @pl.loop(0, num_seqs)
    def _(i):
        for c in store(i):
            c.wait()

    o_copy.wait()


VMEM = pl.BlockSpec(memory_space=pltpu.VMEM)
HBM = pl.BlockSpec(memory_space=pltpu.HBM)


def attention(layer, lengths, qkv, k_cache, v_cache, outs):
    layers, num_seqs, kv_heads, cache_len, head_dim = k_cache.shape
    slots = qkv.shape[2] // head_dim
    rows = kv_heads * slots
    return pl.pallas_call(
        functools.partial(attention_kernel, layer, 2),
        out_shape=(jax.ShapeDtypeStruct(k_cache.shape, k_cache.dtype), jax.ShapeDtypeStruct(v_cache.shape, v_cache.dtype),
                   jax.ShapeDtypeStruct((kv_heads, num_seqs, (slots - 2) * head_dim), BF16)),
        in_specs=[HBM] * (4 + len(outs)),
        out_specs=(HBM, HBM, HBM),
        scratch_shapes=[pltpu.VMEM((num_seqs, kv_heads, cache_len, head_dim), BF16)] * 2
        + [pltpu.VMEM((num_seqs * rows, head_dim), F32)] * 2 + [
            pltpu.VMEM(qkv.shape, BF16), pltpu.VMEM((kv_heads, num_seqs, (slots - 2) * head_dim), BF16),
            pltpu.SMEM((num_seqs,), jnp.int32)]
        + [pltpu.SemaphoreType.DMA((2, num_seqs))] * 2 + [pltpu.SemaphoreType.DMA((3,))],
        input_output_aliases={4: 0, 5: 1} if outs else {},
        compiler_params=pltpu.CompilerParams(vmem_limit_bytes=VMEM_LIMIT),
        cost_estimate=pl.CostEstimate(flops=10 ** 10, bytes_accessed=8 * num_seqs * kv_heads * cache_len * head_dim, transcendentals=0),
        name=f'attention_{layer}',
    )(lengths, qkv, k_cache, v_cache, *outs)


def solution(mesh):
    seq_axes = ('rep', 'x', 'yz')
    hidden_spec = P('rep', ('x', 'yz'))
    cache_spec = P(None, seq_axes, None, None, None)
    in_specs = (hidden_spec, P(None, 'x'), P(None, 'x', 'yz'), P(None, 'x', None, 'yz'), P(None, 'yz', 'x'), P(None, 'yz', 'x'), cache_spec, cache_spec, P(seq_axes))
    out_specs = (hidden_spec, cache_spec, cache_spec)
    swap = [(0, 2), (2, 0), (1, 3), (3, 1)]

    def device_step(hidden, norm_gain, w_attn, w_mlp, w_out, w_down, k_cache, v_cache, lengths):
        rows, part = hidden.shape
        depth, attn_cols = w_attn.shape[1:]
        model_dim = depth * mesh.shape['x']
        mlp_cols = w_mlp.shape[3]
        out_depth = w_out.shape[1]
        cols = mlp_cols // CHUNKS
        units = CHUNKS * PARTS
        lanes = rows // PARTS
        half, shard = lanes // 2, lanes // 4
        seqs = shard // 2
        num_seqs = PARTS * seqs
        sems = pltpu.SemaphoreType.DMA((80,))
        common = {'send': sems, 'recv': sems, 'local': sems}
        front_scratch = {
            'sq_send': pltpu.VMEM((PARTS, 8, lanes), F32), 'sq_recv': pltpu.VMEM((PARTS, 8, 8, lanes), F32),
            'h': pltpu.VMEM((PARTS, depth, lanes), BF16), 'gain_in': pltpu.VMEM(norm_gain.shape, BF16), 'gain': pltpu.VMEM((depth, lanes), F32),
            'even': pltpu.VMEM((depth, 2 * depth), BF16), 'odd': pltpu.VMEM((depth, 2 * depth), BF16),
            'u': pltpu.VMEM((PARTS, lanes, depth), BF16), 'u_rel': pltpu.VMEM((PARTS, lanes, depth), BF16),
            'wa': pltpu.VMEM((depth, attn_cols), BF16), 'wm': pltpu.VMEM((CHUNKS, depth, 2, cols), BF16),
            'a_part': pltpu.VMEM((PARTS, lanes, attn_cols), BF16), 'a_core': pltpu.VMEM((PARTS, half, attn_cols), BF16),
            'a_sum': pltpu.VMEM((PARTS, half, attn_cols), BF16), 'a_across': pltpu.VMEM((PARTS, shard, attn_cols), BF16),
            'a_full': pltpu.VMEM((PARTS, shard, attn_cols), BF16), 'a_yz': pltpu.VMEM((PARTS, seqs, attn_cols), BF16),
            'u2': pltpu.VMEM((PARTS, 2 * lanes, 2 * depth), BF16), 'z_part': pltpu.VMEM((PARTS, CHUNKS, 2 * lanes, cols), BF16),
            'z_recv': pltpu.VMEM((PARTS, CHUNKS, lanes, cols), BF16), 'z_x': pltpu.VMEM((units, half, cols), BF16),
            'z_mine': pltpu.VMEM((units, half, cols), BF16), 'z_early': pltpu.VMEM((EARLY, half, cols), BF16),
        }

        def back_scratch(whole):
            return {
                'o_yz': pltpu.VMEM((num_seqs, out_depth), BF16), 'o': pltpu.VMEM((PARTS, lanes, out_depth), BF16),
                'm': pltpu.VMEM((PARTS, CHUNKS, lanes, cols), BF16), 'z_in': pltpu.VMEM((units, half, cols), BF16),
                'z_got': pltpu.VMEM((units - EARLY, half, cols), BF16), 'o_in': pltpu.VMEM((2, num_seqs, out_depth), BF16),
                'h_in': pltpu.VMEM((PARTS, depth, lanes), BF16),
                'wd': pltpu.VMEM((CHUNKS, cols, depth), BF16), 'wo': pltpu.VMEM((out_depth, depth), BF16),
                'acc': pltpu.VMEM((PARTS, lanes, depth), F32), 'update': pltpu.VMEM((PARTS, lanes, depth), F32),
                'up_part': pltpu.VMEM((PARTS, depth, lanes), BF16),
                'up_recv': pltpu.VMEM((PARTS, depth if whole else part, lanes), BF16),
            }

        front_shapes = (
            jax.ShapeDtypeStruct((2, num_seqs, attn_cols), BF16), jax.ShapeDtypeStruct((units - EARLY, half, cols), BF16),
            jax.ShapeDtypeStruct((units, half, cols), BF16), jax.ShapeDtypeStruct((PARTS, depth, lanes), BF16))
        front_specs = (HBM,) * 4

        def call(kernel, name, collective_id, scratch, in_specs, out_shape, out_specs, *args):
            return pl.pallas_call(
                functools.partial(kernel, tuple(scratch)), out_shape=out_shape, in_specs=list(in_specs), out_specs=out_specs,
                scratch_shapes=list(scratch.values()), name=name,
                compiler_params=pltpu.CompilerParams(collective_id=collective_id, has_side_effects=True, vmem_limit_bytes=VMEM_LIMIT),
            )(*args)

        def start(names, *refs):
            start_kernel(names, model_dim, *refs)

        def middle(names, *refs):
            middle_kernel(names, model_dim, *refs)

        qkv, zsend, zmine, h_block = call(
            start, 'start', 0, {**common, **front_scratch, 'h_in': pltpu.VMEM((part, rows), BF16)}, (HBM,) * 4,
            front_shapes, front_specs, hidden.T, norm_gain, w_attn, w_mlp)
        zgot = lax.ppermute(zsend, 'x', swap)
        k_new, v_new, o = attention(0, lengths, qkv, k_cache, v_cache, ())
        qkv, zsend, zmine, h_block = call(
            middle, 'middle', 1, {**common, **front_scratch, **back_scratch(True)}, (HBM,) * 9,
            front_shapes, front_specs, h_block, o, norm_gain, zmine, zgot, w_down, w_out, w_attn, w_mlp)
        zgot = lax.ppermute(zsend, 'x', swap)
        k_new, v_new, o = attention(1, lengths, qkv, k_cache, v_cache, (k_new, v_new))
        h_out = call(
            end_kernel, 'end', 2, {**common, **back_scratch(False)}, (HBM,) * 6,
            jax.ShapeDtypeStruct((part, rows), BF16), VMEM, h_block, o, zmine, zgot, w_down, w_out)
        return h_out.T, k_new, v_new

    return jax.shard_map(device_step, mesh=mesh, in_specs=in_specs, out_specs=out_specs, check_vma=False)
```

time: 155 us -> 141 us (0.910)
  Pallas kernels: 146 us -> 135 us
  local copies, waits for them, and re-layouts: 7.12 us -> 3.4 us
    pallas_call x3, Pallas kernels: 96.6 us -> 86.6 us  [call(): pl.pallas_call(functools.partial(kernel, tuple(scratch)), out_shape=out_s...]
    unnamed x17 -> x5, local copies, waits for them, and re-layouts: 7.12 us -> 3.4 us
  transfers between devices with their start and end apart: 2 -> 2, of which waited for: 0 -> 0; matrix products, arithmetic and copies ran while one was open for 0% -> 0% of each run, Pallas kernels for 32% -> 35%
where the time goes in v2:
time: 141 us
  Pallas kernels  135 us (96%)
  local copies, waits for them, and re-layouts  3.4 us (2%)
  starting transfers between devices  1.43 us (1%)
    pallas_call x3, Pallas kernels, call(): pl.pallas_call(functools.partial(kernel, tuple(scratch)), out_shape=out_s...  86.6 us
    pallas_call x2, Pallas kernels, attention(): pl.pallas_call(functools.partial(attention_kernel, layer, 2), out_shape=(...  48.5 us
    unnamed x5, local copies, waits for them, and re-layouts  3.4 us
  transfers between devices with their start and end apart: 2, of which 0 were waited for; matrix products, arithmetic and copies ran while one was open for 0% of the time, Pallas kernels for 35%

profile of v2, /device:TPU:0, one launch (start us, length us, event | category | flops | bytes accessed | tf_op | source)
XLA Modules:
  0.0 140.7 jit_solution(12532131933199022523)
XLA Ops:
  0.6 23.5 %start.1 = (bf16[2,32,1024]{2,1,0:T(8,128)(2,1)}, bf16[8,64,896]{2,1,0:T(8,128)(2,1)}, bf16[10,64,896]{2,1,0:T(8,128)(2,1)}, bf16[2,384,128]{2,1,0:T(8,128)(2,1)}) custom-call(bf16[192,256]{1,0:T(8,128)(2,1)} %bitcast.3, bf16[2,384]{1,0:T(2,128)(2,1)} %refs_2_.3, bf16[2,384,1024]{2,1,0:T(8,128)(2,1)} %refs_7_.1, bf16[2,384,2,4480]{3,2,1,0:T(2,128)(2,1)} %refs_8_.1), custom_call_target="tpu_custom_call" | custom-call | tf_op jit(solution)/shard_map/start/pallas_call | solution.py:617
  24.1 0.6 collective-permute-start
  24.7 24.2 %attention_0.1 = (bf16[2,32,2,1024,128]{4,3,2,1,0:T(8,128)(2,1)}, bf16[2,32,2,1024,128]{4,3,2,1,0:T(8,128)(2,1)}, bf16[2,32,768]{2,1,0:T(8,128)(2,1)}) custom-call(s32[32]{0:T(128)} %len_hbm.3, bf16[2,32,1024]{2,1,0:T(8,128)(2,1)} %get-tuple-element.18.qkv_hbm, bf16[2,32,2,1024,128]{4,3,2,1,0:T(8,128)(2,1)} %k_hbm.3, bf16[2,32,2,1024,128]{4,3,2,1,0:T(8,128)(2,1)} %v_hbm.3), custom_call_target="tpu_custom_call" | custom-call | flops 10000000000 | bytes 67108864 | tf_op jit(solution)/shard_map/attention_0/pallas_call | solution.py:545
  48.9 0.0 collective-permute-done.refs_4_
  48.9 0.0 copy-start.1
  48.9 0.9 copy-done.1
  49.8 38.3 %middle.1 = (bf16[2,32,1024]{2,1,0:T(8,128)(2,1)}, bf16[8,64,896]{2,1,0:T(8,128)(2,1)}, bf16[10,64,896]{2,1,0:T(8,128)(2,1)}, bf16[2,384,128]{2,1,0:T(8,128)(2,1)}) custom-call(bf16[2,384,128]{2,1,0:T(8,128)(2,1)} %get-tuple-element.17.refs_0_, bf16[2,32,768]{2,1,0:T(8,128)(2,1)} %get-tuple-element.19.refs_1_, bf16[2,384]{1,0:T(2,128)(2,1)} %refs_2_.3, ...), custom_call_target="tpu_custom_call" | custom-call | tf_op jit(solution)/shard_map/middle/pallas_call | solution.py:617
  88.2 0.8 collective-permute-start.1
  89.0 24.4 %attention_1.1 = (bf16[2,32,2,1024,128]{4,3,2,1,0:T(8,128)(2,1)}, bf16[2,32,2,1024,128]{4,3,2,1,0:T(8,128)(2,1)}, bf16[2,32,768]{2,1,0:T(8,128)(2,1)}) custom-call(s32[32]{0:T(128)} %len_hbm.3, bf16[2,32,1024]{2,1,0:T(8,128)(2,1)} %get-tuple-element.23.qkv_hbm, bf16[2,32,2,1024,128]{4,3,2,1,0:T(8,128)(2,1)} %k_hbm.3, ...), custom_call_target="tpu_custom_call", output_to_operand_aliasing={{0}: (4, {}), {1}: (5, {})} | custom-call | flops 10000000000 | bytes 67108864 | tf_op jit(solution)/shard_map/attention_1/pallas_call | solution.py:545
  113.4 0.0 collective-permute-done.1.zgot_hbm
  113.4 0.0 copy-start
  113.4 0.9 copy-done
  114.4 24.8 %end.1 = bf16[192,256]{1,0:T(8,128)(2,1)} custom-call(bf16[2,384,128]{2,1,0:T(8,128)(2,1)} %get-tuple-element.22.h_hbm, bf16[2,32,768]{2,1,0:T(8,128)(2,1)} %get-tuple-element.26.o_hbm, bf16[10,64,896]{2,1,0:T(8,128)(2,1)} %get-tuple-element.27.zmine_hbm, bf16[8,64,896]{2,1,0:T(8,128)(2,1)} %copy-done, bf16[2,4480,384]{2,1,0:T(8,128)(2,1)} %wd_hbm.1, ...), custom_call_target="tpu_custom_call" | custom-call | tf_op jit(solution)/shard_map/end/pallas_call | solution.py:617
  139.2 1.5 %copy.17 = bf16[256,192]{0,1:T(8,128)(2,1)} copy(bf16[256,192]{0,1:T(8,128)(2,1)} %bitcast.2) | data formatting | bytes 196608
Async XLA Ops:
  24.1 24.8 %collective-permute-start = (bf16[8,64,896]{2,1,0:T(8,128)(2,1)}, bf16[8,64,896]{2,1,0:T(8,128)(2,1)S(1)}, u32[]{:S(2)}, u32[]{:S(2)}) collective-permute-start(bf16[8,64,896]{2,1,0:T(8,128)(2,1)} %get-tuple-element.21), channel_id=1, source_target_pairs={{0,2},{2,0},{1,3},{3,1},{4,6},{6,4},{5,7},{7,5}} | collective-permute-start | bytes 2752520 | tf_op jit(solution)/shard_map/ppermute | solution.py:632
  48.9 0.9 copy-start.1
  88.2 25.2 %collective-permute-start.1 = (bf16[8,64,896]{2,1,0:T(8,128)(2,1)}, bf16[8,64,896]{2,1,0:T(8,128)(2,1)S(1)}, u32[]{:S(2)}, u32[]{:S(2)}) collective-permute-start(bf16[8,64,896]{2,1,0:T(8,128)(2,1)} %get-tuple-element.28), channel_id=1, source_target_pairs={{0,2},{2,0},{1,3},{3,1},{4,6},{6,4},{5,7},{7,5}} | collective-permute-start | bytes 2752520 | tf_op jit(solution)/shard_map/ppermute | solution.py:637
  113.4 0.9 copy-start

commit v3 on v2

--- a/solution.py
+++ b/solution.py
@@ -13,8 +13,9 @@
 F32 = jnp.float32
 
 CHUNKS = 5
-EARLY = 2
-VMEM_LIMIT = 62 * 2 ** 20
+EARLY = 1
+LAG = 2
+VMEM_LIMIT = 67043328
 
 
 def dot(a, b):
@@ -24,7 +25,7 @@
 class Links:
     def __init__(self, send_sems, recv_sems, local_sems, everyone):
         self.send_sems, self.recv_sems, self.local_sems = send_sems, recv_sems, local_sems
-        self.sent, self.used, self.local_used = [], 0, 0
+        self.groups, self.used, self.local_groups, self.local_used = {}, 0, {}, 0
         x, y = lax.axis_index('x'), lax.axis_index('yz')
         self.x, self.y = x, y
         core = lax.rem(x, 2)
@@ -32,7 +33,7 @@
         self.blocks = self.along_x + (x,)
         self.targets = tuple({'x': p, 'yz': y} for p in self.blocks) + ({'x': x, 'yz': 1 - y},) + tuple(
             {'x': p, 'yz': 1 - y} for p in self.along_x)
-        self.peers = [k for k in range(8 if everyone else 5) if k != OWN]
+        self.peers = [k for k in range(8) if k != OWN] if everyone else [DIAG, PARTNER, ACROSS, YZ, ACROSS_YZ]
         self.barrier = pltpu.get_barrier_semaphore()
         for k in self.peers:
             pl.semaphore_signal(self.barrier, inc=1, device_id=self.targets[k], device_id_type=MESH)
@@ -40,29 +41,36 @@
     def meet(self):
         pl.semaphore_wait(self.barrier, len(self.peers))
 
-    def push(self, src, dst, to):
+    def push(self, src, dst, to, group):
         k = self.used
         self.used += 1
+        g = self.groups.setdefault(group, len(self.groups))
         copy = pltpu.make_async_remote_copy(
-            src_ref=src, dst_ref=dst, send_sem=self.send_sems.at[k], recv_sem=self.recv_sems.at[k],
+            src_ref=src, dst_ref=dst, send_sem=self.send_sems.at[g], recv_sem=self.recv_sems.at[k],
             device_id=self.targets[to], device_id_type=MESH)
         copy.start()
-        self.sent.append(copy)
         return copy
 
-    def copy(self, src, dst):
-        k = self.local_used
-        self.local_used += 1
+    def copy(self, src, dst, group=None):
+        if group is None or group not in self.local_groups:
+            k = self.local_used
+            self.local_used += 1
+            if group is not None:
+                self.local_groups[group] = k
+        else:
+            k = self.local_groups[group]
         copy = pltpu.make_async_copy(src, dst, self.local_sems.at[k])
         copy.start()
         return copy
 
-    def drain(self):
-        for copy in self.sent:
-            copy.wait_send()
-
-
-DIAG, PARTNER, ACROSS, OWN, YZ = 0, 1, 2, 3, 4
+    def drain(self, sent, stored):
+        for group, g in self.groups.items():
+            pltpu.make_async_copy(sent[group], sent[group], self.send_sems.at[g]).wait()
+        for group, k in self.local_groups.items():
+            pltpu.make_async_copy(stored[group], stored[group], self.local_sems.at[k]).wait()
+
+
+DIAG, PARTNER, ACROSS, OWN, YZ, ACROSS_YZ = 0, 1, 2, 3, 4, 7
 PARTS = 2
 
 
@@ -92,7 +100,7 @@
         self.wa = links.copy(wa_hbm.at[layer], s['wa'])
         self.wm = [links.copy(wm_hbm.at[layer, :, :, pl.ds(j * self.cols, self.cols)], s['wm'].at[j]) for j in range(self.chunks)]
         self.wa_ready, self.wm_ready = False, [False] * self.chunks
-        self.a_core, self.a_across, self.a_yz, self.z_core, self.early, self.out_copies = {}, {}, {}, {}, {}, []
+        self.a_core, self.a_got, self.z_core, self.early = {}, {}, {}, {}
         self.sq = {}
 
     def constants(self):
@@ -105,7 +113,7 @@
     def send_squares(self, p, h_t, to):
         s = self.s
         s['sq_send'][p] = jnp.broadcast_to(jnp.sum(h_t * h_t, axis=0, keepdims=True), s['sq_send'].shape[1:])
-        self.sq[p] = [self.links.push(s['sq_send'].at[p], s['sq_recv'].at[p, k], k) for k in to]
+        self.sq[p] = [self.links.push(s['sq_send'].at[p], s['sq_recv'].at[p, k], k, 'sq') for k in to]
 
     def normalize(self, p, h_t, to):
         s, links = self.s, self.links
@@ -123,7 +131,7 @@
             self.wa.wait()
             self.wa_ready = True
         s['a_part'][p] = dot(u, s['wa'][...]).astype(BF16)
-        self.a_core[p] = links.push(s['a_part'].at[p, pl.ds(0, 2 * shard)], s['a_core'].at[p], PARTNER)
+        self.a_core[p] = links.push(s['a_part'].at[p, pl.ds(0, 2 * shard)], s['a_core'].at[p], PARTNER, 'a_core')
 
     def spread(self, p):
         s = self.s
@@ -139,22 +147,24 @@
         half = s['a_core'].shape[1]
         self.a_core[p].wait_recv()
         s['a_sum'][p] = (s['a_part'][p, half:].astype(F32) + s['a_core'][p].astype(F32)).astype(BF16)
-        self.a_across[p] = self.links.push(s['a_sum'].at[p, pl.ds(0, half // 2)], s['a_across'].at[p], ACROSS)
-
-    def attend_across(self, p):
+        shard, seqs = half // 2, s['a_got'].shape[2]
+        y = self.links.y
+        here, there = pl.multiple_of(y * seqs, seqs), pl.multiple_of((1 - y) * seqs, seqs)
+        self.a_got[p] = [
+            self.links.push(s['a_sum'].at[p, pl.ds(there, seqs)], s['a_got'].at[p, 2], ACROSS_YZ, 'a_got'),
+            self.links.push(s['a_sum'].at[p, pl.ds(here, seqs)], s['a_got'].at[p, 0], ACROSS, 'a_got'),
+            self.links.push(s['a_sum'].at[p, pl.ds(shard + there, seqs)], s['a_got'].at[p, 1], YZ, 'a_got')]
+
+    def attend_ends(self, p):
         s, y = self.s, self.links.y
-        shard, seqs = s['a_across'].shape[1], s['a_yz'].shape[1]
-        self.a_across[p].wait_recv()
-        s['a_full'][p] = (s['a_sum'][p, shard:].astype(F32) + s['a_across'][p].astype(F32)).astype(BF16)
-        self.a_yz[p] = self.links.push(s['a_full'].at[p, pl.ds(pl.multiple_of((1 - y) * seqs, seqs), seqs)], s['a_yz'].at[p], YZ)
-        self.out_copies.append(self.links.copy(
-            s['a_full'].at[p, pl.ds(pl.multiple_of(y * seqs, seqs), seqs)], self.qkv_out.at[y, pl.ds(p * seqs, seqs)]))
-
-    def attend_yz(self, p):
-        s, y = self.s, self.links.y
-        seqs = s['a_yz'].shape[1]
-        self.a_yz[p].wait_recv()
-        self.out_copies.append(self.links.copy(s['a_yz'].at[p], self.qkv_out.at[1 - y, pl.ds(p * seqs, seqs)]))
+        shard, seqs = s['a_sum'].shape[1] // 2, s['a_got'].shape[2]
+        for c in self.a_got[p]:
+            c.wait_recv()
+        own = s['a_sum'][p, pl.ds(shard + pl.multiple_of(y * seqs, seqs), seqs), :]
+        s['a_full'][p, 0] = (own.astype(F32) + s['a_got'][p, 0].astype(F32)).astype(BF16)
+        s['a_full'][p, 1] = (s['a_got'][p, 1].astype(F32) + s['a_got'][p, 2].astype(F32)).astype(BF16)
+        for k, head in enumerate((y, 1 - y)):
+            self.links.copy(s['a_full'].at[p, k], self.qkv_out.at[head, pl.ds(p * seqs, seqs)], 'qkv')
 
     def project(self, p, j):
         s = self.s
@@ -163,7 +173,7 @@
             self.wm_ready[j] = True
         s['z_part'][p, j] = dot(s['u2'][p], s['wm'][j].reshape(2 * self.depth, self.cols)).astype(BF16)
         half = s['z_recv'].shape[2]
-        self.z_core[p, j] = self.links.push(s['z_part'].at[p, j, pl.ds(0, half)], s['z_recv'].at[p, j], PARTNER)
+        self.z_core[p, j] = self.links.push(s['z_part'].at[p, j, pl.ds(0, half)], s['z_recv'].at[p, j], PARTNER, 'z')
 
     def combine(self, p, j):
         s, unit = self.s, p * self.chunks + j
@@ -172,27 +182,24 @@
         self.z_core[p, j].wait_recv()
         s['z_x'][unit] = (s['z_part'][p, j, half:half + shard2].astype(F32) + s['z_recv'][p, j, :shard2].astype(F32)).astype(BF16)
         if unit < EARLY:
-            self.early[unit] = self.links.push(s['z_x'].at[unit], s['z_early'].at[unit], ACROSS)
+            self.early[unit] = self.links.push(s['z_x'].at[unit], s['z_early'].at[unit], ACROSS, 'early')
         else:
-            self.out_copies.append(self.links.copy(s['z_x'].at[unit], self.zsend_out.at[unit - EARLY]))
+            self.links.copy(s['z_x'].at[unit], self.zsend_out.at[unit - EARLY], 'z_x')
         s['z_mine'][unit] = (s['z_part'][p, j, half + shard2:].astype(F32) + s['z_recv'][p, j, shard2:].astype(F32)).astype(BF16)
         if unit >= EARLY:
-            self.out_copies.append(self.links.copy(s['z_mine'].at[unit], self.zmine_out.at[unit]))
+            self.links.copy(s['z_mine'].at[unit], self.zmine_out.at[unit], 'z_mine')
 
     def finish(self):
         s = self.s
         for unit in range(EARLY):
             self.early[unit].wait_recv()
             s['z_mine'][unit] = (s['z_mine'][unit].astype(F32) + s['z_early'][unit].astype(F32)).astype(BF16)
-            self.out_copies.append(self.links.copy(s['z_mine'].at[unit], self.zmine_out.at[unit]))
-        for p in range(PARTS):
-            self.attend_yz(p)
-        for c in self.out_copies:
-            c.wait()
-
-    def run(self, steps):
-        for name, *args in steps:
-            getattr(self, name)(*args)
+            self.links.copy(s['z_mine'].at[unit], self.zmine_out.at[unit], 'z_mine')
+
+    def sizes(self):
+        s = self.s
+        return ({'a_core': s['a_core'], 'a_got': s['a_got'], 'z': s['z_recv'], 'early': s['z_early']},
+                {'z_x': s['z_x'].at[pl.ds(EARLY, s['z_x'].shape[0] - EARLY)], 'z_mine': s['z_mine'], 'qkv': s['a_full'], 'h': s['h']})
 
 
 class Back:
@@ -230,17 +237,17 @@
         return self.s['m'].at[p, j, pl.ds(k * shard, shard)]
 
     def send(self, p, j):
-        self.across[p, j] = self.links.push(self.block(p, j, OWN), self.block(p, j, ACROSS), ACROSS)
-        self.partner[p, j] = self.links.push(self.block(p, j, OWN), self.block(p, j, PARTNER), PARTNER)
+        self.across[p, j] = self.links.push(self.block(p, j, OWN), self.block(p, j, ACROSS), ACROSS, 'm')
+        self.partner[p, j] = self.links.push(self.block(p, j, OWN), self.block(p, j, PARTNER), PARTNER, 'm')
 
     def forward(self, p, j):
         self.across[p, j].wait_recv()
-        self.diag[p, j] = self.links.push(self.block(p, j, ACROSS), self.block(p, j, DIAG), PARTNER)
+        self.diag[p, j] = self.links.push(self.block(p, j, ACROSS), self.block(p, j, DIAG), PARTNER, 'm')
 
     def send_o_yz(self):
         y, s = self.links.y, self.s
         self.o_copy.wait()
-        self.o_yz = self.links.push(s['o_in'].at[1 - y], s['o_yz'], YZ)
+        self.o_yz = self.links.push(s['o_in'].at[1 - y], s['o_yz'], YZ, 'o_yz')
 
     def o_block(self, p, k):
         shard = self.s['o'].shape[1] // 4
@@ -254,12 +261,12 @@
         for p in range(PARTS):
             s['o'][p, pl.ds(OWN * shard + pl.multiple_of(y * seqs, seqs), seqs), :] = s['o_in'][y, p * seqs:(p + 1) * seqs]
             s['o'][p, pl.ds(OWN * shard + pl.multiple_of((1 - y) * seqs, seqs), seqs), :] = s['o_yz'][p * seqs:(p + 1) * seqs]
-            self.o_across[p] = self.links.push(self.o_block(p, OWN), self.o_block(p, ACROSS), ACROSS)
-            self.o_partner[p] = self.links.push(self.o_block(p, OWN), self.o_block(p, PARTNER), PARTNER)
+            self.o_across[p] = self.links.push(self.o_block(p, OWN), self.o_block(p, ACROSS), ACROSS, 'o')
+            self.o_partner[p] = self.links.push(self.o_block(p, OWN), self.o_block(p, PARTNER), PARTNER, 'o')
 
     def forward_o(self, p):
         self.o_across[p].wait_recv()
-        self.o_diag[p] = self.links.push(self.o_block(p, ACROSS), self.o_block(p, DIAG), PARTNER)
+        self.o_diag[p] = self.links.push(self.o_block(p, ACROSS), self.o_block(p, DIAG), PARTNER, 'o')
 
     def project_o(self, p):
         s = self.s
@@ -294,7 +301,7 @@
         else:
             part = s['up_recv'].shape[1]
             src = s['up_part'].at[p, pl.ds(pl.multiple_of((1 - links.y) * part, part), part)]
-        self.up[p] = links.push(src, s['up_recv'].at[p], YZ)
+        self.up[p] = links.push(src, s['up_recv'].at[p], YZ, 'up')
 
     def update(self, p):
         s, links = self.s, self.links
@@ -305,6 +312,11 @@
             part = s['up_recv'].shape[1]
             own = s['up_part'][p, pl.ds(pl.multiple_of(links.y * part, part), part), :]
         return own.astype(F32) + s['up_recv'][p].astype(F32)
+
+    def sizes(self):
+        s = self.s
+        sent = 3 * s['m'].shape[2] // 4
+        return {'m': s['m'].at[:, :, pl.ds(0, sent)], 'o': s['o'].at[:, pl.ds(0, sent)], 'o_yz': s['o_yz'], 'up': s['up_recv']}
 
     def open(self):
         links, chunks = self.links, self.chunks
@@ -338,34 +350,34 @@
     for p in range(PARTS):
         s['h'][p, mine, :] = own[:, p * lanes:(p + 1) * lanes].astype(BF16)
     links.meet()
-    h_yz = [links.push(s['h'].at[p, mine], s['h'].at[p, mine], YZ) for p in range(PARTS)]
+    h_yz = [links.push(s['h'].at[p, mine], s['h'].at[p, mine], YZ, 'h') for p in range(PARTS)]
     to = [k for k in range(8) if k != OWN]
     for p in range(PARTS):
         f.send_squares(p, own[:, p * lanes:(p + 1) * lanes], to)
     f.constants()
     for p in range(PARTS):
         h_yz[p].wait_recv()
-        f.out_copies.append(links.copy(s['h'].at[p], h_out.at[p]))
+        links.copy(s['h'].at[p], h_out.at[p], 'h')
         f.normalize(p, s['h'][p].astype(F32), to)
     f.spread(0)
-    f.project(0, 0)
     f.attend_core(0)
+    f.spread(1)
     f.attend_core(1)
-    f.spread(1)
-    finish_front(f)
-    links.drain()
-
-
-def finish_front(f, begun=1):
+    finish_front(f, 0, {6: 0, 8: 1})
+    sent, stored = f.sizes()
+    links.drain({**sent, 'sq': s['sq_recv'].at[:, pl.ds(0, len(to))], 'h': s['h'].at[:, mine]}, stored)
+
+
+def finish_front(f, begun, exchanges):
     units = [(p, j) for p in range(PARTS) for j in range(f.chunks)]
     for n in range(begun, len(units)):
         f.project(*units[n])
-        f.combine(*units[n - 1])
-        if n == 5:
-            f.attend_across(0)
-        if n == 7:
-            f.attend_across(1)
-    f.combine(*units[-1])
+        if n >= LAG:
+            f.combine(*units[n - LAG])
+        if n in exchanges:
+            f.attend_ends(exchanges[n])
+    for n in range(len(units) - LAG, len(units)):
+        f.combine(*units[n])
     f.finish()
 
 
@@ -383,7 +395,7 @@
     def new_h(p):
         h = (s['h_in'][p].astype(F32) + b.update(p)).astype(BF16)
         s['h'][p] = h
-        f.out_copies.append(links.copy(s['h'].at[p], h_out.at[p]))
+        links.copy(s['h'].at[p], h_out.at[p], 'h')
         f.send_squares(p, h.astype(F32), to)
 
     first_part(b)
@@ -393,16 +405,19 @@
     f.project(0, 0)
     new_h(1)
     f.project(0, 1)
+    f.project(0, 2)
     f.combine(0, 0)
-    f.project(0, 2)
+    f.project(0, 3)
     f.combine(0, 1)
     f.normalize(1, s['h'][1].astype(F32), to)
     f.spread(1)
-    f.project(0, 3)
+    f.project(0, 4)
+    f.attend_core(1)
+    f.attend_ends(0)
     f.combine(0, 2)
-    f.attend_core(1)
-    finish_front(f, 4)
-    links.drain()
+    finish_front(f, 5, {9: 1})
+    sent, stored = f.sizes()
+    links.drain({**sent, **b.sizes(), 'sq': s['sq_recv'].at[:, pl.ds(0, len(to))]}, stored)
 
 
 def first_part(b):
@@ -413,10 +428,10 @@
             b.forward_o(1)
         if j >= 1:
             b.down(0, j - 1)
+    b.project_o(0)
+    b.down(0, b.chunks - 1)
+    b.send_update(0)
     b.forward(1, 0)
-    b.down(0, b.chunks - 1)
-    b.project_o(0)
-    b.send_update(0)
 
 
 def second_part(b, when_updated, when_squared):
@@ -450,7 +465,7 @@
     order = part_order(rows, True)
     h_new = jnp.concatenate(kept + [new_h(1)], axis=1)
     h_out[...] = dot(h_new, order).astype(BF16)
-    links.drain()
+    links.drain(b.sizes(), {})
 
 
 def attention_kernel(layer, per_step, len_hbm, qkv_hbm, k_hbm, v_hbm, *rest):
@@ -580,8 +595,11 @@
         half, shard = lanes // 2, lanes // 4
         seqs = shard // 2
         num_seqs = PARTS * seqs
-        sems = pltpu.SemaphoreType.DMA((80,))
-        common = {'send': sems, 'recv': sems, 'local': sems}
+
+        def semaphores(groups, remote, local):
+            return {'send': pltpu.SemaphoreType.DMA((groups,)), 'recv': pltpu.SemaphoreType.DMA((remote,)),
+                    'local': pltpu.SemaphoreType.DMA((local,))}
+
         front_scratch = {
             'sq_send': pltpu.VMEM((PARTS, 8, lanes), F32), 'sq_recv': pltpu.VMEM((PARTS, 8, 8, lanes), F32),
             'h': pltpu.VMEM((PARTS, depth, lanes), BF16), 'gain_in': pltpu.VMEM(norm_gain.shape, BF16), 'gain': pltpu.VMEM((depth, lanes), F32),
@@ -589,8 +607,8 @@
             'u': pltpu.VMEM((PARTS, lanes, depth), BF16), 'u_rel': pltpu.VMEM((PARTS, lanes, depth), BF16),
             'wa': pltpu.VMEM((depth, attn_cols), BF16), 'wm': pltpu.VMEM((CHUNKS, depth, 2, cols), BF16),
             'a_part': pltpu.VMEM((PARTS, lanes, attn_cols), BF16), 'a_core': pltpu.VMEM((PARTS, half, attn_cols), BF16),
-            'a_sum': pltpu.VMEM((PARTS, half, attn_cols), BF16), 'a_across': pltpu.VMEM((PARTS, shard, attn_cols), BF16),
-            'a_full': pltpu.VMEM((PARTS, shard, attn_cols), BF16), 'a_yz': pltpu.VMEM((PARTS, seqs, attn_cols), BF16),
+            'a_sum': pltpu.VMEM((PARTS, half, attn_cols), BF16), 'a_got': pltpu.VMEM((PARTS, 3, seqs, attn_cols), BF16),
+            'a_full': pltpu.VMEM((PARTS, 2, seqs, attn_cols), BF16),
             'u2': pltpu.VMEM((PARTS, 2 * lanes, 2 * depth), BF16), 'z_part': pltpu.VMEM((PARTS, CHUNKS, 2 * lanes, cols), BF16),
             'z_recv': pltpu.VMEM((PARTS, CHUNKS, lanes, cols), BF16), 'z_x': pltpu.VMEM((units, half, cols), BF16),
             'z_mine': pltpu.VMEM((units, half, cols), BF16), 'z_early': pltpu.VMEM((EARLY, half, cols), BF16),
@@ -627,17 +645,17 @@
             middle_kernel(names, model_dim, *refs)
 
         qkv, zsend, zmine, h_block = call(
-            start, 'start', 0, {**common, **front_scratch, 'h_in': pltpu.VMEM((part, rows), BF16)}, (HBM,) * 4,
+            start, 'start', 0, {**semaphores(6, 35, 12), **front_scratch, 'h_in': pltpu.VMEM((part, rows), BF16)}, (HBM,) * 4,
             front_shapes, front_specs, hidden.T, norm_gain, w_attn, w_mlp)
         zgot = lax.ppermute(zsend, 'x', swap)
         k_new, v_new, o = attention(0, lengths, qkv, k_cache, v_cache, ())
         qkv, zsend, zmine, h_block = call(
-            middle, 'middle', 1, {**common, **front_scratch, **back_scratch(True)}, (HBM,) * 9,
+            middle, 'middle', 1, {**semaphores(9, 64, 38), **front_scratch, **back_scratch(True)}, (HBM,) * 9,
             front_shapes, front_specs, h_block, o, norm_gain, zmine, zgot, w_down, w_out, w_attn, w_mlp)
         zgot = lax.ppermute(zsend, 'x', swap)
         k_new, v_new, o = attention(1, lengths, qkv, k_cache, v_cache, (k_new, v_new))
         h_out = call(
-            end_kernel, 'end', 2, {**common, **back_scratch(False)}, (HBM,) * 6,
+            end_kernel, 'end', 2, {**semaphores(4, 39, 27), **back_scratch(False)}, (HBM,) * 6,
             jax.ShapeDtypeStruct((part, rows), BF16), VMEM, h_block, o, zmine, zgot, w_down, w_out)
         return h_out.T, k_new, v_new
 

time: 141 us -> 130 us (0.922)
  Pallas kernels: 135 us -> 126 us
  local copies, waits for them, and re-layouts: 3.4 us -> 1.54 us
    pallas_call x3, Pallas kernels: 86.6 us -> 77.3 us  [call(): pl.pallas_call(functools.partial(kernel, tuple(scratch)), out_shape=out_s...]
    unnamed x5 -> x1, local copies, waits for them, and re-layouts: 3.4 us -> 1.54 us
  transfers between devices with their start and end apart: 2 -> 2, of which waited for: 0 -> 0; matrix products, arithmetic and copies ran while one was open for 0% -> 0% of each run, Pallas kernels for 35% -> 37%
where the time goes in v3:
time: 130 us; the launch traced here: 129 us
  Pallas kernels  126 us (97%)
  starting transfers between devices  1.62 us (1%)
  local copies, waits for them, and re-layouts  1.54 us (1%)
    pallas_call x3, Pallas kernels, call(): pl.pallas_call(functools.partial(kernel, tuple(scratch)), out_shape=out_s...  77.3 us
    pallas_call x2, Pallas kernels, attention(): pl.pallas_call(functools.partial(attention_kernel, layer, 2), out_shape=(...  48.4 us
  transfers between devices with their start and end apart: 2, of which 0 were waited for; matrix products, arithmetic and copies ran while one was open for 0% of the time, Pallas kernels for 37%

profile of v3, /device:TPU:0, one launch (start us, length us, event | category | flops | bytes accessed | tf_op | source)
XLA Modules:
  0.0 129.5 jit_solution(3069684864624964263)
XLA Ops:
  0.6 19.3 %start.1 = (bf16[2,32,1024]{2,1,0:T(8,128)(2,1)}, bf16[9,64,896]{2,1,0:T(8,128)(2,1)}, bf16[10,64,896]{2,1,0:T(8,128)(2,1)}, bf16[2,384,128]{2,1,0:T(8,128)(2,1)}) custom-call(bf16[192,256]{1,0:T(8,128)(2,1)} %bitcast.3, bf16[2,384]{1,0:T(2,128)(2,1)} %refs_2_.3, bf16[2,384,1024]{2,1,0:T(8,128)(2,1)} %refs_7_.1, bf16[2,384,2,4480]{3,2,1,0:T(2,128)(2,1)} %refs_8_.1), custom_call_target="tpu_custom_call" | custom-call | tf_op jit(solution)/shard_map/start/pallas_call | solution.py:635
  20.0 0.8 collective-permute-start
  20.8 24.2 %attention_0.1 = (bf16[2,32,2,1024,128]{4,3,2,1,0:T(8,128)(2,1)}, bf16[2,32,2,1024,128]{4,3,2,1,0:T(8,128)(2,1)}, bf16[2,32,768]{2,1,0:T(8,128)(2,1)}) custom-call(s32[32]{0:T(128)} %len_hbm.3, bf16[2,32,1024]{2,1,0:T(8,128)(2,1)} %get-tuple-element.18.qkv_hbm, bf16[2,32,2,1024,128]{4,3,2,1,0:T(8,128)(2,1)} %k_hbm.3, bf16[2,32,2,1024,128]{4,3,2,1,0:T(8,128)(2,1)} %v_hbm.3), custom_call_target="tpu_custom_call" | custom-call | flops 10000000000 | bytes 67108864 | tf_op jit(solution)/shard_map/attention_0/pallas_call | solution.py:560
  45.0 0.0 collective-permute-done.refs_4_
  45.0 34.5 %middle.1 = (bf16[2,32,1024]{2,1,0:T(8,128)(2,1)}, bf16[9,64,896]{2,1,0:T(8,128)(2,1)}, bf16[10,64,896]{2,1,0:T(8,128)(2,1)}, bf16[2,384,128]{2,1,0:T(8,128)(2,1)}) custom-call(bf16[2,384,128]{2,1,0:T(8,128)(2,1)} %get-tuple-element.17.refs_0_, bf16[2,32,768]{2,1,0:T(8,128)(2,1)} %get-tuple-element.19.refs_1_, bf16[2,384]{1,0:T(2,128)(2,1)} %refs_2_.3, ...), custom_call_target="tpu_custom_call" | custom-call | tf_op jit(solution)/shard_map/middle/pallas_call | solution.py:635
  79.5 0.8 collective-permute-start.1
  80.3 24.2 %attention_1.1 = (bf16[2,32,2,1024,128]{4,3,2,1,0:T(8,128)(2,1)}, bf16[2,32,2,1024,128]{4,3,2,1,0:T(8,128)(2,1)}, bf16[2,32,768]{2,1,0:T(8,128)(2,1)}) custom-call(s32[32]{0:T(128)} %len_hbm.3, bf16[2,32,1024]{2,1,0:T(8,128)(2,1)} %get-tuple-element.23.qkv_hbm, bf16[2,32,2,1024,128]{4,3,2,1,0:T(8,128)(2,1)} %k_hbm.3, ...), custom_call_target="tpu_custom_call", output_to_operand_aliasing={{0}: (4, {}), {1}: (5, {})} | custom-call | flops 10000000000 | bytes 67108864 | tf_op jit(solution)/shard_map/attention_1/pallas_call | solution.py:560
  104.5 0.0 collective-permute-done.1.zgot_hbm
  104.5 23.5 %end.1 = bf16[192,256]{1,0:T(8,128)(2,1)} custom-call(bf16[2,384,128]{2,1,0:T(8,128)(2,1)} %get-tuple-element.22.h_hbm, bf16[2,32,768]{2,1,0:T(8,128)(2,1)} %get-tuple-element.26.o_hbm, bf16[10,64,896]{2,1,0:T(8,128)(2,1)} %get-tuple-element.27.zmine_hbm, bf16[9,64,896]{2,1,0:T(8,128)(2,1)} %collective-permute-done.1.zgot_hbm, bf16[2,4480,384]{2,1,0:T(8,128)(2,1)} %wd_hbm.1, ...), custom_call_target="tpu_custom_call" | custom-call | tf_op jit(solution)/shard_map/end/pallas_call | solution.py:635
  127.9 1.5 %copy.17 = bf16[256,192]{0,1:T(8,128)(2,1)} copy(bf16[256,192]{0,1:T(8,128)(2,1)} %bitcast.2) | data formatting | bytes 196608
Async XLA Ops:
  20.0 25.0 %collective-permute-start = (bf16[9,64,896]{2,1,0:T(8,128)(2,1)}, bf16[9,64,896]{2,1,0:T(8,128)(2,1)}, u32[]{:S(2)}, u32[]{:S(2)}) collective-permute-start(bf16[9,64,896]{2,1,0:T(8,128)(2,1)} %get-tuple-element.21), channel_id=1, source_target_pairs={{0,2},{2,0},{1,3},{3,1},{4,6},{6,4},{5,7},{7,5}} | collective-permute-start | bytes 3096584 | tf_op jit(solution)/shard_map/ppermute | solution.py:650
  79.5 25.0 %collective-permute-start.1 = (bf16[9,64,896]{2,1,0:T(8,128)(2,1)}, bf16[9,64,896]{2,1,0:T(8,128)(2,1)}, u32[]{:S(2)}, u32[]{:S(2)}) collective-permute-start(bf16[9,64,896]{2,1,0:T(8,128)(2,1)} %get-tuple-element.28), channel_id=1, source_target_pairs={{0,2},{2,0},{1,3},{3,1},{4,6},{6,4},{5,7},{7,5}} | collective-permute-start | bytes 3096584 | tf_op jit(solution)/shard_map/ppermute | solution.py:655

commit v4 on v3

--- a/solution.py
+++ b/solution.py
@@ -15,6 +15,7 @@
 CHUNKS = 5
 EARLY = 1
 LAG = 2
+END_VMEM_LIMIT = 56393728
 VMEM_LIMIT = 67043328
 
 
@@ -23,7 +24,7 @@
 
 
 class Links:
-    def __init__(self, send_sems, recv_sems, local_sems, everyone):
+    def __init__(self, send_sems, recv_sems, local_sems, peers):
         self.send_sems, self.recv_sems, self.local_sems = send_sems, recv_sems, local_sems
         self.groups, self.used, self.local_groups, self.local_used = {}, 0, {}, 0
         x, y = lax.axis_index('x'), lax.axis_index('yz')
@@ -33,7 +34,7 @@
         self.blocks = self.along_x + (x,)
         self.targets = tuple({'x': p, 'yz': y} for p in self.blocks) + ({'x': x, 'yz': 1 - y},) + tuple(
             {'x': p, 'yz': 1 - y} for p in self.along_x)
-        self.peers = [k for k in range(8) if k != OWN] if everyone else [DIAG, PARTNER, ACROSS, YZ, ACROSS_YZ]
+        self.peers = peers
         self.barrier = pltpu.get_barrier_semaphore()
         for k in self.peers:
             pl.semaphore_signal(self.barrier, inc=1, device_id=self.targets[k], device_id_type=MESH)
@@ -71,6 +72,7 @@
 
 
 DIAG, PARTNER, ACROSS, OWN, YZ, ACROSS_YZ = 0, 1, 2, 3, 4, 7
+EVERYONE = [k for k in range(8) if k != OWN]
 PARTS = 2
 
 
@@ -95,11 +97,15 @@
     def __init__(self, links, layer, gain_hbm, wa_hbm, wm_hbm, model_dim, outs, s):
         self.links, self.s, self.layer, self.model_dim = links, s, layer, model_dim
         self.gain_copy = links.copy(gain_hbm, s['gain_in'])
-        self.qkv_out, self.zsend_out, self.zmine_out = outs
-        self.chunks, self.depth, _, self.cols = s['wm'].shape
+        self.qkv_out, self.zsend_out, self.zmine_out, self.h_out = outs
+        self.chunks, self.cols = s['z_recv'].shape[1], s['z_recv'].shape[3]
+        self.depth = s['wa'].shape[0]
         self.wa = links.copy(wa_hbm.at[layer], s['wa'])
-        self.wm = [links.copy(wm_hbm.at[layer, :, :, pl.ds(j * self.cols, self.cols)], s['wm'].at[j]) for j in range(self.chunks)]
-        self.wa_ready, self.wm_ready = False, [False] * self.chunks
+        self.wm = links.copy(wm_hbm.at[layer], s['wm'])
+        self.wa_ready, self.wm_ready = False, False
+        part = self.depth // 2
+        self.mine = pl.ds(pl.multiple_of(links.y * part, part), part)
+        self.h_yz = {}
         self.a_core, self.a_got, self.z_core, self.early = {}, {}, {}, {}
         self.sq = {}
 
@@ -110,18 +116,26 @@
         self.s['gain'][...] = gain
         self.s['even'][...], self.s['odd'][...] = spread_matrices(self.depth)
 
-    def send_squares(self, p, h_t, to):
-        s = self.s
+    def squares(self, p, h_t):
+        s = self.s
+        s['h'][p, self.mine, :] = h_t.astype(BF16)
         s['sq_send'][p] = jnp.broadcast_to(jnp.sum(h_t * h_t, axis=0, keepdims=True), s['sq_send'].shape[1:])
-        self.sq[p] = [self.links.push(s['sq_send'].at[p], s['sq_recv'].at[p, k], k, 'sq') for k in to]
-
-    def normalize(self, p, h_t, to):
+
+    def send_h(self, p):
+        s, links = self.s, self.links
+        self.sq[p] = [links.push(s['sq_send'].at[p], s['sq_recv'].at[p, k], k, 'sq') for k in EVERYONE]
+        self.h_yz[p] = links.push(s['h'].at[p, self.mine], s['h'].at[p, self.mine], YZ, 'h')
+        links.copy(s['h'].at[p, self.mine], self.h_out.at[p], 'h')
+
+    def normalize(self, p):
         s, links = self.s, self.links
         for c in self.sq[p]:
             c.wait_recv()
         total = s['sq_send'][p]
-        for k in sorted(to):
+        for k in EVERYONE:
             total = total + s['sq_recv'][p, k]
+        self.h_yz[p].wait_recv()
+        h_t = s['h'][p].astype(F32)
         inv_rms = lax.rsqrt(total[:1] / self.model_dim + NORM_EPS)
         s['u'][p] = (h_t * inv_rms * s['gain'][...]).T.astype(BF16)
         shard = s['u'].shape[1] // 4
@@ -168,10 +182,11 @@
 
     def project(self, p, j):
         s = self.s
-        if not self.wm_ready[j]:
-            self.wm[j].wait()
-            self.wm_ready[j] = True
-        s['z_part'][p, j] = dot(s['u2'][p], s['wm'][j].reshape(2 * self.depth, self.cols)).astype(BF16)
+        if not self.wm_ready:
+            self.wm.wait()
+            self.wm_ready = True
+        w = s['wm'][:, :, j * self.cols:(j + 1) * self.cols].reshape(2 * self.depth, self.cols)
+        s['z_part'][p, j] = dot(s['u2'][p], w).astype(BF16)
         half = s['z_recv'].shape[2]
         self.z_core[p, j] = self.links.push(s['z_part'].at[p, j, pl.ds(0, half)], s['z_recv'].at[p, j], PARTNER, 'z')
 
@@ -198,33 +213,38 @@
 
     def sizes(self):
         s = self.s
-        return ({'a_core': s['a_core'], 'a_got': s['a_got'], 'z': s['z_recv'], 'early': s['z_early']},
-                {'z_x': s['z_x'].at[pl.ds(EARLY, s['z_x'].shape[0] - EARLY)], 'z_mine': s['z_mine'], 'qkv': s['a_full'], 'h': s['h']})
+        return ({'a_core': s['a_core'], 'a_got': s['a_got'], 'z': s['z_recv'], 'early': s['z_early'],
+                 'sq': s['sq_recv'].at[:, pl.ds(0, len(EVERYONE))], 'h': s['h'].at[:, self.mine]},
+                {'z_x': s['z_x'].at[pl.ds(EARLY, s['z_x'].shape[0] - EARLY)], 'z_mine': s['z_mine'], 'qkv': s['a_full'], 'h': s['h'].at[:, self.mine]})
 
 
 class Back:
-    def __init__(self, links, layer, h_hbm, o_hbm, zgot_hbm, zmine_hbm, wd_hbm, wo_hbm, whole, s):
-        self.links, self.s, self.whole = links, s, whole
-        self.chunks, cols, _ = s['wd'].shape
+    def __init__(self, links, layer, h_hbm, o_hbm, zgot_hbm, zmine_hbm, wd_hbm, wo_hbm, s):
+        self.links, self.s = links, s
+        self.chunks, self.cols = s['m'].shape[1], s['m'].shape[3]
+        units = PARTS * self.chunks
         self.z = []
-        for unit in range(PARTS * self.chunks):
-            self.z.append([links.copy(zmine_hbm.at[unit], s['z_in'].at[unit])])
-            if unit >= EARLY:
-                self.z[-1].append(links.copy(zgot_hbm.at[unit - EARLY], s['z_got'].at[unit - EARLY]))
-            if unit == 0:
+        for first, last in ((0, 1), (1, self.chunks), (self.chunks, units)):
+            run = pl.ds(first, last - first)
+            self.z.append((first, links.copy(zmine_hbm.at[run], s['z_in'].at[run])))
+            start = max(first, EARLY)
+            if start < last:
+                run = pl.ds(start - EARLY, last - start)
+                self.z.append((start, links.copy(zgot_hbm.at[run], s['z_got'].at[run])))
+            if first == 0:
                 self.o_copy = links.copy(o_hbm, s['o_in'])
                 self.h_copy = links.copy(h_hbm, s['h_in'])
-        self.wd = [links.copy(wd_hbm.at[layer, pl.ds(j * cols, cols)], s['wd'].at[j]) for j in range(self.chunks)]
+        self.wd = links.copy(wd_hbm.at[layer], s['wd'])
         self.wo = links.copy(wo_hbm.at[layer], s['wo'])
-        self.wo_ready, self.wd_ready = False, [False] * self.chunks
+        self.wo_ready, self.wd_ready = False, False
         self.across, self.partner, self.diag = {}, {}, {}
         self.o_across, self.o_partner, self.o_diag = {}, {}, {}
         self.up = {}
 
     def mix(self, p, j):
         s, unit = self.s, p * self.chunks + j
-        for c in self.z[unit]:
-            c.wait()
+        while self.z and self.z[0][0] <= unit:
+            self.z.pop(0)[1].wait()
         z = s['z_in'][unit].astype(F32)
         if unit >= EARLY:
             z = (z + s['z_got'][unit - EARLY].astype(F32)).astype(BF16).astype(F32)
@@ -238,7 +258,11 @@
 
     def send(self, p, j):
         self.across[p, j] = self.links.push(self.block(p, j, OWN), self.block(p, j, ACROSS), ACROSS, 'm')
-        self.partner[p, j] = self.links.push(self.block(p, j, OWN), self.block(p, j, PARTNER), PARTNER, 'm')
+
+    def send_partner(self, p):
+        m = self.s['m']
+        shard = m.shape[2] // 4
+        self.partner[p] = self.links.push(m.at[p, :, pl.ds(OWN * shard, shard)], m.at[p, :, pl.ds(PARTNER * shard, shard)], PARTNER, 'm')
 
     def forward(self, p, j):
         self.across[p, j].wait_recv()
@@ -279,12 +303,13 @@
 
     def down(self, p, j):
         s = self.s
-        self.partner[p, j].wait_recv()
+        if j == 0:
+            self.partner[p].wait_recv()
         self.diag[p, j].wait_recv()
-        if not self.wd_ready[j]:
-            self.wd[j].wait()
-            self.wd_ready[j] = True
-        part = dot(s['m'][p, j], s['wd'][j])
+        if not self.wd_ready:
+            self.wd.wait()
+            self.wd_ready = True
+        part = dot(s['m'][p, j], s['wd'][j * self.cols:(j + 1) * self.cols])
         if j == 0:
             s['acc'][p] = part
         else:
@@ -296,22 +321,16 @@
         for k in range(4):
             s['update'][p, pl.ds(pl.multiple_of(links.blocks[k] * shard, shard), shard), :] = s['acc'][p, k * shard:(k + 1) * shard, :]
         s['up_part'][p] = s['update'][p].T.astype(BF16)
-        if self.whole:
-            src = s['up_part'].at[p]
-        else:
-            part = s['up_recv'].shape[1]
-            src = s['up_part'].at[p, pl.ds(pl.multiple_of((1 - links.y) * part, part), part)]
+        part = s['up_recv'].shape[1]
+        src = s['up_part'].at[p, pl.ds(pl.multiple_of((1 - links.y) * part, part), part)]
         self.up[p] = links.push(src, s['up_recv'].at[p], YZ, 'up')
 
-    def update(self, p):
+    def new_h(self, p):
         s, links = self.s, self.links
         self.up[p].wait_recv()
-        if self.whole:
-            own = s['up_part'][p]
-        else:
-            part = s['up_recv'].shape[1]
-            own = s['up_part'][p, pl.ds(pl.multiple_of(links.y * part, part), part), :]
-        return own.astype(F32) + s['up_recv'][p].astype(F32)
+        part = s['up_recv'].shape[1]
+        own = s['up_part'][p, pl.ds(pl.multiple_of(links.y * part, part), part), :]
+        return (s['h_in'][p].astype(F32) + (own.astype(F32) + s['up_recv'][p].astype(F32))).astype(BF16)
 
     def sizes(self):
         s = self.s
@@ -322,50 +341,45 @@
         links, chunks = self.links, self.chunks
         self.mix(0, 0)
         links.meet()
+        self.send(0, 0)
         self.send_o_yz()
-        self.send(0, 0)
         for j in range(1, chunks):
             self.mix(0, j)
             self.send(0, j)
             if j == 2:
                 self.send_o()
-        if chunks < 3:
-            self.send_o()
+        self.send_partner(0)
         for j in range(chunks):
             self.mix(1, j)
             self.send(1, j)
+        self.send_partner(1)
+        self.h_copy.wait()
 
 
 def start_kernel(names, model_dim, h_hbm, gain_hbm, wa_hbm, wm_hbm, qkv_out, zsend_out, zmine_out, h_out, *scratch):
     s = dict(zip(names, scratch))
-    links = Links(s['send'], s['recv'], s['local'], True)
+    links = Links(s['send'], s['recv'], s['local'], EVERYONE)
     h_copy = links.copy(h_hbm, s['h_in'])
-    f = Front(links, 0, gain_hbm, wa_hbm, wm_hbm, model_dim, (qkv_out, zsend_out, zmine_out), s)
-    part, rows = h_hbm.shape
+    f = Front(links, 0, gain_hbm, wa_hbm, wm_hbm, model_dim, (qkv_out, zsend_out, zmine_out, h_out), s)
+    rows = h_hbm.shape[1]
     lanes = rows // PARTS
-    mine = pl.ds(pl.multiple_of(links.y * part, part), part)
     order = part_order(rows, False)
     h_copy.wait()
     own = dot(s['h_in'][...], order)
     for p in range(PARTS):
-        s['h'][p, mine, :] = own[:, p * lanes:(p + 1) * lanes].astype(BF16)
+        f.squares(p, own[:, p * lanes:(p + 1) * lanes])
+    f.constants()
     links.meet()
-    h_yz = [links.push(s['h'].at[p, mine], s['h'].at[p, mine], YZ, 'h') for p in range(PARTS)]
-    to = [k for k in range(8) if k != OWN]
     for p in range(PARTS):
-        f.send_squares(p, own[:, p * lanes:(p + 1) * lanes], to)
-    f.constants()
+        f.send_h(p)
     for p in range(PARTS):
-        h_yz[p].wait_recv()
-        links.copy(s['h'].at[p], h_out.at[p], 'h')
-        f.normalize(p, s['h'][p].astype(F32), to)
+        f.normalize(p)
     f.spread(0)
     f.attend_core(0)
     f.spread(1)
     f.attend_core(1)
     finish_front(f, 0, {6: 0, 8: 1})
-    sent, stored = f.sizes()
-    links.drain({**sent, 'sq': s['sq_recv'].at[:, pl.ds(0, len(to))], 'h': s['h'].at[:, mine]}, stored)
+    links.drain(*f.sizes())
 
 
 def finish_front(f, begun, exchanges):
@@ -384,40 +398,37 @@
 def middle_kernel(names, model_dim, h_hbm, o_hbm, gain_hbm, zmine_hbm, zgot_hbm, wd_hbm, wo_hbm, wa_hbm, wm_hbm, qkv_out, zsend_out,
                   zmine_out, h_out, *scratch):
     s = dict(zip(names, scratch))
-    links = Links(s['send'], s['recv'], s['local'], False)
-    b = Back(links, 0, h_hbm, o_hbm, zgot_hbm, zmine_hbm, wd_hbm, wo_hbm, True, s)
-    f = Front(links, 1, gain_hbm, wa_hbm, wm_hbm, model_dim, (qkv_out, zsend_out, zmine_out), s)
-    to = (DIAG, PARTNER, ACROSS)
+    links = Links(s['send'], s['recv'], s['local'], EVERYONE)
+    b = Back(links, 0, h_hbm, o_hbm, zgot_hbm, zmine_hbm, wd_hbm, wo_hbm, s)
+    f = Front(links, 1, gain_hbm, wa_hbm, wm_hbm, model_dim, (qkv_out, zsend_out, zmine_out, h_out), s)
     b.open()
     f.constants()
-    b.h_copy.wait()
-
-    def new_h(p):
-        h = (s['h_in'][p].astype(F32) + b.update(p)).astype(BF16)
-        s['h'][p] = h
-        links.copy(s['h'].at[p], h_out.at[p], 'h')
-        f.send_squares(p, h.astype(F32), to)
+
+    def pass_h(p):
+        f.squares(p, b.new_h(p).astype(F32))
+        f.send_h(p)
 
     first_part(b)
-    second_part(b, lambda: new_h(0), lambda: f.normalize(0, s['h'][0].astype(F32), to))
+    second_part(b, lambda: pass_h(0))
+    f.normalize(0)
+    pass_h(1)
     f.spread(0)
     f.attend_core(0)
     f.project(0, 0)
-    new_h(1)
     f.project(0, 1)
     f.project(0, 2)
     f.combine(0, 0)
     f.project(0, 3)
     f.combine(0, 1)
-    f.normalize(1, s['h'][1].astype(F32), to)
-    f.spread(1)
+    f.normalize(1)
     f.project(0, 4)
-    f.attend_core(1)
     f.attend_ends(0)
     f.combine(0, 2)
+    f.spread(1)
+    f.attend_core(1)
     finish_front(f, 5, {9: 1})
     sent, stored = f.sizes()
-    links.drain({**sent, **b.sizes(), 'sq': s['sq_recv'].at[:, pl.ds(0, len(to))]}, stored)
+    links.drain({**sent, **b.sizes()}, stored)
 
 
 def first_part(b):
@@ -434,7 +445,7 @@
     b.forward(1, 0)
 
 
-def second_part(b, when_updated, when_squared):
+def second_part(b, when_updated):
     for j in range(1, b.chunks):
         b.forward(1, j)
         b.down(1, j - 1)
@@ -444,27 +455,19 @@
             when_updated()
     b.down(1, b.chunks - 1)
     b.send_update(1)
-    when_squared()
 
 
 def end_kernel(names, h_hbm, o_hbm, zmine_hbm, zgot_hbm, wd_hbm, wo_hbm, h_out, *scratch):
     s = dict(zip(names, scratch))
-    links = Links(s['send'], s['recv'], s['local'], False)
-    b = Back(links, 1, h_hbm, o_hbm, zgot_hbm, zmine_hbm, wd_hbm, wo_hbm, False, s)
-    part, rows = h_out.shape
-    own_rows = pl.ds(pl.multiple_of(links.y * part, part), part)
+    links = Links(s['send'], s['recv'], s['local'], [PARTNER, ACROSS, YZ])
+    b = Back(links, 1, h_hbm, o_hbm, zgot_hbm, zmine_hbm, wd_hbm, wo_hbm, s)
     b.open()
-    b.h_copy.wait()
-
-    def new_h(p):
-        return (s['h_in'][p, own_rows, :].astype(F32) + b.update(p)).astype(BF16)
-
     first_part(b)
-    kept = []
-    second_part(b, lambda: kept.append(new_h(0)), lambda: None)
-    order = part_order(rows, True)
-    h_new = jnp.concatenate(kept + [new_h(1)], axis=1)
-    h_out[...] = dot(h_new, order).astype(BF16)
+    h_new = []
+    second_part(b, lambda: h_new.append(b.new_h(0)))
+    order = part_order(h_out.shape[1], True)
+    h_new.append(b.new_h(1))
+    h_out[...] = dot(jnp.concatenate(h_new, axis=1), order).astype(BF16)
     links.drain(b.sizes(), {})
 
 
@@ -605,7 +608,7 @@
             'h': pltpu.VMEM((PARTS, depth, lanes), BF16), 'gain_in': pltpu.VMEM(norm_gain.shape, BF16), 'gain': pltpu.VMEM((depth, lanes), F32),
             'even': pltpu.VMEM((depth, 2 * depth), BF16), 'odd': pltpu.VMEM((depth, 2 * depth), BF16),
             'u': pltpu.VMEM((PARTS, lanes, depth), BF16), 'u_rel': pltpu.VMEM((PARTS, lanes, depth), BF16),
-            'wa': pltpu.VMEM((depth, attn_cols), BF16), 'wm': pltpu.VMEM((CHUNKS, depth, 2, cols), BF16),
+            'wa': pltpu.VMEM((depth, attn_cols), BF16), 'wm': pltpu.VMEM((depth, 2, mlp_cols), BF16),
             'a_part': pltpu.VMEM((PARTS, lanes, attn_cols), BF16), 'a_core': pltpu.VMEM((PARTS, half, attn_cols), BF16),
             'a_sum': pltpu.VMEM((PARTS, half, attn_cols), BF16), 'a_got': pltpu.VMEM((PARTS, 3, seqs, attn_cols), BF16),
             'a_full': pltpu.VMEM((PARTS, 2, seqs, attn_cols), BF16),
@@ -614,28 +617,26 @@
             'z_mine': pltpu.VMEM((units, half, cols), BF16), 'z_early': pltpu.VMEM((EARLY, half, cols), BF16),
         }
 
-        def back_scratch(whole):
-            return {
-                'o_yz': pltpu.VMEM((num_seqs, out_depth), BF16), 'o': pltpu.VMEM((PARTS, lanes, out_depth), BF16),
-                'm': pltpu.VMEM((PARTS, CHUNKS, lanes, cols), BF16), 'z_in': pltpu.VMEM((units, half, cols), BF16),
-                'z_got': pltpu.VMEM((units - EARLY, half, cols), BF16), 'o_in': pltpu.VMEM((2, num_seqs, out_depth), BF16),
-                'h_in': pltpu.VMEM((PARTS, depth, lanes), BF16),
-                'wd': pltpu.VMEM((CHUNKS, cols, depth), BF16), 'wo': pltpu.VMEM((out_depth, depth), BF16),
-                'acc': pltpu.VMEM((PARTS, lanes, depth), F32), 'update': pltpu.VMEM((PARTS, lanes, depth), F32),
-                'up_part': pltpu.VMEM((PARTS, depth, lanes), BF16),
-                'up_recv': pltpu.VMEM((PARTS, depth if whole else part, lanes), BF16),
-            }
+        back_scratch = {
+            'o_yz': pltpu.VMEM((num_seqs, out_depth), BF16), 'o': pltpu.VMEM((PARTS, lanes, out_depth), BF16),
+            'm': pltpu.VMEM((PARTS, CHUNKS, lanes, cols), BF16), 'z_in': pltpu.VMEM((units, half, cols), BF16),
+            'z_got': pltpu.VMEM((units - EARLY, half, cols), BF16), 'o_in': pltpu.VMEM((2, num_seqs, out_depth), BF16),
+            'h_in': pltpu.VMEM((PARTS, part, lanes), BF16),
+            'wd': pltpu.VMEM((mlp_cols, depth), BF16), 'wo': pltpu.VMEM((out_depth, depth), BF16),
+            'acc': pltpu.VMEM((PARTS, lanes, depth), F32), 'update': pltpu.VMEM((PARTS, lanes, depth), F32),
+            'up_part': pltpu.VMEM((PARTS, depth, lanes), BF16), 'up_recv': pltpu.VMEM((PARTS, part, lanes), BF16),
+        }
 
         front_shapes = (
             jax.ShapeDtypeStruct((2, num_seqs, attn_cols), BF16), jax.ShapeDtypeStruct((units - EARLY, half, cols), BF16),
-            jax.ShapeDtypeStruct((units, half, cols), BF16), jax.ShapeDtypeStruct((PARTS, depth, lanes), BF16))
+            jax.ShapeDtypeStruct((units, half, cols), BF16), jax.ShapeDtypeStruct((PARTS, part, lanes), BF16))
         front_specs = (HBM,) * 4
 
         def call(kernel, name, collective_id, scratch, in_specs, out_shape, out_specs, *args):
             return pl.pallas_call(
                 functools.partial(kernel, tuple(scratch)), out_shape=out_shape, in_specs=list(in_specs), out_specs=out_specs,
                 scratch_shapes=list(scratch.values()), name=name,
-                compiler_params=pltpu.CompilerParams(collective_id=collective_id, has_side_effects=True, vmem_limit_bytes=VMEM_LIMIT),
+                compiler_params=pltpu.CompilerParams(collective_id=collective_id, has_side_effects=True, vmem_limit_bytes=END_VMEM_LIMIT if kernel is end_kernel else VMEM_LIMIT),
             )(*args)
 
         def start(names, *refs):
@@ -645,17 +646,17 @@
             middle_kernel(names, model_dim, *refs)
 
         qkv, zsend, zmine, h_block = call(
-            start, 'start', 0, {**semaphores(6, 35, 12), **front_scratch, 'h_in': pltpu.VMEM((part, rows), BF16)}, (HBM,) * 4,
+            start, 'start', 0, {**semaphores(6, 35, 8), **front_scratch, 'h_in': pltpu.VMEM((part, rows), BF16)}, (HBM,) * 4,
             front_shapes, front_specs, hidden.T, norm_gain, w_attn, w_mlp)
         zgot = lax.ppermute(zsend, 'x', swap)
         k_new, v_new, o = attention(0, lengths, qkv, k_cache, v_cache, ())
         qkv, zsend, zmine, h_block = call(
-            middle, 'middle', 1, {**semaphores(9, 64, 38), **front_scratch, **back_scratch(True)}, (HBM,) * 9,
+            middle, 'middle', 1, {**semaphores(10, 66, 16), **front_scratch, **back_scratch}, (HBM,) * 9,
             front_shapes, front_specs, h_block, o, norm_gain, zmine, zgot, w_down, w_out, w_attn, w_mlp)
         zgot = lax.ppermute(zsend, 'x', swap)
         k_new, v_new, o = attention(1, lengths, qkv, k_cache, v_cache, (k_new, v_new))
         h_out = call(
-            end_kernel, 'end', 2, {**semaphores(4, 39, 27), **back_scratch(False)}, (HBM,) * 6,
+            end_kernel, 'end', 2, {**semaphores(4, 31, 9), **back_scratch}, (HBM,) * 6,
             jax.ShapeDtypeStruct((part, rows), BF16), VMEM, h_block, o, zmine, zgot, w_down, w_out)
         return h_out.T, k_new, v_new
 

time: 130 us -> 128 us (0.985)
  Pallas kernels: 126 us -> 124 us
    pallas_call x3, Pallas kernels: 77.3 us -> 75.2 us  [call(): pl.pallas_call(functools.partial(kernel, tuple(scratch)), out_shape=out_s...]
  transfers between devices with their start and end apart: 2 -> 2, of which waited for: 0 -> 0; matrix products, arithmetic and copies ran while one was open for 0% -> 0% of each run, Pallas kernels for 37% -> 38%
where the time goes in v4:
time: 128 us; the launch traced here: 127 us
  Pallas kernels  124 us (97%)
  starting transfers between devices  2.51 us (2%)
    pallas_call x3, Pallas kernels, call(): pl.pallas_call(functools.partial(kernel, tuple(scratch)), out_shape=out_s...  75.2 us
    pallas_call x2, Pallas kernels, attention(): pl.pallas_call(functools.partial(attention_kernel, layer, 2), out_shape=(...  48.4 us
  transfers between devices with their start and end apart: 2, of which 0 were waited for; matrix products, arithmetic and copies ran while one was open for 0% of the time, Pallas kernels for 38%

profile of v4, /device:TPU:0, one launch (start us, length us, event | category | flops | bytes accessed | tf_op | source)
XLA Modules:
  0.0 127.4 jit_solution(4644633103843920481)
XLA Ops:
  0.6 19.1 %start.1 = (bf16[2,32,1024]{2,1,0:T(8,128)(2,1)}, bf16[9,64,896]{2,1,0:T(8,128)(2,1)}, bf16[10,64,896]{2,1,0:T(8,128)(2,1)}, bf16[2,192,128]{2,1,0:T(8,128)(2,1)}) custom-call(bf16[192,256]{1,0:T(8,128)(2,1)} %bitcast.3, bf16[2,384]{1,0:T(2,128)(2,1)} %refs_2_.3, bf16[2,384,1024]{2,1,0:T(8,128)(2,1)} %refs_7_.1, bf16[2,384,2,4480]{3,2,1,0:T(2,128)(2,1)} %refs_8_.1), custom_call_target="tpu_custom_call" | custom-call | tf_op jit(solution)/shard_map/start/pallas_call | solution.py:636
  19.7 1.2 collective-permute-start
  20.9 24.2 %attention_0.1 = (bf16[2,32,2,1024,128]{4,3,2,1,0:T(8,128)(2,1)}, bf16[2,32,2,1024,128]{4,3,2,1,0:T(8,128)(2,1)}, bf16[2,32,768]{2,1,0:T(8,128)(2,1)}) custom-call(s32[32]{0:T(128)} %len_hbm.3, bf16[2,32,1024]{2,1,0:T(8,128)(2,1)} %get-tuple-element.18.qkv_hbm, bf16[2,32,2,1024,128]{4,3,2,1,0:T(8,128)(2,1)} %k_hbm.3, bf16[2,32,2,1024,128]{4,3,2,1,0:T(8,128)(2,1)} %v_hbm.3), custom_call_target="tpu_custom_call" | custom-call | flops 10000000000 | bytes 67108864 | tf_op jit(solution)/shard_map/attention_0/pallas_call | solution.py:563
  45.1 0.0 collective-permute-done.refs_4_
  45.1 34.1 %middle.1 = (bf16[2,32,1024]{2,1,0:T(8,128)(2,1)}, bf16[9,64,896]{2,1,0:T(8,128)(2,1)}, bf16[10,64,896]{2,1,0:T(8,128)(2,1)}, bf16[2,192,128]{2,1,0:T(8,128)(2,1)}) custom-call(bf16[2,192,128]{2,1,0:T(8,128)(2,1)} %get-tuple-element.17.refs_0_, bf16[2,32,768]{2,1,0:T(8,128)(2,1)} %get-tuple-element.19.refs_1_, bf16[2,384]{1,0:T(2,128)(2,1)} %refs_2_.3, ...), custom_call_target="tpu_custom_call" | custom-call | tf_op jit(solution)/shard_map/middle/pallas_call | solution.py:636
  79.3 1.3 %collective-permute-start.1 = (bf16[9,64,896]{2,1,0:T(8,128)(2,1)}, bf16[9,64,896]{2,1,0:T(8,128)(2,1)}, u32[]{:S(2)}, u32[]{:S(2)}) collective-permute-start(bf16[9,64,896]{2,1,0:T(8,128)(2,1)} %get-tuple-element.28), channel_id=1, source_target_pairs={{0,2},{2,0},{1,3},{3,1},{4,6},{6,4},{5,7},{7,5}} | collective-permute-start | bytes 3096584 | tf_op jit(solution)/shard_map/ppermute | solution.py:656
  80.6 24.2 %attention_1.1 = (bf16[2,32,2,1024,128]{4,3,2,1,0:T(8,128)(2,1)}, bf16[2,32,2,1024,128]{4,3,2,1,0:T(8,128)(2,1)}, bf16[2,32,768]{2,1,0:T(8,128)(2,1)}) custom-call(s32[32]{0:T(128)} %len_hbm.3, bf16[2,32,1024]{2,1,0:T(8,128)(2,1)} %get-tuple-element.23.qkv_hbm, bf16[2,32,2,1024,128]{4,3,2,1,0:T(8,128)(2,1)} %k_hbm.3, ...), custom_call_target="tpu_custom_call", output_to_operand_aliasing={{0}: (4, {}), {1}: (5, {})} | custom-call | flops 10000000000 | bytes 67108864 | tf_op jit(solution)/shard_map/attention_1/pallas_call | solution.py:563
  104.7 0.0 collective-permute-done.1.zgot_hbm
  104.8 22.0 %end.1 = bf16[192,256]{1,0:T(8,128)(2,1)S(1)} custom-call(bf16[2,192,128]{2,1,0:T(8,128)(2,1)} %get-tuple-element.22.h_hbm, bf16[2,32,768]{2,1,0:T(8,128)(2,1)} %get-tuple-element.26.o_hbm, bf16[10,64,896]{2,1,0:T(8,128)(2,1)} %get-tuple-element.27.zmine_hbm, bf16[9,64,896]{2,1,0:T(8,128)(2,1)} %collective-permute-done.1.zgot_hbm, ...), custom_call_target="tpu_custom_call" | custom-call | tf_op jit(solution)/shard_map/end/pallas_call | solution.py:636
  126.8 0.6 copy.17
Async XLA Ops:
  19.7 25.4 %collective-permute-start = (bf16[9,64,896]{2,1,0:T(8,128)(2,1)}, bf16[9,64,896]{2,1,0:T(8,128)(2,1)}, u32[]{:S(2)}, u32[]{:S(2)}) collective-permute-start(bf16[9,64,896]{2,1,0:T(8,128)(2,1)} %get-tuple-element.21), channel_id=1, source_target_pairs={{0,2},{2,0},{1,3},{3,1},{4,6},{6,4},{5,7},{7,5}} | collective-permute-start | bytes 3096584 | tf_op jit(solution)/shard_map/ppermute | solution.py:651
  79.3 25.5 %collective-permute-start.1 = (bf16[9,64,896]{2,1,0:T(8,128)(2,1)}, bf16[9,64,896]{2,1,0:T(8,128)(2,1)}, u32[]{:S(2)}, u32[]{:S(2)}) collective-permute-start(bf16[9,64,896]{2,1,0:T(8,128)(2,1)} %get-tuple-element.28), channel_id=1, source_target_pairs={{0,2},{2,0},{1,3},{3,1},{4,6},{6,4},{5,7},{7,5}} | collective-permute-start | bytes 3096584 | tf_op jit(solution)/shard_map/ppermute | solution.py:656

commit v5 on v4

--- a/solution.py
+++ b/solution.py
@@ -277,16 +277,16 @@
         shard = self.s['o'].shape[1] // 4
         return self.s['o'].at[p, pl.ds(k * shard, shard)]
 
-    def send_o(self):
+    def send_o(self, p):
         y, s = self.links.y, self.s
-        self.o_yz.wait_recv()
+        if p == 0:
+            self.o_yz.wait_recv()
         shard = s['o'].shape[1] // 4
         seqs = shard // 2
-        for p in range(PARTS):
-            s['o'][p, pl.ds(OWN * shard + pl.multiple_of(y * seqs, seqs), seqs), :] = s['o_in'][y, p * seqs:(p + 1) * seqs]
-            s['o'][p, pl.ds(OWN * shard + pl.multiple_of((1 - y) * seqs, seqs), seqs), :] = s['o_yz'][p * seqs:(p + 1) * seqs]
-            self.o_across[p] = self.links.push(self.o_block(p, OWN), self.o_block(p, ACROSS), ACROSS, 'o')
-            self.o_partner[p] = self.links.push(self.o_block(p, OWN), self.o_block(p, PARTNER), PARTNER, 'o')
+        s['o'][p, pl.ds(OWN * shard + pl.multiple_of(y * seqs, seqs), seqs), :] = s['o_in'][y, p * seqs:(p + 1) * seqs]
+        s['o'][p, pl.ds(OWN * shard + pl.multiple_of((1 - y) * seqs, seqs), seqs), :] = s['o_yz'][p * seqs:(p + 1) * seqs]
+        self.o_across[p] = self.links.push(self.o_block(p, OWN), self.o_block(p, ACROSS), ACROSS, 'o')
+        self.o_partner[p] = self.links.push(self.o_block(p, OWN), self.o_block(p, PARTNER), PARTNER, 'o')
 
     def forward_o(self, p):
         self.o_across[p].wait_recv()
@@ -347,11 +347,13 @@
             self.mix(0, j)
             self.send(0, j)
             if j == 2:
-                self.send_o()
+                self.send_o(0)
         self.send_partner(0)
         for j in range(chunks):
             self.mix(1, j)
             self.send(1, j)
+            if j == 1:
+                self.send_o(1)
         self.send_partner(1)
         self.h_copy.wait()
 
@@ -420,13 +422,26 @@
     f.combine(0, 0)
     f.project(0, 3)
     f.combine(0, 1)
+    f.project(0, 4)
+    f.combine(0, 2)
+    f.combine(0, 3)
     f.normalize(1)
-    f.project(0, 4)
+    f.spread(1)
+    f.project(1, 0)
+    f.attend_core(1)
+    f.combine(0, 4)
     f.attend_ends(0)
-    f.combine(0, 2)
-    f.spread(1)
-    f.attend_core(1)
-    finish_front(f, 5, {9: 1})
+    f.project(1, 1)
+    f.project(1, 2)
+    f.combine(1, 0)
+    f.project(1, 3)
+    f.combine(1, 1)
+    f.project(1, 4)
+    f.combine(1, 2)
+    f.combine(1, 3)
+    f.attend_ends(1)
+    f.combine(1, 4)
+    f.finish()
     sent, stored = f.sizes()
     links.drain({**sent, **b.sizes()}, stored)
 
@@ -436,7 +451,6 @@
         b.forward(0, j)
         if j == 2:
             b.forward_o(0)
-            b.forward_o(1)
         if j >= 1:
             b.down(0, j - 1)
     b.project_o(0)
@@ -448,10 +462,12 @@
 def second_part(b, when_updated):
     for j in range(1, b.chunks):
         b.forward(1, j)
+        if j == 1:
+            b.forward_o(1)
         b.down(1, j - 1)
-        if j == 1:
+        if j == 2:
             b.project_o(1)
-        if j == b.chunks - 2:
+        if j == b.chunks - 3:
             when_updated()
     b.down(1, b.chunks - 1)
     b.send_update(1)

time: 128 us -> 127 us (level)
  no operation moved by 1% of the time
where the time goes in v5:
time: 127 us
  Pallas kernels  123 us (97%)
  starting transfers between devices  2.52 us (2%)
    pallas_call x3, Pallas kernels, call(): pl.pallas_call(functools.partial(kernel, tuple(scratch)), out_shape=out_s...  74.5 us
    pallas_call x2, Pallas kernels, attention(): pl.pallas_call(functools.partial(attention_kernel, layer, 2), out_shape=(...  48.4 us
  transfers between devices with their start and end apart: 2, of which 0 were waited for; matrix products, arithmetic and copies ran while one was open for 0% of the time, Pallas kernels for 38%

profile of v5, /device:TPU:0, one launch (start us, length us, event | category | flops | bytes accessed | tf_op | source)
XLA Modules:
  0.0 126.7 jit_solution(5822726294200057915)
XLA Ops:
  0.6 19.1 %start.1 = (bf16[2,32,1024]{2,1,0:T(8,128)(2,1)}, bf16[9,64,896]{2,1,0:T(8,128)(2,1)}, bf16[10,64,896]{2,1,0:T(8,128)(2,1)}, bf16[2,192,128]{2,1,0:T(8,128)(2,1)}) custom-call(bf16[192,256]{1,0:T(8,128)(2,1)} %bitcast.3, bf16[2,384]{1,0:T(2,128)(2,1)} %refs_2_.3, bf16[2,384,1024]{2,1,0:T(8,128)(2,1)} %refs_7_.1, bf16[2,384,2,4480]{3,2,1,0:T(2,128)(2,1)} %refs_8_.1), custom_call_target="tpu_custom_call" | custom-call | tf_op jit(solution)/shard_map/start/pallas_call | solution.py:652
  19.7 1.2 collective-permute-start
  20.9 24.2 %attention_0.1 = (bf16[2,32,2,1024,128]{4,3,2,1,0:T(8,128)(2,1)}, bf16[2,32,2,1024,128]{4,3,2,1,0:T(8,128)(2,1)}, bf16[2,32,768]{2,1,0:T(8,128)(2,1)}) custom-call(s32[32]{0:T(128)} %len_hbm.3, bf16[2,32,1024]{2,1,0:T(8,128)(2,1)} %get-tuple-element.18.qkv_hbm, bf16[2,32,2,1024,128]{4,3,2,1,0:T(8,128)(2,1)} %k_hbm.3, bf16[2,32,2,1024,128]{4,3,2,1,0:T(8,128)(2,1)} %v_hbm.3), custom_call_target="tpu_custom_call" | custom-call | flops 10000000000 | bytes 67108864 | tf_op jit(solution)/shard_map/attention_0/pallas_call | solution.py:579
  45.1 0.0 collective-permute-done.refs_4_
  45.1 33.4 %middle.1 = (bf16[2,32,1024]{2,1,0:T(8,128)(2,1)}, bf16[9,64,896]{2,1,0:T(8,128)(2,1)}, bf16[10,64,896]{2,1,0:T(8,128)(2,1)}, bf16[2,192,128]{2,1,0:T(8,128)(2,1)}) custom-call(bf16[2,192,128]{2,1,0:T(8,128)(2,1)} %get-tuple-element.17.refs_0_, bf16[2,32,768]{2,1,0:T(8,128)(2,1)} %get-tuple-element.19.refs_1_, bf16[2,384]{1,0:T(2,128)(2,1)} %refs_2_.3, ...), custom_call_target="tpu_custom_call" | custom-call | tf_op jit(solution)/shard_map/middle/pallas_call | solution.py:652
  78.6 1.3 %collective-permute-start.1 = (bf16[9,64,896]{2,1,0:T(8,128)(2,1)}, bf16[9,64,896]{2,1,0:T(8,128)(2,1)}, u32[]{:S(2)}, u32[]{:S(2)}) collective-permute-start(bf16[9,64,896]{2,1,0:T(8,128)(2,1)} %get-tuple-element.28), channel_id=1, source_target_pairs={{0,2},{2,0},{1,3},{3,1},{4,6},{6,4},{5,7},{7,5}} | collective-permute-start | bytes 3096584 | tf_op jit(solution)/shard_map/ppermute | solution.py:672
  79.9 24.2 %attention_1.1 = (bf16[2,32,2,1024,128]{4,3,2,1,0:T(8,128)(2,1)}, bf16[2,32,2,1024,128]{4,3,2,1,0:T(8,128)(2,1)}, bf16[2,32,768]{2,1,0:T(8,128)(2,1)}) custom-call(s32[32]{0:T(128)} %len_hbm.3, bf16[2,32,1024]{2,1,0:T(8,128)(2,1)} %get-tuple-element.23.qkv_hbm, bf16[2,32,2,1024,128]{4,3,2,1,0:T(8,128)(2,1)} %k_hbm.3, ...), custom_call_target="tpu_custom_call", output_to_operand_aliasing={{0}: (4, {}), {1}: (5, {})} | custom-call | flops 10000000000 | bytes 67108864 | tf_op jit(solution)/shard_map/attention_1/pallas_call | solution.py:579
  104.0 0.0 collective-permute-done.1.zgot_hbm
  104.1 22.0 %end.1 = bf16[192,256]{1,0:T(8,128)(2,1)S(1)} custom-call(bf16[2,192,128]{2,1,0:T(8,128)(2,1)} %get-tuple-element.22.h_hbm, bf16[2,32,768]{2,1,0:T(8,128)(2,1)} %get-tuple-element.26.o_hbm, bf16[10,64,896]{2,1,0:T(8,128)(2,1)} %get-tuple-element.27.zmine_hbm, bf16[9,64,896]{2,1,0:T(8,128)(2,1)} %collective-permute-done.1.zgot_hbm, ...), custom_call_target="tpu_custom_call" | custom-call | tf_op jit(solution)/shard_map/end/pallas_call | solution.py:652
  126.1 0.6 copy.17
Async XLA Ops:
  19.7 25.4 %collective-permute-start = (bf16[9,64,896]{2,1,0:T(8,128)(2,1)}, bf16[9,64,896]{2,1,0:T(8,128)(2,1)}, u32[]{:S(2)}, u32[]{:S(2)}) collective-permute-start(bf16[9,64,896]{2,1,0:T(8,128)(2,1)} %get-tuple-element.21), channel_id=1, source_target_pairs={{0,2},{2,0},{1,3},{3,1},{4,6},{6,4},{5,7},{7,5}} | collective-permute-start | bytes 3096584 | tf_op jit(solution)/shard_map/ppermute | solution.py:667
  78.6 25.5 %collective-permute-start.1 = (bf16[9,64,896]{2,1,0:T(8,128)(2,1)}, bf16[9,64,896]{2,1,0:T(8,128)(2,1)}, u32[]{:S(2)}, u32[]{:S(2)}) collective-permute-start(bf16[9,64,896]{2,1,0:T(8,128)(2,1)} %get-tuple-element.28), channel_id=1, source_target_pairs={{0,2},{2,0},{1,3},{3,1},{4,6},{6,4},{5,7},{7,5}} | collective-permute-start | bytes 3096584 | tf_op jit(solution)/shard_map/ppermute | solution.py:672

commit v6 on v5

--- a/solution.py
+++ b/solution.py
@@ -14,7 +14,6 @@
 
 CHUNKS = 5
 EARLY = 1
-LAG = 2
 END_VMEM_LIMIT = 56393728
 VMEM_LIMIT = 67043328
 
@@ -114,7 +113,8 @@
         self.gain_copy.wait()
         gain = jnp.broadcast_to(self.s['gain_in'][self.layer:self.layer + 1, :].astype(F32), (lanes, self.depth)).T
         self.s['gain'][...] = gain
-        self.s['even'][...], self.s['odd'][...] = spread_matrices(self.depth)
+        if 'even' in self.s:
+            self.s['even'][...], self.s['odd'][...] = spread_matrices(self.depth)
 
     def squares(self, p, h_t):
         s = self.s
@@ -187,6 +187,39 @@
             self.wm_ready = True
         w = s['wm'][:, :, j * self.cols:(j + 1) * self.cols].reshape(2 * self.depth, self.cols)
         s['z_part'][p, j] = dot(s['u2'][p], w).astype(BF16)
+        self.push_core(p, j)
+
+    def split_weights(self):
+        s, run = self.s, 128
+        i = lax.broadcasted_iota(jnp.int32, (2 * run, 2 * run), 0)
+        j = lax.broadcasted_iota(jnp.int32, (2 * run, 2 * run), 1)
+        place = jnp.where(i < run, 2 * i, 2 * (i - run) + 1)
+        order = jnp.where(j == place, jnp.ones((), F32), jnp.zeros((), F32)).astype(BF16)
+        self.wm.wait()
+        for c in range(self.chunks):
+            cols = slice(c * self.cols, (c + 1) * self.cols)
+            for e in range(self.depth // run):
+                rows = slice(e * run, (e + 1) * run)
+                w = dot(order, s['wm'][rows, :, cols].reshape(2 * run, self.cols)).astype(BF16)
+                s['w_split'][0, rows, cols] = w[:run]
+                s['w_split'][1, rows, cols] = w[run:]
+
+    def project_all(self, j):
+        s = self.s
+        lanes = s['u'].shape[1]
+        shard = lanes // 4
+        u = s['u_rel'][...].reshape(PARTS * lanes, self.depth)
+        cols = slice(j * self.cols, (j + 1) * self.cols)
+        gate, up = dot(u, s['w_split'][0, :, cols]).astype(BF16), dot(u, s['w_split'][1, :, cols]).astype(BF16)
+        for p in range(PARTS):
+            for k in range(4):
+                rows = slice(p * lanes + k * shard, p * lanes + (k + 1) * shard)
+                s['z_part'][p, j, 2 * k * shard:(2 * k + 1) * shard] = gate[rows]
+                s['z_part'][p, j, (2 * k + 1) * shard:(2 * k + 2) * shard] = up[rows]
+            self.push_core(p, j)
+
+    def push_core(self, p, j):
+        s = self.s
         half = s['z_recv'].shape[2]
         self.z_core[p, j] = self.links.push(s['z_part'].at[p, j, pl.ds(0, half)], s['z_recv'].at[p, j], PARTNER, 'z')
 
@@ -374,27 +407,23 @@
     links.meet()
     for p in range(PARTS):
         f.send_h(p)
+    f.split_weights()
     for p in range(PARTS):
         f.normalize(p)
-    f.spread(0)
-    f.attend_core(0)
-    f.spread(1)
-    f.attend_core(1)
-    finish_front(f, 0, {6: 0, 8: 1})
+    f.project_all(0)
+    for p in range(PARTS):
+        f.attend_core(p)
+    for j in range(1, f.chunks):
+        f.project_all(j)
+        if j == f.chunks - 1:
+            f.attend_ends(0)
+        for p in range(PARTS):
+            f.combine(p, j - 1)
+    f.attend_ends(1)
+    for p in range(PARTS):
+        f.combine(p, f.chunks - 1)
+    f.finish()
     links.drain(*f.sizes())
-
-
-def finish_front(f, begun, exchanges):
-    units = [(p, j) for p in range(PARTS) for j in range(f.chunks)]
-    for n in range(begun, len(units)):
-        f.project(*units[n])
-        if n >= LAG:
-            f.combine(*units[n - LAG])
-        if n in exchanges:
-            f.attend_ends(exchanges[n])
-    for n in range(len(units) - LAG, len(units)):
-        f.combine(*units[n])
-    f.finish()
 
 
 def middle_kernel(names, model_dim, h_hbm, o_hbm, gain_hbm, zmine_hbm, zgot_hbm, wd_hbm, wo_hbm, wa_hbm, wm_hbm, qkv_out, zsend_out,
@@ -622,17 +651,21 @@
         front_scratch = {
             'sq_send': pltpu.VMEM((PARTS, 8, lanes), F32), 'sq_recv': pltpu.VMEM((PARTS, 8, 8, lanes), F32),
             'h': pltpu.VMEM((PARTS, depth, lanes), BF16), 'gain_in': pltpu.VMEM(norm_gain.shape, BF16), 'gain': pltpu.VMEM((depth, lanes), F32),
-            'even': pltpu.VMEM((depth, 2 * depth), BF16), 'odd': pltpu.VMEM((depth, 2 * depth), BF16),
             'u': pltpu.VMEM((PARTS, lanes, depth), BF16), 'u_rel': pltpu.VMEM((PARTS, lanes, depth), BF16),
             'wa': pltpu.VMEM((depth, attn_cols), BF16), 'wm': pltpu.VMEM((depth, 2, mlp_cols), BF16),
             'a_part': pltpu.VMEM((PARTS, lanes, attn_cols), BF16), 'a_core': pltpu.VMEM((PARTS, half, attn_cols), BF16),
             'a_sum': pltpu.VMEM((PARTS, half, attn_cols), BF16), 'a_got': pltpu.VMEM((PARTS, 3, seqs, attn_cols), BF16),
             'a_full': pltpu.VMEM((PARTS, 2, seqs, attn_cols), BF16),
-            'u2': pltpu.VMEM((PARTS, 2 * lanes, 2 * depth), BF16), 'z_part': pltpu.VMEM((PARTS, CHUNKS, 2 * lanes, cols), BF16),
+            'z_part': pltpu.VMEM((PARTS, CHUNKS, 2 * lanes, cols), BF16),
             'z_recv': pltpu.VMEM((PARTS, CHUNKS, lanes, cols), BF16), 'z_x': pltpu.VMEM((units, half, cols), BF16),
             'z_mine': pltpu.VMEM((units, half, cols), BF16), 'z_early': pltpu.VMEM((EARLY, half, cols), BF16),
         }
 
+        split_scratch = {'w_split': pltpu.VMEM((2, depth, mlp_cols), BF16)}
+        spread_scratch = {
+            'even': pltpu.VMEM((depth, 2 * depth), BF16), 'odd': pltpu.VMEM((depth, 2 * depth), BF16),
+            'u2': pltpu.VMEM((PARTS, 2 * lanes, 2 * depth), BF16),
+        }
         back_scratch = {
             'o_yz': pltpu.VMEM((num_seqs, out_depth), BF16), 'o': pltpu.VMEM((PARTS, lanes, out_depth), BF16),
             'm': pltpu.VMEM((PARTS, CHUNKS, lanes, cols), BF16), 'z_in': pltpu.VMEM((units, half, cols), BF16),
@@ -662,12 +695,12 @@
             middle_kernel(names, model_dim, *refs)
 
         qkv, zsend, zmine, h_block = call(
-            start, 'start', 0, {**semaphores(6, 35, 8), **front_scratch, 'h_in': pltpu.VMEM((part, rows), BF16)}, (HBM,) * 4,
+            start, 'start', 0, {**semaphores(6, 35, 8), **front_scratch, **split_scratch, 'h_in': pltpu.VMEM((part, rows), BF16)}, (HBM,) * 4,
             front_shapes, front_specs, hidden.T, norm_gain, w_attn, w_mlp)
         zgot = lax.ppermute(zsend, 'x', swap)
         k_new, v_new, o = attention(0, lengths, qkv, k_cache, v_cache, ())
         qkv, zsend, zmine, h_block = call(
-            middle, 'middle', 1, {**semaphores(10, 66, 16), **front_scratch, **back_scratch}, (HBM,) * 9,
+            middle, 'middle', 1, {**semaphores(10, 66, 16), **front_scratch, **spread_scratch, **back_scratch}, (HBM,) * 9,
             front_shapes, front_specs, h_block, o, norm_gain, zmine, zgot, w_down, w_out, w_attn, w_mlp)
         zgot = lax.ppermute(zsend, 'x', swap)
         k_new, v_new, o = attention(1, lengths, qkv, k_cache, v_cache, (k_new, v_new))

time: 127 us -> 126 us (level)
  no operation moved by 1% of the time
where the time goes in v6:
time: 126 us
  Pallas kernels  122 us (97%)
  starting transfers between devices  2.11 us (2%)
    pallas_call x3, Pallas kernels, call(): pl.pallas_call(functools.partial(kernel, tuple(scratch)), out_shape=out_s...  74 us
    pallas_call x2, Pallas kernels, attention(): pl.pallas_call(functools.partial(attention_kernel, layer, 2), out_shape=(...  48.4 us
  transfers between devices with their start and end apart: 2, of which 0 were waited for; matrix products, arithmetic and copies ran while one was open for 0% of the time, Pallas kernels for 38%

profile of v6, /device:TPU:0, one launch (start us, length us, event | category | flops | bytes accessed | tf_op | source)
XLA Modules:
  0.0 125.8 jit_solution(10616197826036550625)
XLA Ops:
  0.6 18.1 %start.1 = (bf16[2,32,1024]{2,1,0:T(8,128)(2,1)}, bf16[9,64,896]{2,1,0:T(8,128)(2,1)}, bf16[10,64,896]{2,1,0:T(8,128)(2,1)}, bf16[2,192,128]{2,1,0:T(8,128)(2,1)}) custom-call(bf16[192,256]{1,0:T(8,128)(2,1)} %bitcast.3, bf16[2,384]{1,0:T(2,128)(2,1)} %refs_2_.3, bf16[2,384,1024]{2,1,0:T(8,128)(2,1)} %refs_7_.1, bf16[2,384,2,4480]{3,2,1,0:T(2,128)(2,1)} %refs_8_.1), custom_call_target="tpu_custom_call" | custom-call | tf_op jit(solution)/shard_map/start/pallas_call | solution.py:685
  18.7 1.0 collective-permute-start
  19.7 24.2 %attention_0.1 = (bf16[2,32,2,1024,128]{4,3,2,1,0:T(8,128)(2,1)}, bf16[2,32,2,1024,128]{4,3,2,1,0:T(8,128)(2,1)}, bf16[2,32,768]{2,1,0:T(8,128)(2,1)}) custom-call(s32[32]{0:T(128)} %len_hbm.3, bf16[2,32,1024]{2,1,0:T(8,128)(2,1)} %get-tuple-element.18.qkv_hbm, bf16[2,32,2,1024,128]{4,3,2,1,0:T(8,128)(2,1)} %k_hbm.3, bf16[2,32,2,1024,128]{4,3,2,1,0:T(8,128)(2,1)} %v_hbm.3), custom_call_target="tpu_custom_call" | custom-call | flops 10000000000 | bytes 67108864 | tf_op jit(solution)/shard_map/attention_0/pallas_call | solution.py:608
  43.8 0.0 collective-permute-done.refs_4_
  43.9 33.9 %middle.1 = (bf16[2,32,1024]{2,1,0:T(8,128)(2,1)}, bf16[9,64,896]{2,1,0:T(8,128)(2,1)}, bf16[10,64,896]{2,1,0:T(8,128)(2,1)}, bf16[2,192,128]{2,1,0:T(8,128)(2,1)}) custom-call(bf16[2,192,128]{2,1,0:T(8,128)(2,1)} %get-tuple-element.17.refs_0_, bf16[2,32,768]{2,1,0:T(8,128)(2,1)} %get-tuple-element.19.refs_1_, bf16[2,384]{1,0:T(2,128)(2,1)} %refs_2_.3, ...), custom_call_target="tpu_custom_call" | custom-call | tf_op jit(solution)/shard_map/middle/pallas_call | solution.py:685
  77.7 1.1 collective-permute-start.1
  78.9 24.2 %attention_1.1 = (bf16[2,32,2,1024,128]{4,3,2,1,0:T(8,128)(2,1)}, bf16[2,32,2,1024,128]{4,3,2,1,0:T(8,128)(2,1)}, bf16[2,32,768]{2,1,0:T(8,128)(2,1)}) custom-call(s32[32]{0:T(128)} %len_hbm.3, bf16[2,32,1024]{2,1,0:T(8,128)(2,1)} %get-tuple-element.23.qkv_hbm, bf16[2,32,2,1024,128]{4,3,2,1,0:T(8,128)(2,1)} %k_hbm.3, ...), custom_call_target="tpu_custom_call", output_to_operand_aliasing={{0}: (4, {}), {1}: (5, {})} | custom-call | flops 10000000000 | bytes 67108864 | tf_op jit(solution)/shard_map/attention_1/pallas_call | solution.py:608
  103.1 0.0 collective-permute-done.1.zgot_hbm
  103.1 22.1 %end.1 = bf16[192,256]{1,0:T(8,128)(2,1)S(1)} custom-call(bf16[2,192,128]{2,1,0:T(8,128)(2,1)} %get-tuple-element.22.h_hbm, bf16[2,32,768]{2,1,0:T(8,128)(2,1)} %get-tuple-element.26.o_hbm, bf16[10,64,896]{2,1,0:T(8,128)(2,1)} %get-tuple-element.27.zmine_hbm, bf16[9,64,896]{2,1,0:T(8,128)(2,1)} %collective-permute-done.1.zgot_hbm, ...), custom_call_target="tpu_custom_call" | custom-call | tf_op jit(solution)/shard_map/end/pallas_call | solution.py:685
  125.1 0.6 copy.17
Async XLA Ops:
  18.7 25.1 %collective-permute-start = (bf16[9,64,896]{2,1,0:T(8,128)(2,1)}, bf16[9,64,896]{2,1,0:T(8,128)(2,1)}, u32[]{:S(2)}, u32[]{:S(2)}) collective-permute-start(bf16[9,64,896]{2,1,0:T(8,128)(2,1)} %get-tuple-element.21), channel_id=1, source_target_pairs={{0,2},{2,0},{1,3},{3,1},{4,6},{6,4},{5,7},{7,5}} | collective-permute-start | bytes 3096584 | tf_op jit(solution)/shard_map/ppermute | solution.py:700
  77.7 25.3 %collective-permute-start.1 = (bf16[9,64,896]{2,1,0:T(8,128)(2,1)}, bf16[9,64,896]{2,1,0:T(8,128)(2,1)}, u32[]{:S(2)}, u32[]{:S(2)}) collective-permute-start(bf16[9,64,896]{2,1,0:T(8,128)(2,1)} %get-tuple-element.28), channel_id=1, source_target_pairs={{0,2},{2,0},{1,3},{3,1},{4,6},{6,4},{5,7},{7,5}} | collective-permute-start | bytes 3096584 | tf_op jit(solution)/shard_map/ppermute | solution.py:705

commit v7 on v6

--- a/solution.py
+++ b/solution.py
@@ -12,8 +12,11 @@
 BF16 = jnp.bfloat16
 F32 = jnp.float32
 
+SQ_ROWS = 1
+PER_COPY = 4
+PER_STEP = 2
 CHUNKS = 5
-EARLY = 1
+EARLY = (1, 2)
 END_VMEM_LIMIT = 56393728
 VMEM_LIMIT = 67043328
 
@@ -75,13 +78,6 @@
 PARTS = 2
 
 
-def spread_matrices(depth):
-    row = lax.broadcasted_iota(jnp.int32, (depth, 2 * depth), 0)
-    col = lax.broadcasted_iota(jnp.int32, (depth, 2 * depth), 1)
-    one, zero = jnp.ones((), F32), jnp.zeros((), F32)
-    return (jnp.where(col == 2 * row, one, zero).astype(BF16), jnp.where(col == 2 * row + 1, one, zero).astype(BF16))
-
-
 def part_order(rows, inverse):
     i = lax.broadcasted_iota(jnp.int32, (rows, rows), 0)
     j = lax.broadcasted_iota(jnp.int32, (rows, rows), 1)
@@ -95,13 +91,14 @@
 class Front:
     def __init__(self, links, layer, gain_hbm, wa_hbm, wm_hbm, model_dim, outs, s):
         self.links, self.s, self.layer, self.model_dim = links, s, layer, model_dim
+        self.kept = EARLY[layer]
         self.gain_copy = links.copy(gain_hbm, s['gain_in'])
         self.qkv_out, self.zsend_out, self.zmine_out, self.h_out = outs
         self.chunks, self.cols = s['z_recv'].shape[1], s['z_recv'].shape[3]
         self.depth = s['wa'].shape[0]
         self.wa = links.copy(wa_hbm.at[layer], s['wa'])
         self.wm = links.copy(wm_hbm.at[layer], s['wm'])
-        self.wa_ready, self.wm_ready = False, False
+        self.wa_ready = False
         part = self.depth // 2
         self.mine = pl.ds(pl.multiple_of(links.y * part, part), part)
         self.h_yz = {}
@@ -113,8 +110,6 @@
         self.gain_copy.wait()
         gain = jnp.broadcast_to(self.s['gain_in'][self.layer:self.layer + 1, :].astype(F32), (lanes, self.depth)).T
         self.s['gain'][...] = gain
-        if 'even' in self.s:
-            self.s['even'][...], self.s['odd'][...] = spread_matrices(self.depth)
 
     def squares(self, p, h_t):
         s = self.s
@@ -147,15 +142,6 @@
         s['a_part'][p] = dot(u, s['wa'][...]).astype(BF16)
         self.a_core[p] = links.push(s['a_part'].at[p, pl.ds(0, 2 * shard)], s['a_core'].at[p], PARTNER, 'a_core')
 
-    def spread(self, p):
-        s = self.s
-        u = s['u_rel'][p]
-        gate, up = dot(u, s['even'][...]).astype(BF16), dot(u, s['odd'][...]).astype(BF16)
-        shard = u.shape[0] // 4
-        for k in range(4):
-            s['u2'][p, 2 * k * shard:(2 * k + 1) * shard] = gate[k * shard:(k + 1) * shard]
-            s['u2'][p, (2 * k + 1) * shard:(2 * k + 2) * shard] = up[k * shard:(k + 1) * shard]
-
     def attend_core(self, p):
         s = self.s
         half = s['a_core'].shape[1]
@@ -180,40 +166,31 @@
         for k, head in enumerate((y, 1 - y)):
             self.links.copy(s['a_full'].at[p, k], self.qkv_out.at[head, pl.ds(p * seqs, seqs)], 'qkv')
 
-    def project(self, p, j):
-        s = self.s
-        if not self.wm_ready:
-            self.wm.wait()
-            self.wm_ready = True
-        w = s['wm'][:, :, j * self.cols:(j + 1) * self.cols].reshape(2 * self.depth, self.cols)
-        s['z_part'][p, j] = dot(s['u2'][p], w).astype(BF16)
-        self.push_core(p, j)
-
-    def split_weights(self):
+    def split_weights(self, c):
         s, run = self.s, 128
         i = lax.broadcasted_iota(jnp.int32, (2 * run, 2 * run), 0)
         j = lax.broadcasted_iota(jnp.int32, (2 * run, 2 * run), 1)
         place = jnp.where(i < run, 2 * i, 2 * (i - run) + 1)
         order = jnp.where(j == place, jnp.ones((), F32), jnp.zeros((), F32)).astype(BF16)
-        self.wm.wait()
-        for c in range(self.chunks):
-            cols = slice(c * self.cols, (c + 1) * self.cols)
-            for e in range(self.depth // run):
-                rows = slice(e * run, (e + 1) * run)
-                w = dot(order, s['wm'][rows, :, cols].reshape(2 * run, self.cols)).astype(BF16)
-                s['w_split'][0, rows, cols] = w[:run]
-                s['w_split'][1, rows, cols] = w[run:]
-
-    def project_all(self, j):
+        if c == 0:
+            self.wm.wait()
+        cols = slice(c * self.cols, (c + 1) * self.cols)
+        for e in range(self.depth // run):
+            rows = slice(e * run, (e + 1) * run)
+            w = dot(order, s['wm'][rows, :, cols].reshape(2 * run, self.cols)).astype(BF16)
+            s['w_split'][0, rows, cols] = w[:run]
+            s['w_split'][1, rows, cols] = w[run:]
+
+    def project(self, parts, j):
         s = self.s
         lanes = s['u'].shape[1]
         shard = lanes // 4
-        u = s['u_rel'][...].reshape(PARTS * lanes, self.depth)
+        u = jnp.concatenate([s['u_rel'][p] for p in parts], axis=0)
         cols = slice(j * self.cols, (j + 1) * self.cols)
         gate, up = dot(u, s['w_split'][0, :, cols]).astype(BF16), dot(u, s['w_split'][1, :, cols]).astype(BF16)
-        for p in range(PARTS):
+        for n, p in enumerate(parts):
             for k in range(4):
-                rows = slice(p * lanes + k * shard, p * lanes + (k + 1) * shard)
+                rows = slice(n * lanes + k * shard, n * lanes + (k + 1) * shard)
                 s['z_part'][p, j, 2 * k * shard:(2 * k + 1) * shard] = gate[rows]
                 s['z_part'][p, j, (2 * k + 1) * shard:(2 * k + 2) * shard] = up[rows]
             self.push_core(p, j)
@@ -229,17 +206,17 @@
         shard2 = half // 2
         self.z_core[p, j].wait_recv()
         s['z_x'][unit] = (s['z_part'][p, j, half:half + shard2].astype(F32) + s['z_recv'][p, j, :shard2].astype(F32)).astype(BF16)
-        if unit < EARLY:
+        if unit < self.kept:
             self.early[unit] = self.links.push(s['z_x'].at[unit], s['z_early'].at[unit], ACROSS, 'early')
         else:
-            self.links.copy(s['z_x'].at[unit], self.zsend_out.at[unit - EARLY], 'z_x')
+            self.links.copy(s['z_x'].at[unit], self.zsend_out.at[unit - self.kept], 'z_x')
         s['z_mine'][unit] = (s['z_part'][p, j, half + shard2:].astype(F32) + s['z_recv'][p, j, shard2:].astype(F32)).astype(BF16)
-        if unit >= EARLY:
+        if unit >= self.kept:
             self.links.copy(s['z_mine'].at[unit], self.zmine_out.at[unit], 'z_mine')
 
     def finish(self):
         s = self.s
-        for unit in range(EARLY):
+        for unit in range(self.kept):
             self.early[unit].wait_recv()
             s['z_mine'][unit] = (s['z_mine'][unit].astype(F32) + s['z_early'][unit].astype(F32)).astype(BF16)
             self.links.copy(s['z_mine'].at[unit], self.zmine_out.at[unit], 'z_mine')
@@ -248,21 +225,22 @@
         s = self.s
         return ({'a_core': s['a_core'], 'a_got': s['a_got'], 'z': s['z_recv'], 'early': s['z_early'],
                  'sq': s['sq_recv'].at[:, pl.ds(0, len(EVERYONE))], 'h': s['h'].at[:, self.mine]},
-                {'z_x': s['z_x'].at[pl.ds(EARLY, s['z_x'].shape[0] - EARLY)], 'z_mine': s['z_mine'], 'qkv': s['a_full'], 'h': s['h'].at[:, self.mine]})
+                {'z_x': s['z_x'].at[pl.ds(self.kept, s['z_x'].shape[0] - self.kept)], 'z_mine': s['z_mine'], 'qkv': s['a_full'], 'h': s['h'].at[:, self.mine]})
 
 
 class Back:
     def __init__(self, links, layer, h_hbm, o_hbm, zgot_hbm, zmine_hbm, wd_hbm, wo_hbm, s):
         self.links, self.s = links, s
+        self.kept = EARLY[layer]
         self.chunks, self.cols = s['m'].shape[1], s['m'].shape[3]
         units = PARTS * self.chunks
         self.z = []
         for first, last in ((0, 1), (1, self.chunks), (self.chunks, units)):
             run = pl.ds(first, last - first)
             self.z.append((first, links.copy(zmine_hbm.at[run], s['z_in'].at[run])))
-            start = max(first, EARLY)
+            start = max(first, self.kept)
             if start < last:
-                run = pl.ds(start - EARLY, last - start)
+                run = pl.ds(start - self.kept, last - start)
                 self.z.append((start, links.copy(zgot_hbm.at[run], s['z_got'].at[run])))
             if first == 0:
                 self.o_copy = links.copy(o_hbm, s['o_in'])
@@ -279,8 +257,8 @@
         while self.z and self.z[0][0] <= unit:
             self.z.pop(0)[1].wait()
         z = s['z_in'][unit].astype(F32)
-        if unit >= EARLY:
-            z = (z + s['z_got'][unit - EARLY].astype(F32)).astype(BF16).astype(F32)
+        if unit >= self.kept:
+            z = (z + s['z_got'][unit - self.kept].astype(F32)).astype(BF16).astype(F32)
         shard = z.shape[0] // 2
         gate, up = z[:shard], z[shard:]
         s['m'][p, j, OWN * shard:] = (gate * jax.nn.sigmoid(gate) * up).astype(BF16)
@@ -407,14 +385,15 @@
     links.meet()
     for p in range(PARTS):
         f.send_h(p)
-    f.split_weights()
+    for j in range(f.chunks):
+        f.split_weights(j)
     for p in range(PARTS):
         f.normalize(p)
-    f.project_all(0)
+    f.project(range(PARTS), 0)
     for p in range(PARTS):
         f.attend_core(p)
     for j in range(1, f.chunks):
-        f.project_all(j)
+        f.project(range(PARTS), j)
         if j == f.chunks - 1:
             f.attend_ends(0)
         for p in range(PARTS):
@@ -439,33 +418,31 @@
         f.squares(p, b.new_h(p).astype(F32))
         f.send_h(p)
 
-    first_part(b)
+    first_part(b, f.split_weights)
     second_part(b, lambda: pass_h(0))
     f.normalize(0)
+    f.project([0], 0)
+    f.attend_core(0)
     pass_h(1)
-    f.spread(0)
-    f.attend_core(0)
-    f.project(0, 0)
-    f.project(0, 1)
-    f.project(0, 2)
+    f.project([0], 1)
+    f.project([0], 2)
     f.combine(0, 0)
-    f.project(0, 3)
+    f.project([0], 3)
     f.combine(0, 1)
-    f.project(0, 4)
+    f.project([0], 4)
     f.combine(0, 2)
     f.combine(0, 3)
     f.normalize(1)
-    f.spread(1)
-    f.project(1, 0)
+    f.project([1], 0)
+    f.combine(0, 4)
+    f.project([1], 1)
     f.attend_core(1)
-    f.combine(0, 4)
     f.attend_ends(0)
-    f.project(1, 1)
-    f.project(1, 2)
+    f.project([1], 2)
     f.combine(1, 0)
-    f.project(1, 3)
+    f.project([1], 3)
     f.combine(1, 1)
-    f.project(1, 4)
+    f.project([1], 4)
     f.combine(1, 2)
     f.combine(1, 3)
     f.attend_ends(1)
@@ -475,9 +452,11 @@
     links.drain({**sent, **b.sizes()}, stored)
 
 
-def first_part(b):
+def first_part(b, filler):
     for j in range(b.chunks):
         b.forward(0, j)
+        if filler is not None:
+            filler(j)
         if j == 2:
             b.forward_o(0)
         if j >= 1:
@@ -507,7 +486,7 @@
     links = Links(s['send'], s['recv'], s['local'], [PARTNER, ACROSS, YZ])
     b = Back(links, 1, h_hbm, o_hbm, zgot_hbm, zmine_hbm, wd_hbm, wo_hbm, s)
     b.open()
-    first_part(b)
+    first_part(b, None)
     h_new = []
     second_part(b, lambda: h_new.append(b.new_h(0)))
     order = part_order(h_out.shape[1], True)
@@ -516,29 +495,31 @@
     links.drain(b.sizes(), {})
 
 
-def attention_kernel(layer, per_step, len_hbm, qkv_hbm, k_hbm, v_hbm, *rest):
+def attention_kernel(layer, per_copy, per_step, len_hbm, qkv_hbm, k_hbm, v_hbm, *rest):
     k_out, v_out, o_hbm, kbuf, vbuf, q_scr, o_scr, qkv_ref, o_ref, len_ref, in_sem, out_sem, small_sem = rest[-13:]
     num_seqs, kv_heads, cache_len, head_dim = kbuf.shape
     slots = qkv_ref.shape[2] // head_dim
     rows = kv_heads * slots
     scale = head_dim ** -0.5
 
-    def load(i):
-        return (pltpu.make_async_copy(k_hbm.at[layer, i], kbuf.at[i], in_sem.at[0, i]),
-                pltpu.make_async_copy(v_hbm.at[layer, i], vbuf.at[i], in_sem.at[1, i]))
-
-    def store(i):
-        return (pltpu.make_async_copy(kbuf.at[i], k_out.at[layer, i], out_sem.at[0, i]),
-                pltpu.make_async_copy(vbuf.at[i], v_out.at[layer, i], out_sem.at[1, i]))
+    def load(n):
+        run = pl.ds(n * per_copy, per_copy)
+        return (pltpu.make_async_copy(k_hbm.at[layer, run], kbuf.at[run], in_sem.at[0, n]),
+                pltpu.make_async_copy(v_hbm.at[layer, run], vbuf.at[run], in_sem.at[1, n]))
+
+    def store(n):
+        run = pl.ds(n * per_copy, per_copy)
+        return (pltpu.make_async_copy(kbuf.at[run], k_out.at[layer, run], out_sem.at[0, n]),
+                pltpu.make_async_copy(vbuf.at[run], v_out.at[layer, run], out_sem.at[1, n]))
 
     qkv_copy = pltpu.make_async_copy(qkv_hbm, qkv_ref, small_sem.at[0])
     len_copy = pltpu.make_async_copy(len_hbm, len_ref, small_sem.at[1])
     qkv_copy.start()
     len_copy.start()
 
-    @pl.loop(0, num_seqs)
-    def _(i):
-        for c in load(i):
+    @pl.loop(0, num_seqs // per_copy)
+    def _(n):
+        for c in load(n):
             c.start()
 
     qkv_copy.wait()
@@ -551,12 +532,11 @@
     tile_row = lax.broadcasted_iota(jnp.int32, (16, head_dim), 0)
     position = lax.broadcasted_iota(jnp.int32, (rows, cache_len), 1)
 
-    @pl.loop(0, num_seqs // per_step)
-    def _(step):
-        group = [step * per_step + sub for sub in range(per_step)]
-        for i in group:
-            for c in load(i):
-                c.wait()
+    def patch(n):
+        for c in load(n):
+            c.wait()
+        for sub in range(per_copy):
+            i = n * per_copy + sub
             length = len_ref[i]
             base = pl.multiple_of((length // 16) * 16, 16)
             hit = tile_row == length - base
@@ -565,8 +545,10 @@
                     new = q_scr[pl.ds(i * rows + head * slots + j, 1), :]
                     old = buf[i, head, pl.ds(base, 16), :].astype(F32)
                     buf[i, head, pl.ds(base, 16), :] = jnp.where(hit, new, old).astype(buf.dtype)
-            for c in store(i):
-                c.start()
+        for c in store(n):
+            c.start()
+
+    def attend(group):
         scores, probs = [], []
         for i in group:
             q = q_scr[pl.ds(pl.multiple_of(i * rows, rows), rows), :].astype(BF16)
@@ -582,6 +564,12 @@
             o_scr[pl.ds(pl.multiple_of(i * rows, rows), rows), :] = jnp.concatenate(
                 [by_head[head][head * slots:(head + 1) * slots] for head in range(kv_heads)], axis=0)
 
+    @pl.loop(0, num_seqs // per_copy)
+    def _(n):
+        patch(n)
+        for first in range(0, per_copy, per_step):
+            attend([n * per_copy + first + sub for sub in range(per_step)])
+
     for head in range(kv_heads):
         for j in range(slots - 2):
             o_ref[head, :, j * head_dim:(j + 1) * head_dim] = (
@@ -589,9 +577,9 @@
     o_copy = pltpu.make_async_copy(o_ref, o_hbm, small_sem.at[2])
     o_copy.start()
 
-    @pl.loop(0, num_seqs)
-    def _(i):
-        for c in store(i):
+    @pl.loop(0, num_seqs // per_copy)
+    def _(n):
+        for c in store(n):
             c.wait()
 
     o_copy.wait()
@@ -606,7 +594,7 @@
     slots = qkv.shape[2] // head_dim
     rows = kv_heads * slots
     return pl.pallas_call(
-        functools.partial(attention_kernel, layer, 2),
+        functools.partial(attention_kernel, layer, PER_COPY, PER_STEP),
         out_shape=(jax.ShapeDtypeStruct(k_cache.shape, k_cache.dtype), jax.ShapeDtypeStruct(v_cache.shape, v_cache.dtype),
                    jax.ShapeDtypeStruct((kv_heads, num_seqs, (slots - 2) * head_dim), BF16)),
         in_specs=[HBM] * (4 + len(outs)),
@@ -615,7 +603,7 @@
         + [pltpu.VMEM((num_seqs * rows, head_dim), F32)] * 2 + [
             pltpu.VMEM(qkv.shape, BF16), pltpu.VMEM((kv_heads, num_seqs, (slots - 2) * head_dim), BF16),
             pltpu.SMEM((num_seqs,), jnp.int32)]
-        + [pltpu.SemaphoreType.DMA((2, num_seqs))] * 2 + [pltpu.SemaphoreType.DMA((3,))],
+        + [pltpu.SemaphoreType.DMA((2, num_seqs // PER_COPY))] * 2 + [pltpu.SemaphoreType.DMA((3,))],
         input_output_aliases={4: 0, 5: 1} if outs else {},
         compiler_params=pltpu.CompilerParams(vmem_limit_bytes=VMEM_LIMIT),
         cost_estimate=pl.CostEstimate(flops=10 ** 10, bytes_accessed=8 * num_seqs * kv_heads * cache_len * head_dim, transcendentals=0),
@@ -648,37 +636,38 @@
             return {'send': pltpu.SemaphoreType.DMA((groups,)), 'recv': pltpu.SemaphoreType.DMA((remote,)),
                     'local': pltpu.SemaphoreType.DMA((local,))}
 
-        front_scratch = {
-            'sq_send': pltpu.VMEM((PARTS, 8, lanes), F32), 'sq_recv': pltpu.VMEM((PARTS, 8, 8, lanes), F32),
-            'h': pltpu.VMEM((PARTS, depth, lanes), BF16), 'gain_in': pltpu.VMEM(norm_gain.shape, BF16), 'gain': pltpu.VMEM((depth, lanes), F32),
-            'u': pltpu.VMEM((PARTS, lanes, depth), BF16), 'u_rel': pltpu.VMEM((PARTS, lanes, depth), BF16),
-            'wa': pltpu.VMEM((depth, attn_cols), BF16), 'wm': pltpu.VMEM((depth, 2, mlp_cols), BF16),
-            'a_part': pltpu.VMEM((PARTS, lanes, attn_cols), BF16), 'a_core': pltpu.VMEM((PARTS, half, attn_cols), BF16),
-            'a_sum': pltpu.VMEM((PARTS, half, attn_cols), BF16), 'a_got': pltpu.VMEM((PARTS, 3, seqs, attn_cols), BF16),
-            'a_full': pltpu.VMEM((PARTS, 2, seqs, attn_cols), BF16),
-            'z_part': pltpu.VMEM((PARTS, CHUNKS, 2 * lanes, cols), BF16),
-            'z_recv': pltpu.VMEM((PARTS, CHUNKS, lanes, cols), BF16), 'z_x': pltpu.VMEM((units, half, cols), BF16),
-            'z_mine': pltpu.VMEM((units, half, cols), BF16), 'z_early': pltpu.VMEM((EARLY, half, cols), BF16),
-        }
-
-        split_scratch = {'w_split': pltpu.VMEM((2, depth, mlp_cols), BF16)}
-        spread_scratch = {
-            'even': pltpu.VMEM((depth, 2 * depth), BF16), 'odd': pltpu.VMEM((depth, 2 * depth), BF16),
-            'u2': pltpu.VMEM((PARTS, 2 * lanes, 2 * depth), BF16),
-        }
+        def front_scratch(layer):
+            return {
+                'sq_send': pltpu.VMEM((PARTS, SQ_ROWS, lanes), F32), 'sq_recv': pltpu.VMEM((PARTS, 8, SQ_ROWS, lanes), F32),
+                'h': pltpu.VMEM((PARTS, depth, lanes), BF16), 'gain_in': pltpu.VMEM(norm_gain.shape, BF16), 'gain': pltpu.VMEM((depth, lanes), F32),
+                'u': pltpu.VMEM((PARTS, lanes, depth), BF16), 'u_rel': pltpu.VMEM((PARTS, lanes, depth), BF16),
+                'wa': pltpu.VMEM((depth, attn_cols), BF16), 'wm': pltpu.VMEM((depth, 2, mlp_cols), BF16),
+                'w_split': pltpu.VMEM((2, depth, mlp_cols), BF16),
+                'a_part': pltpu.VMEM((PARTS, lanes, attn_cols), BF16), 'a_core': pltpu.VMEM((PARTS, half, attn_cols), BF16),
+                'a_sum': pltpu.VMEM((PARTS, half, attn_cols), BF16), 'a_got': pltpu.VMEM((PARTS, 3, seqs, attn_cols), BF16),
+                'a_full': pltpu.VMEM((PARTS, 2, seqs, attn_cols), BF16),
+                'z_part': pltpu.VMEM((PARTS, CHUNKS, 2 * lanes, cols), BF16),
+                'z_recv': pltpu.VMEM((PARTS, CHUNKS, lanes, cols), BF16), 'z_x': pltpu.VMEM((units, half, cols), BF16),
+                'z_mine': pltpu.VMEM((units, half, cols), BF16), 'z_early': pltpu.VMEM((EARLY[layer], half, cols), BF16),
+            }
+
         back_scratch = {
             'o_yz': pltpu.VMEM((num_seqs, out_depth), BF16), 'o': pltpu.VMEM((PARTS, lanes, out_depth), BF16),
             'm': pltpu.VMEM((PARTS, CHUNKS, lanes, cols), BF16), 'z_in': pltpu.VMEM((units, half, cols), BF16),
-            'z_got': pltpu.VMEM((units - EARLY, half, cols), BF16), 'o_in': pltpu.VMEM((2, num_seqs, out_depth), BF16),
+            'o_in': pltpu.VMEM((2, num_seqs, out_depth), BF16),
             'h_in': pltpu.VMEM((PARTS, part, lanes), BF16),
             'wd': pltpu.VMEM((mlp_cols, depth), BF16), 'wo': pltpu.VMEM((out_depth, depth), BF16),
             'acc': pltpu.VMEM((PARTS, lanes, depth), F32), 'update': pltpu.VMEM((PARTS, lanes, depth), F32),
             'up_part': pltpu.VMEM((PARTS, depth, lanes), BF16), 'up_recv': pltpu.VMEM((PARTS, part, lanes), BF16),
         }
 
-        front_shapes = (
-            jax.ShapeDtypeStruct((2, num_seqs, attn_cols), BF16), jax.ShapeDtypeStruct((units - EARLY, half, cols), BF16),
-            jax.ShapeDtypeStruct((units, half, cols), BF16), jax.ShapeDtypeStruct((PARTS, part, lanes), BF16))
+        def got_scratch(layer):
+            return {'z_got': pltpu.VMEM((units - EARLY[layer], half, cols), BF16)}
+
+        def front_shapes(layer):
+            return (
+                jax.ShapeDtypeStruct((2, num_seqs, attn_cols), BF16), jax.ShapeDtypeStruct((units - EARLY[layer], half, cols), BF16),
+                jax.ShapeDtypeStruct((units, half, cols), BF16), jax.ShapeDtypeStruct((PARTS, part, lanes), BF16))
         front_specs = (HBM,) * 4
 
         def call(kernel, name, collective_id, scratch, in_specs, out_shape, out_specs, *args):
@@ -695,17 +684,17 @@
             middle_kernel(names, model_dim, *refs)
 
         qkv, zsend, zmine, h_block = call(
-            start, 'start', 0, {**semaphores(6, 35, 8), **front_scratch, **split_scratch, 'h_in': pltpu.VMEM((part, rows), BF16)}, (HBM,) * 4,
-            front_shapes, front_specs, hidden.T, norm_gain, w_attn, w_mlp)
+            start, 'start', 0, {**semaphores(6, 34 + EARLY[0], 8), **front_scratch(0), 'h_in': pltpu.VMEM((part, rows), BF16)}, (HBM,) * 4,
+            front_shapes(0), front_specs, hidden.T, norm_gain, w_attn, w_mlp)
         zgot = lax.ppermute(zsend, 'x', swap)
         k_new, v_new, o = attention(0, lengths, qkv, k_cache, v_cache, ())
         qkv, zsend, zmine, h_block = call(
-            middle, 'middle', 1, {**semaphores(10, 66, 16), **front_scratch, **spread_scratch, **back_scratch}, (HBM,) * 9,
-            front_shapes, front_specs, h_block, o, norm_gain, zmine, zgot, w_down, w_out, w_attn, w_mlp)
+            middle, 'middle', 1, {**semaphores(10, 65 + EARLY[1], 16), **front_scratch(1), **back_scratch, **got_scratch(0)}, (HBM,) * 9,
+            front_shapes(1), front_specs, h_block, o, norm_gain, zmine, zgot, w_down, w_out, w_attn, w_mlp)
         zgot = lax.ppermute(zsend, 'x', swap)
         k_new, v_new, o = attention(1, lengths, qkv, k_cache, v_cache, (k_new, v_new))
         h_out = call(
-            end_kernel, 'end', 2, {**semaphores(4, 31, 9), **back_scratch}, (HBM,) * 6,
+            end_kernel, 'end', 2, {**semaphores(4, 31, 9), **back_scratch, **got_scratch(1)}, (HBM,) * 6,
             jax.ShapeDtypeStruct((part, rows), BF16), VMEM, h_block, o, zmine, zgot, w_down, w_out)
         return h_out.T, k_new, v_new
 

time: 126 us -> 122 us (0.968)
  Pallas kernels: 122 us -> 117 us
  waiting for transfers between devices: 0.01 us -> 1.57 us
    pallas_call x2, Pallas kernels: 48.4 us -> 44.3 us  [attention(): pl.pallas_call(functools.partial(attention_kernel, layer, PER_COPY, PER_S...]
    ppermute x2, waiting for transfers between devices: 0.01 us -> 1.57 us  [device_step(): zgot = lax.ppermute(zsend, 'x', swap)]
  transfers between devices with their start and end apart: 2 -> 2, of which waited for: 0 -> 1; matrix products, arithmetic and copies ran while one was open for 0% -> 0% of each run, Pallas kernels for 38% -> 36%
where the time goes in v7:
time: 122 us
  Pallas kernels  117 us (96%)
  starting transfers between devices  1.87 us (2%)
  waiting for transfers between devices  1.57 us (1%)
    pallas_call x3, Pallas kernels, call(): pl.pallas_call(functools.partial(kernel, tuple(scratch)), out_shape=out_s...  73 us
    pallas_call x2, Pallas kernels, attention(): pl.pallas_call(functools.partial(attention_kernel, layer, PER_COPY, PER_S...  44.3 us
  transfers between devices with their start and end apart: 2, of which 1 were waited for; matrix products, arithmetic and copies ran while one was open for 0% of the time, Pallas kernels for 36%

profile of v7, /device:TPU:0, one launch (start us, length us, event | category | flops | bytes accessed | tf_op | source)
XLA Modules:
  0.0 122.1 jit_solution(16316362585338263230)
XLA Ops:
  0.6 18.1 %start.1 = (bf16[2,32,1024]{2,1,0:T(8,128)(2,1)}, bf16[9,64,896]{2,1,0:T(8,128)(2,1)}, bf16[10,64,896]{2,1,0:T(8,128)(2,1)}, bf16[2,192,128]{2,1,0:T(8,128)(2,1)}) custom-call(bf16[192,256]{1,0:T(8,128)(2,1)} %bitcast.3, bf16[2,384]{1,0:T(2,128)(2,1)} %refs_2_.3, bf16[2,384,1024]{2,1,0:T(8,128)(2,1)} %refs_7_.1, bf16[2,384,2,4480]{3,2,1,0:T(2,128)(2,1)} %refs_8_.1), custom_call_target="tpu_custom_call" | custom-call | tf_op jit(solution)/shard_map/start/pallas_call | solution.py:674
  18.7 0.6 collective-permute-start
  19.3 22.2 %attention_0.1 = (bf16[2,32,2,1024,128]{4,3,2,1,0:T(8,128)(2,1)}, bf16[2,32,2,1024,128]{4,3,2,1,0:T(8,128)(2,1)}, bf16[2,32,768]{2,1,0:T(8,128)(2,1)}) custom-call(s32[32]{0:T(128)} %len_hbm.3, bf16[2,32,1024]{2,1,0:T(8,128)(2,1)} %get-tuple-element.18.qkv_hbm, bf16[2,32,2,1024,128]{4,3,2,1,0:T(8,128)(2,1)} %k_hbm.3, bf16[2,32,2,1024,128]{4,3,2,1,0:T(8,128)(2,1)} %v_hbm.3), custom_call_target="tpu_custom_call" | custom-call | flops 10000000000 | bytes 67108864 | tf_op jit(solution)/shard_map/attention_0/pallas_call | solution.py:596
  41.5 1.6 %collective-permute-done.refs_4_ = bf16[9,64,896]{2,1,0:T(8,128)(2,1)} collective-permute-done((bf16[9,64,896]{2,1,0:T(8,128)(2,1)}, bf16[9,64,896]{2,1,0:T(8,128)(2,1)}, u32[]{:S(2)}, u32[]{:S(2)}) %collective-permute-start) | collective-permute-done | bytes 1032224 | tf_op jit(solution)/shard_map/ppermute | solution.py:689
  43.1 33.3 %middle.1 = (bf16[2,32,1024]{2,1,0:T(8,128)(2,1)}, bf16[8,64,896]{2,1,0:T(8,128)(2,1)}, bf16[10,64,896]{2,1,0:T(8,128)(2,1)}, bf16[2,192,128]{2,1,0:T(8,128)(2,1)}) custom-call(bf16[2,192,128]{2,1,0:T(8,128)(2,1)} %get-tuple-element.17.refs_0_, bf16[2,32,768]{2,1,0:T(8,128)(2,1)} %get-tuple-element.19.refs_1_, bf16[2,384]{1,0:T(2,128)(2,1)} %refs_2_.3, ...), custom_call_target="tpu_custom_call" | custom-call | tf_op jit(solution)/shard_map/middle/pallas_call | solution.py:674
  76.4 1.2 %collective-permute-start.1 = (bf16[8,64,896]{2,1,0:T(8,128)(2,1)}, bf16[8,64,896]{2,1,0:T(8,128)(2,1)}, u32[]{:S(2)}, u32[]{:S(2)}) collective-permute-start(bf16[8,64,896]{2,1,0:T(8,128)(2,1)} %get-tuple-element.28), channel_id=1, source_target_pairs={{0,2},{2,0},{1,3},{3,1},{4,6},{6,4},{5,7},{7,5}} | collective-permute-start | bytes 2752520 | tf_op jit(solution)/shard_map/ppermute | solution.py:694
  77.6 22.2 %attention_1.1 = (bf16[2,32,2,1024,128]{4,3,2,1,0:T(8,128)(2,1)}, bf16[2,32,2,1024,128]{4,3,2,1,0:T(8,128)(2,1)}, bf16[2,32,768]{2,1,0:T(8,128)(2,1)}) custom-call(s32[32]{0:T(128)} %len_hbm.3, bf16[2,32,1024]{2,1,0:T(8,128)(2,1)} %get-tuple-element.23.qkv_hbm, bf16[2,32,2,1024,128]{4,3,2,1,0:T(8,128)(2,1)} %k_hbm.3, ...), custom_call_target="tpu_custom_call", output_to_operand_aliasing={{0}: (4, {}), {1}: (5, {})} | custom-call | flops 10000000000 | bytes 67108864 | tf_op jit(solution)/shard_map/attention_1/pallas_call | solution.py:596
  99.8 0.0 collective-permute-done.1.zgot_hbm
  99.8 21.7 %end.1 = bf16[192,256]{1,0:T(8,128)(2,1)S(1)} custom-call(bf16[2,192,128]{2,1,0:T(8,128)(2,1)} %get-tuple-element.22.h_hbm, bf16[2,32,768]{2,1,0:T(8,128)(2,1)} %get-tuple-element.26.o_hbm, bf16[10,64,896]{2,1,0:T(8,128)(2,1)} %get-tuple-element.27.zmine_hbm, bf16[8,64,896]{2,1,0:T(8,128)(2,1)} %collective-permute-done.1.zgot_hbm, ...), custom_call_target="tpu_custom_call" | custom-call | tf_op jit(solution)/shard_map/end/pallas_call | solution.py:674
  121.5 0.6 copy.17
Async XLA Ops:
  18.7 24.4 %collective-permute-start = (bf16[9,64,896]{2,1,0:T(8,128)(2,1)}, bf16[9,64,896]{2,1,0:T(8,128)(2,1)}, u32[]{:S(2)}, u32[]{:S(2)}) collective-permute-start(bf16[9,64,896]{2,1,0:T(8,128)(2,1)} %get-tuple-element.21), channel_id=1, source_target_pairs={{0,2},{2,0},{1,3},{3,1},{4,6},{6,4},{5,7},{7,5}} | collective-permute-start | bytes 3096584 | tf_op jit(solution)/shard_map/ppermute | solution.py:689
  76.4 23.4 %collective-permute-start.1 = (bf16[8,64,896]{2,1,0:T(8,128)(2,1)}, bf16[8,64,896]{2,1,0:T(8,128)(2,1)}, u32[]{:S(2)}, u32[]{:S(2)}) collective-permute-start(bf16[8,64,896]{2,1,0:T(8,128)(2,1)} %get-tuple-element.28), channel_id=1, source_target_pairs={{0,2},{2,0},{1,3},{3,1},{4,6},{6,4},{5,7},{7,5}} | collective-permute-start | bytes 2752520 | tf_op jit(solution)/shard_map/ppermute | solution.py:694

commit v8 on v7

--- a/solution.py
+++ b/solution.py
@@ -17,6 +17,7 @@
 PER_STEP = 2
 CHUNKS = 5
 EARLY = (1, 2)
+CARRY = (0, 2)
 END_VMEM_LIMIT = 56393728
 VMEM_LIMIT = 67043328
 
@@ -78,6 +79,12 @@
 PARTS = 2
 
 
+def gated(z):
+    shard = z.shape[0] // 2
+    gate, up = z[:shard].astype(F32), z[shard:].astype(F32)
+    return (gate * jax.nn.sigmoid(gate) * up).astype(BF16)
+
+
 def part_order(rows, inverse):
     i = lax.broadcasted_iota(jnp.int32, (rows, rows), 0)
     j = lax.broadcasted_iota(jnp.int32, (rows, rows), 1)
@@ -91,7 +98,7 @@
 class Front:
     def __init__(self, links, layer, gain_hbm, wa_hbm, wm_hbm, model_dim, outs, s):
         self.links, self.s, self.layer, self.model_dim = links, s, layer, model_dim
-        self.kept = EARLY[layer]
+        self.kept, self.carry = EARLY[layer], CARRY[layer]
         self.gain_copy = links.copy(gain_hbm, s['gain_in'])
         self.qkv_out, self.zsend_out, self.zmine_out, self.h_out = outs
         self.chunks, self.cols = s['z_recv'].shape[1], s['z_recv'].shape[3]
@@ -214,26 +221,32 @@
         if unit >= self.kept:
             self.links.copy(s['z_mine'].at[unit], self.zmine_out.at[unit], 'z_mine')
 
-    def finish(self):
+    def take_early(self):
         s = self.s
         for unit in range(self.kept):
             self.early[unit].wait_recv()
             s['z_mine'][unit] = (s['z_mine'][unit].astype(F32) + s['z_early'][unit].astype(F32)).astype(BF16)
             self.links.copy(s['z_mine'].at[unit], self.zmine_out.at[unit], 'z_mine')
+        if self.carry:
+            shard = s['z_mine'].shape[1] // 2
+            for unit in range(self.carry):
+                s['m_early'][unit * shard:(unit + 1) * shard] = gated(s['z_mine'][unit])
+            self.links.copy(s['m_early'], self.zsend_out.at[s['z_x'].shape[0] - self.kept], 'm_early')
 
     def sizes(self):
         s = self.s
         return ({'a_core': s['a_core'], 'a_got': s['a_got'], 'z': s['z_recv'], 'early': s['z_early'],
                  'sq': s['sq_recv'].at[:, pl.ds(0, len(EVERYONE))], 'h': s['h'].at[:, self.mine]},
-                {'z_x': s['z_x'].at[pl.ds(self.kept, s['z_x'].shape[0] - self.kept)], 'z_mine': s['z_mine'], 'qkv': s['a_full'], 'h': s['h'].at[:, self.mine]})
+                {'z_x': s['z_x'].at[pl.ds(self.kept, s['z_x'].shape[0] - self.kept)], 'z_mine': s['z_mine'], 'qkv': s['a_full'], 'h': s['h'].at[:, self.mine], 'm_early': s.get('m_early')})
 
 
 class Back:
     def __init__(self, links, layer, h_hbm, o_hbm, zgot_hbm, zmine_hbm, wd_hbm, wo_hbm, s):
         self.links, self.s = links, s
-        self.kept = EARLY[layer]
+        self.kept, self.carry = EARLY[layer], CARRY[layer]
         self.chunks, self.cols = s['m'].shape[1], s['m'].shape[3]
         units = PARTS * self.chunks
+        shard = s['m'].shape[2] // 4
         self.z = []
         for first, last in ((0, 1), (1, self.chunks), (self.chunks, units)):
             run = pl.ds(first, last - first)
@@ -243,6 +256,8 @@
                 run = pl.ds(start - self.kept, last - start)
                 self.z.append((start, links.copy(zgot_hbm.at[run], s['z_got'].at[run])))
             if first == 0:
+                self.carried = [links.copy(zgot_hbm.at[units - self.kept, pl.ds(j * shard, shard)], self.block(0, j, ACROSS))
+                                for j in range(self.carry)]
                 self.o_copy = links.copy(o_hbm, s['o_in'])
                 self.h_copy = links.copy(h_hbm, s['h_in'])
         self.wd = links.copy(wd_hbm.at[layer], s['wd'])
@@ -256,19 +271,18 @@
         s, unit = self.s, p * self.chunks + j
         while self.z and self.z[0][0] <= unit:
             self.z.pop(0)[1].wait()
-        z = s['z_in'][unit].astype(F32)
+        z = s['z_in'][unit]
         if unit >= self.kept:
-            z = (z + s['z_got'][unit - self.kept].astype(F32)).astype(BF16).astype(F32)
-        shard = z.shape[0] // 2
-        gate, up = z[:shard], z[shard:]
-        s['m'][p, j, OWN * shard:] = (gate * jax.nn.sigmoid(gate) * up).astype(BF16)
+            z = (z.astype(F32) + s['z_got'][unit - self.kept].astype(F32)).astype(BF16)
+        s['m'][p, j, OWN * (z.shape[0] // 2):] = gated(z)
 
     def block(self, p, j, k):
         shard = self.s['m'].shape[2] // 4
         return self.s['m'].at[p, j, pl.ds(k * shard, shard)]
 
     def send(self, p, j):
-        self.across[p, j] = self.links.push(self.block(p, j, OWN), self.block(p, j, ACROSS), ACROSS, 'm')
+        if p > 0 or j >= self.carry:
+            self.across[p, j] = self.links.push(self.block(p, j, OWN), self.block(p, j, ACROSS), ACROSS, 'm_across')
 
     def send_partner(self, p):
         m = self.s['m']
@@ -276,7 +290,10 @@
         self.partner[p] = self.links.push(m.at[p, :, pl.ds(OWN * shard, shard)], m.at[p, :, pl.ds(PARTNER * shard, shard)], PARTNER, 'm')
 
     def forward(self, p, j):
-        self.across[p, j].wait_recv()
+        if p > 0 or j >= self.carry:
+            self.across[p, j].wait_recv()
+        else:
+            self.carried[j].wait()
         self.diag[p, j] = self.links.push(self.block(p, j, ACROSS), self.block(p, j, DIAG), PARTNER, 'm')
 
     def send_o_yz(self):
@@ -346,7 +363,9 @@
     def sizes(self):
         s = self.s
         sent = 3 * s['m'].shape[2] // 4
-        return {'m': s['m'].at[:, :, pl.ds(0, sent)], 'o': s['o'].at[:, pl.ds(0, sent)], 'o_yz': s['o_yz'], 'up': s['up_recv']}
+        shard = sent // 3
+        return {'m': s['m'].at[:, :, pl.ds(0, 2 * shard)],
+                'm_across': s['m'].at[:, pl.ds(0, self.chunks - self.carry // PARTS), pl.ds(0, shard)], 'o': s['o'].at[:, pl.ds(0, sent)], 'o_yz': s['o_yz'], 'up': s['up_recv']}
 
     def open(self):
         links, chunks = self.links, self.chunks
@@ -401,7 +420,7 @@
     f.attend_ends(1)
     for p in range(PARTS):
         f.combine(p, f.chunks - 1)
-    f.finish()
+    f.take_early()
     links.drain(*f.sizes())
 
 
@@ -445,9 +464,9 @@
     f.project([1], 4)
     f.combine(1, 2)
     f.combine(1, 3)
+    f.take_early()
+    f.combine(1, 4)
     f.attend_ends(1)
-    f.combine(1, 4)
-    f.finish()
     sent, stored = f.sizes()
     links.drain({**sent, **b.sizes()}, stored)
 
@@ -666,7 +685,7 @@
 
         def front_shapes(layer):
             return (
-                jax.ShapeDtypeStruct((2, num_seqs, attn_cols), BF16), jax.ShapeDtypeStruct((units - EARLY[layer], half, cols), BF16),
+                jax.ShapeDtypeStruct((2, num_seqs, attn_cols), BF16), jax.ShapeDtypeStruct((units - EARLY[layer] + CARRY[layer] // PARTS, half, cols), BF16),
                 jax.ShapeDtypeStruct((units, half, cols), BF16), jax.ShapeDtypeStruct((PARTS, part, lanes), BF16))
         front_specs = (HBM,) * 4
 
@@ -689,12 +708,13 @@
         zgot = lax.ppermute(zsend, 'x', swap)
         k_new, v_new, o = attention(0, lengths, qkv, k_cache, v_cache, ())
         qkv, zsend, zmine, h_block = call(
-            middle, 'middle', 1, {**semaphores(10, 65 + EARLY[1], 16), **front_scratch(1), **back_scratch, **got_scratch(0)}, (HBM,) * 9,
+            middle, 'middle', 1, {**semaphores(11, 65 + EARLY[1], 17), **front_scratch(1), **back_scratch, **got_scratch(0),
+                       'm_early': pltpu.VMEM((half, cols), BF16)}, (HBM,) * 9,
             front_shapes(1), front_specs, h_block, o, norm_gain, zmine, zgot, w_down, w_out, w_attn, w_mlp)
         zgot = lax.ppermute(zsend, 'x', swap)
         k_new, v_new, o = attention(1, lengths, qkv, k_cache, v_cache, (k_new, v_new))
         h_out = call(
-            end_kernel, 'end', 2, {**semaphores(4, 31, 9), **back_scratch, **got_scratch(1)}, (HBM,) * 6,
+            end_kernel, 'end', 2, {**semaphores(5, 29, 11), **back_scratch, **got_scratch(1)}, (HBM,) * 6,
             jax.ShapeDtypeStruct((part, rows), BF16), VMEM, h_block, o, zmine, zgot, w_down, w_out)
         return h_out.T, k_new, v_new
 

time: 122 us -> 122 us (level)
    pallas_call x3, Pallas kernels: 73 us -> 71.8 us  [call(): pl.pallas_call(functools.partial(kernel, tuple(scratch)), out_shape=out_s...]
  transfers between devices with their start and end apart: 2 -> 2, of which waited for: 1 -> 2; matrix products, arithmetic and copies ran while one was open for 0% -> 0% of each run, Pallas kernels for 36% -> 36%
where the time goes in v8:
time: 122 us
  Pallas kernels  116 us (95%)
  waiting for transfers between devices  2.39 us (2%)
  starting transfers between devices  1.87 us (2%)
    pallas_call x3, Pallas kernels, call(): pl.pallas_call(functools.partial(kernel, tuple(scratch)), out_shape=out_s...  71.8 us
    pallas_call x2, Pallas kernels, attention(): pl.pallas_call(functools.partial(attention_kernel, layer, PER_COPY, PER_S...  44.3 us
  transfers between devices with their start and end apart: 2, of which 2 were waited for; matrix products, arithmetic and copies ran while one was open for 0% of the time, Pallas kernels for 36%

profile of v8, /device:TPU:0, one launch (start us, length us, event | category | flops | bytes accessed | tf_op | source)
XLA Modules:
  0.0 121.7 jit_solution(3184608081676912440)
XLA Ops:
  0.6 18.1 %start.1 = (bf16[2,32,1024]{2,1,0:T(8,128)(2,1)}, bf16[9,64,896]{2,1,0:T(8,128)(2,1)}, bf16[10,64,896]{2,1,0:T(8,128)(2,1)}, bf16[2,192,128]{2,1,0:T(8,128)(2,1)}) custom-call(bf16[192,256]{1,0:T(8,128)(2,1)} %bitcast.3, bf16[2,384]{1,0:T(2,128)(2,1)} %refs_2_.3, bf16[2,384,1024]{2,1,0:T(8,128)(2,1)} %refs_7_.1, bf16[2,384,2,4480]{3,2,1,0:T(2,128)(2,1)} %refs_8_.1), custom_call_target="tpu_custom_call" | custom-call | tf_op jit(solution)/shard_map/start/pallas_call | solution.py:693
  18.7 0.6 collective-permute-start
  19.3 22.2 %attention_0.1 = (bf16[2,32,2,1024,128]{4,3,2,1,0:T(8,128)(2,1)}, bf16[2,32,2,1024,128]{4,3,2,1,0:T(8,128)(2,1)}, bf16[2,32,768]{2,1,0:T(8,128)(2,1)}) custom-call(s32[32]{0:T(128)} %len_hbm.3, bf16[2,32,1024]{2,1,0:T(8,128)(2,1)} %get-tuple-element.18.qkv_hbm, bf16[2,32,2,1024,128]{4,3,2,1,0:T(8,128)(2,1)} %k_hbm.3, bf16[2,32,2,1024,128]{4,3,2,1,0:T(8,128)(2,1)} %v_hbm.3), custom_call_target="tpu_custom_call" | custom-call | flops 10000000000 | bytes 67108864 | tf_op jit(solution)/shard_map/attention_0/pallas_call | solution.py:615
  41.5 1.6 %collective-permute-done.refs_4_ = bf16[9,64,896]{2,1,0:T(8,128)(2,1)} collective-permute-done((bf16[9,64,896]{2,1,0:T(8,128)(2,1)}, bf16[9,64,896]{2,1,0:T(8,128)(2,1)}, u32[]{:S(2)}, u32[]{:S(2)}) %collective-permute-start) | collective-permute-done | bytes 1032224 | tf_op jit(solution)/shard_map/ppermute | solution.py:708
  43.1 33.1 %middle.1 = (bf16[2,32,1024]{2,1,0:T(8,128)(2,1)}, bf16[9,64,896]{2,1,0:T(8,128)(2,1)}, bf16[10,64,896]{2,1,0:T(8,128)(2,1)}, bf16[2,192,128]{2,1,0:T(8,128)(2,1)}) custom-call(bf16[2,192,128]{2,1,0:T(8,128)(2,1)} %get-tuple-element.17.refs_0_, bf16[2,32,768]{2,1,0:T(8,128)(2,1)} %get-tuple-element.19.refs_1_, bf16[2,384]{1,0:T(2,128)(2,1)} %refs_2_.3, ...), custom_call_target="tpu_custom_call" | custom-call | tf_op jit(solution)/shard_map/middle/pallas_call | solution.py:693
  76.2 1.2 %collective-permute-start.1 = (bf16[9,64,896]{2,1,0:T(8,128)(2,1)}, bf16[9,64,896]{2,1,0:T(8,128)(2,1)}, u32[]{:S(2)}, u32[]{:S(2)}) collective-permute-start(bf16[9,64,896]{2,1,0:T(8,128)(2,1)} %get-tuple-element.28), channel_id=1, source_target_pairs={{0,2},{2,0},{1,3},{3,1},{4,6},{6,4},{5,7},{7,5}} | collective-permute-start | bytes 3096584 | tf_op jit(solution)/shard_map/ppermute | solution.py:714
  77.4 22.2 %attention_1.1 = (bf16[2,32,2,1024,128]{4,3,2,1,0:T(8,128)(2,1)}, bf16[2,32,2,1024,128]{4,3,2,1,0:T(8,128)(2,1)}, bf16[2,32,768]{2,1,0:T(8,128)(2,1)}) custom-call(s32[32]{0:T(128)} %len_hbm.3, bf16[2,32,1024]{2,1,0:T(8,128)(2,1)} %get-tuple-element.23.qkv_hbm, bf16[2,32,2,1024,128]{4,3,2,1,0:T(8,128)(2,1)} %k_hbm.3, ...), custom_call_target="tpu_custom_call", output_to_operand_aliasing={{0}: (4, {}), {1}: (5, {})} | custom-call | flops 10000000000 | bytes 67108864 | tf_op jit(solution)/shard_map/attention_1/pallas_call | solution.py:615
  99.6 0.8 collective-permute-done.1.zgot_hbm
  100.4 20.6 %end.1 = bf16[192,256]{1,0:T(8,128)(2,1)S(1)} custom-call(bf16[2,192,128]{2,1,0:T(8,128)(2,1)} %get-tuple-element.22.h_hbm, bf16[2,32,768]{2,1,0:T(8,128)(2,1)} %get-tuple-element.26.o_hbm, bf16[10,64,896]{2,1,0:T(8,128)(2,1)} %get-tuple-element.27.zmine_hbm, bf16[9,64,896]{2,1,0:T(8,128)(2,1)} %collective-permute-done.1.zgot_hbm, ...), custom_call_target="tpu_custom_call" | custom-call | tf_op jit(solution)/shard_map/end/pallas_call | solution.py:693
  121.0 0.6 copy.17
Async XLA Ops:
  18.7 24.4 %collective-permute-start = (bf16[9,64,896]{2,1,0:T(8,128)(2,1)}, bf16[9,64,896]{2,1,0:T(8,128)(2,1)}, u32[]{:S(2)}, u32[]{:S(2)}) collective-permute-start(bf16[9,64,896]{2,1,0:T(8,128)(2,1)} %get-tuple-element.21), channel_id=1, source_target_pairs={{0,2},{2,0},{1,3},{3,1},{4,6},{6,4},{5,7},{7,5}} | collective-permute-start | bytes 3096584 | tf_op jit(solution)/shard_map/ppermute | solution.py:708
  76.2 24.2 %collective-permute-start.1 = (bf16[9,64,896]{2,1,0:T(8,128)(2,1)}, bf16[9,64,896]{2,1,0:T(8,128)(2,1)}, u32[]{:S(2)}, u32[]{:S(2)}) collective-permute-start(bf16[9,64,896]{2,1,0:T(8,128)(2,1)} %get-tuple-element.28), channel_id=1, source_target_pairs={{0,2},{2,0},{1,3},{3,1},{4,6},{6,4},{5,7},{7,5}} | collective-permute-start | bytes 3096584 | tf_op jit(solution)/shard_map/ppermute | solution.py:714

commit v9 on v8

--- a/solution.py
+++ b/solution.py
@@ -1,4 +1,5 @@
 import functools
+import types
 
 import jax
 import jax.numpy as jnp
@@ -99,12 +100,12 @@
     def __init__(self, links, layer, gain_hbm, wa_hbm, wm_hbm, model_dim, outs, s):
         self.links, self.s, self.layer, self.model_dim = links, s, layer, model_dim
         self.kept, self.carry = EARLY[layer], CARRY[layer]
-        self.gain_copy = links.copy(gain_hbm, s['gain_in'])
+        self.gain_copy = links.copy(gain_hbm, s.gain_in)
         self.qkv_out, self.zsend_out, self.zmine_out, self.h_out = outs
-        self.chunks, self.cols = s['z_recv'].shape[1], s['z_recv'].shape[3]
-        self.depth = s['wa'].shape[0]
-        self.wa = links.copy(wa_hbm.at[layer], s['wa'])
-        self.wm = links.copy(wm_hbm.at[layer], s['wm'])
+        self.chunks, self.cols = s.z_recv.shape[1], s.z_recv.shape[3]
+        self.depth = s.wa.shape[0]
+        self.wa = links.copy(wa_hbm.at[layer], s.wa)
+        self.wm = links.copy(wm_hbm.at[layer], s.wm)
         self.wa_ready = False
         part = self.depth // 2
         self.mine = pl.ds(pl.multiple_of(links.y * part, part), part)
@@ -113,65 +114,65 @@
         self.sq = {}
 
     def constants(self):
-        lanes = self.s['u'].shape[1]
+        lanes = self.s.u.shape[1]
         self.gain_copy.wait()
-        gain = jnp.broadcast_to(self.s['gain_in'][self.layer:self.layer + 1, :].astype(F32), (lanes, self.depth)).T
-        self.s['gain'][...] = gain
+        gain = jnp.broadcast_to(self.s.gain_in[self.layer:self.layer + 1, :].astype(F32), (lanes, self.depth)).T
+        self.s.gain[...] = gain
 
     def squares(self, p, h_t):
         s = self.s
-        s['h'][p, self.mine, :] = h_t.astype(BF16)
-        s['sq_send'][p] = jnp.broadcast_to(jnp.sum(h_t * h_t, axis=0, keepdims=True), s['sq_send'].shape[1:])
+        s.h[p, self.mine, :] = h_t.astype(BF16)
+        s.sq_send[p] = jnp.broadcast_to(jnp.sum(h_t * h_t, axis=0, keepdims=True), s.sq_send.shape[1:])
 
     def send_h(self, p):
         s, links = self.s, self.links
-        self.sq[p] = [links.push(s['sq_send'].at[p], s['sq_recv'].at[p, k], k, 'sq') for k in EVERYONE]
-        self.h_yz[p] = links.push(s['h'].at[p, self.mine], s['h'].at[p, self.mine], YZ, 'h')
-        links.copy(s['h'].at[p, self.mine], self.h_out.at[p], 'h')
+        self.sq[p] = [links.push(s.sq_send.at[p], s.sq_recv.at[p, k], k, 'sq') for k in EVERYONE]
+        self.h_yz[p] = links.push(s.h.at[p, self.mine], s.h.at[p, self.mine], YZ, 'h')
+        links.copy(s.h.at[p, self.mine], self.h_out.at[p], 'h')
 
     def normalize(self, p):
         s, links = self.s, self.links
         for c in self.sq[p]:
             c.wait_recv()
-        total = s['sq_send'][p]
+        total = s.sq_send[p]
         for k in EVERYONE:
-            total = total + s['sq_recv'][p, k]
+            total = total + s.sq_recv[p, k]
         self.h_yz[p].wait_recv()
-        h_t = s['h'][p].astype(F32)
+        h_t = s.h[p].astype(F32)
         inv_rms = lax.rsqrt(total[:1] / self.model_dim + NORM_EPS)
-        s['u'][p] = (h_t * inv_rms * s['gain'][...]).T.astype(BF16)
-        shard = s['u'].shape[1] // 4
-        u = jnp.concatenate([s['u'][p, pl.ds(pl.multiple_of(b * shard, shard), shard), :] for b in links.blocks], axis=0)
-        s['u_rel'][p] = u
+        s.u[p] = (h_t * inv_rms * s.gain[...]).T.astype(BF16)
+        shard = s.u.shape[1] // 4
+        u = jnp.concatenate([s.u[p, pl.ds(pl.multiple_of(b * shard, shard), shard), :] for b in links.blocks], axis=0)
+        s.u_rel[p] = u
         if not self.wa_ready:
             self.wa.wait()
             self.wa_ready = True
-        s['a_part'][p] = dot(u, s['wa'][...]).astype(BF16)
-        self.a_core[p] = links.push(s['a_part'].at[p, pl.ds(0, 2 * shard)], s['a_core'].at[p], PARTNER, 'a_core')
+        s.a_part[p] = dot(u, s.wa[...]).astype(BF16)
+        self.a_core[p] = links.push(s.a_part.at[p, pl.ds(0, 2 * shard)], s.a_core.at[p], PARTNER, 'a_core')
 
     def attend_core(self, p):
         s = self.s
-        half = s['a_core'].shape[1]
+        half = s.a_core.shape[1]
         self.a_core[p].wait_recv()
-        s['a_sum'][p] = (s['a_part'][p, half:].astype(F32) + s['a_core'][p].astype(F32)).astype(BF16)
-        shard, seqs = half // 2, s['a_got'].shape[2]
+        s.a_sum[p] = (s.a_part[p, half:].astype(F32) + s.a_core[p].astype(F32)).astype(BF16)
+        shard, seqs = half // 2, s.a_got.shape[2]
         y = self.links.y
         here, there = pl.multiple_of(y * seqs, seqs), pl.multiple_of((1 - y) * seqs, seqs)
         self.a_got[p] = [
-            self.links.push(s['a_sum'].at[p, pl.ds(there, seqs)], s['a_got'].at[p, 2], ACROSS_YZ, 'a_got'),
-            self.links.push(s['a_sum'].at[p, pl.ds(here, seqs)], s['a_got'].at[p, 0], ACROSS, 'a_got'),
-            self.links.push(s['a_sum'].at[p, pl.ds(shard + there, seqs)], s['a_got'].at[p, 1], YZ, 'a_got')]
+            self.links.push(s.a_sum.at[p, pl.ds(there, seqs)], s.a_got.at[p, 2], ACROSS_YZ, 'a_got'),
+            self.links.push(s.a_sum.at[p, pl.ds(here, seqs)], s.a_got.at[p, 0], ACROSS, 'a_got'),
+            self.links.push(s.a_sum.at[p, pl.ds(shard + there, seqs)], s.a_got.at[p, 1], YZ, 'a_got')]
 
     def attend_ends(self, p):
         s, y = self.s, self.links.y
-        shard, seqs = s['a_sum'].shape[1] // 2, s['a_got'].shape[2]
+        shard, seqs = s.a_sum.shape[1] // 2, s.a_got.shape[2]
         for c in self.a_got[p]:
             c.wait_recv()
-        own = s['a_sum'][p, pl.ds(shard + pl.multiple_of(y * seqs, seqs), seqs), :]
-        s['a_full'][p, 0] = (own.astype(F32) + s['a_got'][p, 0].astype(F32)).astype(BF16)
-        s['a_full'][p, 1] = (s['a_got'][p, 1].astype(F32) + s['a_got'][p, 2].astype(F32)).astype(BF16)
+        own = s.a_sum[p, pl.ds(shard + pl.multiple_of(y * seqs, seqs), seqs), :]
+        s.a_full[p, 0] = (own.astype(F32) + s.a_got[p, 0].astype(F32)).astype(BF16)
+        s.a_full[p, 1] = (s.a_got[p, 1].astype(F32) + s.a_got[p, 2].astype(F32)).astype(BF16)
         for k, head in enumerate((y, 1 - y)):
-            self.links.copy(s['a_full'].at[p, k], self.qkv_out.at[head, pl.ds(p * seqs, seqs)], 'qkv')
+            self.links.copy(s.a_full.at[p, k], self.qkv_out.at[head, pl.ds(p * seqs, seqs)], 'qkv')
 
     def split_weights(self, c):
         s, run = self.s, 128
@@ -184,84 +185,84 @@
         cols = slice(c * self.cols, (c + 1) * self.cols)
         for e in range(self.depth // run):
             rows = slice(e * run, (e + 1) * run)
-            w = dot(order, s['wm'][rows, :, cols].reshape(2 * run, self.cols)).astype(BF16)
-            s['w_split'][0, rows, cols] = w[:run]
-            s['w_split'][1, rows, cols] = w[run:]
+            w = dot(order, s.wm[rows, :, cols].reshape(2 * run, self.cols)).astype(BF16)
+            s.w_split[0, rows, cols] = w[:run]
+            s.w_split[1, rows, cols] = w[run:]
 
     def project(self, parts, j):
         s = self.s
-        lanes = s['u'].shape[1]
+        lanes = s.u.shape[1]
         shard = lanes // 4
-        u = jnp.concatenate([s['u_rel'][p] for p in parts], axis=0)
+        u = jnp.concatenate([s.u_rel[p] for p in parts], axis=0)
         cols = slice(j * self.cols, (j + 1) * self.cols)
-        gate, up = dot(u, s['w_split'][0, :, cols]).astype(BF16), dot(u, s['w_split'][1, :, cols]).astype(BF16)
+        gate, up = dot(u, s.w_split[0, :, cols]).astype(BF16), dot(u, s.w_split[1, :, cols]).astype(BF16)
         for n, p in enumerate(parts):
             for k in range(4):
                 rows = slice(n * lanes + k * shard, n * lanes + (k + 1) * shard)
-                s['z_part'][p, j, 2 * k * shard:(2 * k + 1) * shard] = gate[rows]
-                s['z_part'][p, j, (2 * k + 1) * shard:(2 * k + 2) * shard] = up[rows]
+                s.z_part[p, j, 2 * k * shard:(2 * k + 1) * shard] = gate[rows]
+                s.z_part[p, j, (2 * k + 1) * shard:(2 * k + 2) * shard] = up[rows]
             self.push_core(p, j)
 
     def push_core(self, p, j):
         s = self.s
-        half = s['z_recv'].shape[2]
-        self.z_core[p, j] = self.links.push(s['z_part'].at[p, j, pl.ds(0, half)], s['z_recv'].at[p, j], PARTNER, 'z')
+        half = s.z_recv.shape[2]
+        self.z_core[p, j] = self.links.push(s.z_part.at[p, j, pl.ds(0, half)], s.z_recv.at[p, j], PARTNER, 'z')
 
     def combine(self, p, j):
         s, unit = self.s, p * self.chunks + j
-        half = s['z_recv'].shape[2]
+        half = s.z_recv.shape[2]
         shard2 = half // 2
         self.z_core[p, j].wait_recv()
-        s['z_x'][unit] = (s['z_part'][p, j, half:half + shard2].astype(F32) + s['z_recv'][p, j, :shard2].astype(F32)).astype(BF16)
+        s.z_x[unit] = (s.z_part[p, j, half:half + shard2].astype(F32) + s.z_recv[p, j, :shard2].astype(F32)).astype(BF16)
         if unit < self.kept:
-            self.early[unit] = self.links.push(s['z_x'].at[unit], s['z_early'].at[unit], ACROSS, 'early')
+            self.early[unit] = self.links.push(s.z_x.at[unit], s.z_early.at[unit], ACROSS, 'early')
         else:
-            self.links.copy(s['z_x'].at[unit], self.zsend_out.at[unit - self.kept], 'z_x')
-        s['z_mine'][unit] = (s['z_part'][p, j, half + shard2:].astype(F32) + s['z_recv'][p, j, shard2:].astype(F32)).astype(BF16)
+            self.links.copy(s.z_x.at[unit], self.zsend_out.at[unit - self.kept], 'z_x')
+        s.z_mine[unit] = (s.z_part[p, j, half + shard2:].astype(F32) + s.z_recv[p, j, shard2:].astype(F32)).astype(BF16)
         if unit >= self.kept:
-            self.links.copy(s['z_mine'].at[unit], self.zmine_out.at[unit], 'z_mine')
+            self.links.copy(s.z_mine.at[unit], self.zmine_out.at[unit], 'z_mine')
 
     def take_early(self):
         s = self.s
         for unit in range(self.kept):
             self.early[unit].wait_recv()
-            s['z_mine'][unit] = (s['z_mine'][unit].astype(F32) + s['z_early'][unit].astype(F32)).astype(BF16)
-            self.links.copy(s['z_mine'].at[unit], self.zmine_out.at[unit], 'z_mine')
+            s.z_mine[unit] = (s.z_mine[unit].astype(F32) + s.z_early[unit].astype(F32)).astype(BF16)
+            self.links.copy(s.z_mine.at[unit], self.zmine_out.at[unit], 'z_mine')
         if self.carry:
-            shard = s['z_mine'].shape[1] // 2
+            shard = s.z_mine.shape[1] // 2
             for unit in range(self.carry):
-                s['m_early'][unit * shard:(unit + 1) * shard] = gated(s['z_mine'][unit])
-            self.links.copy(s['m_early'], self.zsend_out.at[s['z_x'].shape[0] - self.kept], 'm_early')
+                s.m_early[unit * shard:(unit + 1) * shard] = gated(s.z_mine[unit])
+            self.links.copy(s.m_early, self.zsend_out.at[s.z_x.shape[0] - self.kept], 'm_early')
 
     def sizes(self):
         s = self.s
-        return ({'a_core': s['a_core'], 'a_got': s['a_got'], 'z': s['z_recv'], 'early': s['z_early'],
-                 'sq': s['sq_recv'].at[:, pl.ds(0, len(EVERYONE))], 'h': s['h'].at[:, self.mine]},
-                {'z_x': s['z_x'].at[pl.ds(self.kept, s['z_x'].shape[0] - self.kept)], 'z_mine': s['z_mine'], 'qkv': s['a_full'], 'h': s['h'].at[:, self.mine], 'm_early': s.get('m_early')})
+        return (dict(a_core=s.a_core, a_got=s.a_got, z=s.z_recv, early=s.z_early,
+                 sq=s.sq_recv.at[:, pl.ds(0, len(EVERYONE))], h=s.h.at[:, self.mine]),
+                dict(z_x=s.z_x.at[pl.ds(self.kept, s.z_x.shape[0] - self.kept)], z_mine=s.z_mine, qkv=s.a_full, h=s.h.at[:, self.mine], m_early=getattr(s, 'm_early', None)))
 
 
 class Back:
     def __init__(self, links, layer, h_hbm, o_hbm, zgot_hbm, zmine_hbm, wd_hbm, wo_hbm, s):
         self.links, self.s = links, s
         self.kept, self.carry = EARLY[layer], CARRY[layer]
-        self.chunks, self.cols = s['m'].shape[1], s['m'].shape[3]
+        self.chunks, self.cols = s.m.shape[1], s.m.shape[3]
         units = PARTS * self.chunks
-        shard = s['m'].shape[2] // 4
+        shard = s.m.shape[2] // 4
         self.z = []
         for first, last in ((0, 1), (1, self.chunks), (self.chunks, units)):
             run = pl.ds(first, last - first)
-            self.z.append((first, links.copy(zmine_hbm.at[run], s['z_in'].at[run])))
+            self.z.append((first, links.copy(zmine_hbm.at[run], s.z_in.at[run])))
             start = max(first, self.kept)
             if start < last:
                 run = pl.ds(start - self.kept, last - start)
-                self.z.append((start, links.copy(zgot_hbm.at[run], s['z_got'].at[run])))
+                self.z.append((start, links.copy(zgot_hbm.at[run], s.z_got.at[run])))
             if first == 0:
                 self.carried = [links.copy(zgot_hbm.at[units - self.kept, pl.ds(j * shard, shard)], self.block(0, j, ACROSS))
                                 for j in range(self.carry)]
-                self.o_copy = links.copy(o_hbm, s['o_in'])
-                self.h_copy = links.copy(h_hbm, s['h_in'])
-        self.wd = links.copy(wd_hbm.at[layer], s['wd'])
-        self.wo = links.copy(wo_hbm.at[layer], s['wo'])
+                self.o_copy = links.copy(o_hbm, s.o_in)
+                self.h_copy = links.copy(h_hbm, s.h_in)
+        self.wd = links.copy(wd_hbm.at[layer], s.wd)
+        self.wo = links.copy(wo_hbm.at[layer], s.wo)
         self.wo_ready, self.wd_ready = False, False
         self.across, self.partner, self.diag = {}, {}, {}
         self.o_across, self.o_partner, self.o_diag = {}, {}, {}
@@ -271,21 +272,21 @@
         s, unit = self.s, p * self.chunks + j
         while self.z and self.z[0][0] <= unit:
             self.z.pop(0)[1].wait()
-        z = s['z_in'][unit]
+        z = s.z_in[unit]
         if unit >= self.kept:
-            z = (z.astype(F32) + s['z_got'][unit - self.kept].astype(F32)).astype(BF16)
-        s['m'][p, j, OWN * (z.shape[0] // 2):] = gated(z)
+            z = (z.astype(F32) + s.z_got[unit - self.kept].astype(F32)).astype(BF16)
+        s.m[p, j, OWN * (z.shape[0] // 2):] = gated(z)
 
     def block(self, p, j, k):
-        shard = self.s['m'].shape[2] // 4
-        return self.s['m'].at[p, j, pl.ds(k * shard, shard)]
+        shard = self.s.m.shape[2] // 4
+        return self.s.m.at[p, j, pl.ds(k * shard, shard)]
 
     def send(self, p, j):
         if p > 0 or j >= self.carry:
             self.across[p, j] = self.links.push(self.block(p, j, OWN), self.block(p, j, ACROSS), ACROSS, 'm_across')
 
     def send_partner(self, p):
-        m = self.s['m']
+        m = self.s.m
         shard = m.shape[2] // 4
         self.partner[p] = self.links.push(m.at[p, :, pl.ds(OWN * shard, shard)], m.at[p, :, pl.ds(PARTNER * shard, shard)], PARTNER, 'm')
 
@@ -299,20 +300,20 @@
     def send_o_yz(self):
         y, s = self.links.y, self.s
         self.o_copy.wait()
-        self.o_yz = self.links.push(s['o_in'].at[1 - y], s['o_yz'], YZ, 'o_yz')
+        self.o_yz = self.links.push(s.o_in.at[1 - y], s.o_yz, YZ, 'o_yz')
 
     def o_block(self, p, k):
-        shard = self.s['o'].shape[1] // 4
-        return self.s['o'].at[p, pl.ds(k * shard, shard)]
+        shard = self.s.o.shape[1] // 4
+        return self.s.o.at[p, pl.ds(k * shard, shard)]
 
     def send_o(self, p):
         y, s = self.links.y, self.s
         if p == 0:
             self.o_yz.wait_recv()
-        shard = s['o'].shape[1] // 4
+        shard = s.o.shape[1] // 4
         seqs = shard // 2
-        s['o'][p, pl.ds(OWN * shard + pl.multiple_of(y * seqs, seqs), seqs), :] = s['o_in'][y, p * seqs:(p + 1) * seqs]
-        s['o'][p, pl.ds(OWN * shard + pl.multiple_of((1 - y) * seqs, seqs), seqs), :] = s['o_yz'][p * seqs:(p + 1) * seqs]
+        s.o[p, pl.ds(OWN * shard + pl.multiple_of(y * seqs, seqs), seqs), :] = s.o_in[y, p * seqs:(p + 1) * seqs]
+        s.o[p, pl.ds(OWN * shard + pl.multiple_of((1 - y) * seqs, seqs), seqs), :] = s.o_yz[p * seqs:(p + 1) * seqs]
         self.o_across[p] = self.links.push(self.o_block(p, OWN), self.o_block(p, ACROSS), ACROSS, 'o')
         self.o_partner[p] = self.links.push(self.o_block(p, OWN), self.o_block(p, PARTNER), PARTNER, 'o')
 
@@ -327,7 +328,7 @@
         if not self.wo_ready:
             self.wo.wait()
             self.wo_ready = True
-        s['acc'][p] += dot(s['o'][p], s['wo'][...])
+        s.acc[p] += dot(s.o[p], s.wo[...])
 
     def down(self, p, j):
         s = self.s
@@ -337,35 +338,35 @@
         if not self.wd_ready:
             self.wd.wait()
             self.wd_ready = True
-        part = dot(s['m'][p, j], s['wd'][j * self.cols:(j + 1) * self.cols])
+        part = dot(s.m[p, j], s.wd[j * self.cols:(j + 1) * self.cols])
         if j == 0:
-            s['acc'][p] = part
+            s.acc[p] = part
         else:
-            s['acc'][p] += part
+            s.acc[p] += part
 
     def send_update(self, p):
         s, links = self.s, self.links
-        shard = s['acc'].shape[1] // 4
+        shard = s.acc.shape[1] // 4
         for k in range(4):
-            s['update'][p, pl.ds(pl.multiple_of(links.blocks[k] * shard, shard), shard), :] = s['acc'][p, k * shard:(k + 1) * shard, :]
-        s['up_part'][p] = s['update'][p].T.astype(BF16)
-        part = s['up_recv'].shape[1]
-        src = s['up_part'].at[p, pl.ds(pl.multiple_of((1 - links.y) * part, part), part)]
-        self.up[p] = links.push(src, s['up_recv'].at[p], YZ, 'up')
+            s.update[p, pl.ds(pl.multiple_of(links.blocks[k] * shard, shard), shard), :] = s.acc[p, k * shard:(k + 1) * shard, :]
+        s.up_part[p] = s.update[p].T.astype(BF16)
+        part = s.up_recv.shape[1]
+        src = s.up_part.at[p, pl.ds(pl.multiple_of((1 - links.y) * part, part), part)]
+        self.up[p] = links.push(src, s.up_recv.at[p], YZ, 'up')
 
     def new_h(self, p):
         s, links = self.s, self.links
         self.up[p].wait_recv()
-        part = s['up_recv'].shape[1]
-        own = s['up_part'][p, pl.ds(pl.multiple_of(links.y * part, part), part), :]
-        return (s['h_in'][p].astype(F32) + (own.astype(F32) + s['up_recv'][p].astype(F32))).astype(BF16)
+        part = s.up_recv.shape[1]
+        own = s.up_part[p, pl.ds(pl.multiple_of(links.y * part, part), part), :]
+        return (s.h_in[p].astype(F32) + (own.astype(F32) + s.up_recv[p].astype(F32))).astype(BF16)
 
     def sizes(self):
         s = self.s
-        sent = 3 * s['m'].shape[2] // 4
+        sent = 3 * s.m.shape[2] // 4
         shard = sent // 3
-        return {'m': s['m'].at[:, :, pl.ds(0, 2 * shard)],
-                'm_across': s['m'].at[:, pl.ds(0, self.chunks - self.carry // PARTS), pl.ds(0, shard)], 'o': s['o'].at[:, pl.ds(0, sent)], 'o_yz': s['o_yz'], 'up': s['up_recv']}
+        return dict(m=s.m.at[:, :, pl.ds(0, 2 * shard)],
+                m_across=s.m.at[:, pl.ds(0, self.chunks - self.carry // PARTS), pl.ds(0, shard)], o=s.o.at[:, pl.ds(0, sent)], o_yz=s.o_yz, up=s.up_recv)
 
     def open(self):
         links, chunks = self.links, self.chunks
@@ -389,15 +390,15 @@
 
 
 def start_kernel(names, model_dim, h_hbm, gain_hbm, wa_hbm, wm_hbm, qkv_out, zsend_out, zmine_out, h_out, *scratch):
-    s = dict(zip(names, scratch))
-    links = Links(s['send'], s['recv'], s['local'], EVERYONE)
-    h_copy = links.copy(h_hbm, s['h_in'])
+    s = types.SimpleNamespace(**dict(zip(names, scratch)))
+    links = Links(s.send, s.recv, s.local, EVERYONE)
+    h_copy = links.copy(h_hbm, s.h_in)
     f = Front(links, 0, gain_hbm, wa_hbm, wm_hbm, model_dim, (qkv_out, zsend_out, zmine_out, h_out), s)
     rows = h_hbm.shape[1]
     lanes = rows // PARTS
     order = part_order(rows, False)
     h_copy.wait()
-    own = dot(s['h_in'][...], order)
+    own = dot(s.h_in[...], order)
     for p in range(PARTS):
         f.squares(p, own[:, p * lanes:(p + 1) * lanes])
     f.constants()
@@ -426,8 +427,8 @@
 
 def middle_kernel(names, model_dim, h_hbm, o_hbm, gain_hbm, zmine_hbm, zgot_hbm, wd_hbm, wo_hbm, wa_hbm, wm_hbm, qkv_out, zsend_out,
                   zmine_out, h_out, *scratch):
-    s = dict(zip(names, scratch))
-    links = Links(s['send'], s['recv'], s['local'], EVERYONE)
+    s = types.SimpleNamespace(**dict(zip(names, scratch)))
+    links = Links(s.send, s.recv, s.local, EVERYONE)
     b = Back(links, 0, h_hbm, o_hbm, zgot_hbm, zmine_hbm, wd_hbm, wo_hbm, s)
     f = Front(links, 1, gain_hbm, wa_hbm, wm_hbm, model_dim, (qkv_out, zsend_out, zmine_out, h_out), s)
     b.open()
@@ -468,7 +469,7 @@
     f.combine(1, 4)
     f.attend_ends(1)
     sent, stored = f.sizes()
-    links.drain({**sent, **b.sizes()}, stored)
+    links.drain(dict(**sent, **b.sizes()), stored)
 
 
 def first_part(b, filler):
@@ -501,8 +502,8 @@
 
 
 def end_kernel(names, h_hbm, o_hbm, zmine_hbm, zgot_hbm, wd_hbm, wo_hbm, h_out, *scratch):
-    s = dict(zip(names, scratch))
-    links = Links(s['send'], s['recv'], s['local'], [PARTNER, ACROSS, YZ])
+    s = types.SimpleNamespace(**dict(zip(names, scratch)))
+    links = Links(s.send, s.recv, s.local, [PARTNER, ACROSS, YZ])
     b = Back(links, 1, h_hbm, o_hbm, zgot_hbm, zmine_hbm, wd_hbm, wo_hbm, s)
     b.open()
     first_part(b, None)
@@ -652,36 +653,36 @@
         num_seqs = PARTS * seqs
 
         def semaphores(groups, remote, local):
-            return {'send': pltpu.SemaphoreType.DMA((groups,)), 'recv': pltpu.SemaphoreType.DMA((remote,)),
-                    'local': pltpu.SemaphoreType.DMA((local,))}
+            return dict(send=pltpu.SemaphoreType.DMA((groups,)), recv=pltpu.SemaphoreType.DMA((remote,)),
+                    local=pltpu.SemaphoreType.DMA((local,)))
 
         def front_scratch(layer):
-            return {
-                'sq_send': pltpu.VMEM((PARTS, SQ_ROWS, lanes), F32), 'sq_recv': pltpu.VMEM((PARTS, 8, SQ_ROWS, lanes), F32),
-                'h': pltpu.VMEM((PARTS, depth, lanes), BF16), 'gain_in': pltpu.VMEM(norm_gain.shape, BF16), 'gain': pltpu.VMEM((depth, lanes), F32),
-                'u': pltpu.VMEM((PARTS, lanes, depth), BF16), 'u_rel': pltpu.VMEM((PARTS, lanes, depth), BF16),
-                'wa': pltpu.VMEM((depth, attn_cols), BF16), 'wm': pltpu.VMEM((depth, 2, mlp_cols), BF16),
-                'w_split': pltpu.VMEM((2, depth, mlp_cols), BF16),
-                'a_part': pltpu.VMEM((PARTS, lanes, attn_cols), BF16), 'a_core': pltpu.VMEM((PARTS, half, attn_cols), BF16),
-                'a_sum': pltpu.VMEM((PARTS, half, attn_cols), BF16), 'a_got': pltpu.VMEM((PARTS, 3, seqs, attn_cols), BF16),
-                'a_full': pltpu.VMEM((PARTS, 2, seqs, attn_cols), BF16),
-                'z_part': pltpu.VMEM((PARTS, CHUNKS, 2 * lanes, cols), BF16),
-                'z_recv': pltpu.VMEM((PARTS, CHUNKS, lanes, cols), BF16), 'z_x': pltpu.VMEM((units, half, cols), BF16),
-                'z_mine': pltpu.VMEM((units, half, cols), BF16), 'z_early': pltpu.VMEM((EARLY[layer], half, cols), BF16),
-            }
-
-        back_scratch = {
-            'o_yz': pltpu.VMEM((num_seqs, out_depth), BF16), 'o': pltpu.VMEM((PARTS, lanes, out_depth), BF16),
-            'm': pltpu.VMEM((PARTS, CHUNKS, lanes, cols), BF16), 'z_in': pltpu.VMEM((units, half, cols), BF16),
-            'o_in': pltpu.VMEM((2, num_seqs, out_depth), BF16),
-            'h_in': pltpu.VMEM((PARTS, part, lanes), BF16),
-            'wd': pltpu.VMEM((mlp_cols, depth), BF16), 'wo': pltpu.VMEM((out_depth, depth), BF16),
-            'acc': pltpu.VMEM((PARTS, lanes, depth), F32), 'update': pltpu.VMEM((PARTS, lanes, depth), F32),
-            'up_part': pltpu.VMEM((PARTS, depth, lanes), BF16), 'up_recv': pltpu.VMEM((PARTS, part, lanes), BF16),
-        }
+            return dict(
+                sq_send=pltpu.VMEM((PARTS, SQ_ROWS, lanes), F32), sq_recv=pltpu.VMEM((PARTS, 8, SQ_ROWS, lanes), F32),
+                h=pltpu.VMEM((PARTS, depth, lanes), BF16), gain_in=pltpu.VMEM(norm_gain.shape, BF16), gain=pltpu.VMEM((depth, lanes), F32),
+                u=pltpu.VMEM((PARTS, lanes, depth), BF16), u_rel=pltpu.VMEM((PARTS, lanes, depth), BF16),
+                wa=pltpu.VMEM((depth, attn_cols), BF16), wm=pltpu.VMEM((depth, 2, mlp_cols), BF16),
+                w_split=pltpu.VMEM((2, depth, mlp_cols), BF16),
+                a_part=pltpu.VMEM((PARTS, lanes, attn_cols), BF16), a_core=pltpu.VMEM((PARTS, half, attn_cols), BF16),
+                a_sum=pltpu.VMEM((PARTS, half, attn_cols), BF16), a_got=pltpu.VMEM((PARTS, 3, seqs, attn_cols), BF16),
+                a_full=pltpu.VMEM((PARTS, 2, seqs, attn_cols), BF16),
+                z_part=pltpu.VMEM((PARTS, CHUNKS, 2 * lanes, cols), BF16),
+                z_recv=pltpu.VMEM((PARTS, CHUNKS, lanes, cols), BF16), z_x=pltpu.VMEM((units, half, cols), BF16),
+                z_mine=pltpu.VMEM((units, half, cols), BF16), z_early=pltpu.VMEM((EARLY[layer], half, cols), BF16),
+            )
+
+        back_scratch = dict(
+            o_yz=pltpu.VMEM((num_seqs, out_depth), BF16), o=pltpu.VMEM((PARTS, lanes, out_depth), BF16),
+            m=pltpu.VMEM((PARTS, CHUNKS, lanes, cols), BF16), z_in=pltpu.VMEM((units, half, cols), BF16),
+            o_in=pltpu.VMEM((2, num_seqs, out_depth), BF16),
+            h_in=pltpu.VMEM((PARTS, part, lanes), BF16),
+            wd=pltpu.VMEM((mlp_cols, depth), BF16), wo=pltpu.VMEM((out_depth, depth), BF16),
+            acc=pltpu.VMEM((PARTS, lanes, depth), F32), update=pltpu.VMEM((PARTS, lanes, depth), F32),
+            up_part=pltpu.VMEM((PARTS, depth, lanes), BF16), up_recv=pltpu.VMEM((PARTS, part, lanes), BF16),
+        )
 
         def got_scratch(layer):
-            return {'z_got': pltpu.VMEM((units - EARLY[layer], half, cols), BF16)}
+            return dict(z_got=pltpu.VMEM((units - EARLY[layer], half, cols), BF16))
 
         def front_shapes(layer):
             return (
@@ -703,18 +704,18 @@
             middle_kernel(names, model_dim, *refs)
 
         qkv, zsend, zmine, h_block = call(
-            start, 'start', 0, {**semaphores(6, 34 + EARLY[0], 8), **front_scratch(0), 'h_in': pltpu.VMEM((part, rows), BF16)}, (HBM,) * 4,
+            start, 'start', 0, dict(**semaphores(6, 34 + EARLY[0], 8), **front_scratch(0), h_in=pltpu.VMEM((part, rows), BF16)), (HBM,) * 4,
             front_shapes(0), front_specs, hidden.T, norm_gain, w_attn, w_mlp)
         zgot = lax.ppermute(zsend, 'x', swap)
         k_new, v_new, o = attention(0, lengths, qkv, k_cache, v_cache, ())
         qkv, zsend, zmine, h_block = call(
-            middle, 'middle', 1, {**semaphores(11, 65 + EARLY[1], 17), **front_scratch(1), **back_scratch, **got_scratch(0),
-                       'm_early': pltpu.VMEM((half, cols), BF16)}, (HBM,) * 9,
+            middle, 'middle', 1, dict(**semaphores(11, 65 + EARLY[1], 17), **front_scratch(1), **back_scratch, **got_scratch(0),
+                       m_early=pltpu.VMEM((half, cols), BF16)), (HBM,) * 9,
             front_shapes(1), front_specs, h_block, o, norm_gain, zmine, zgot, w_down, w_out, w_attn, w_mlp)
         zgot = lax.ppermute(zsend, 'x', swap)
         k_new, v_new, o = attention(1, lengths, qkv, k_cache, v_cache, (k_new, v_new))
         h_out = call(
-            end_kernel, 'end', 2, {**semaphores(5, 29, 11), **back_scratch, **got_scratch(1)}, (HBM,) * 6,
+            end_kernel, 'end', 2, dict(**semaphores(5, 29, 11), **back_scratch, **got_scratch(1)), (HBM,) * 6,
             jax.ShapeDtypeStruct((part, rows), BF16), VMEM, h_block, o, zmine, zgot, w_down, w_out)
         return h_out.T, k_new, v_new
 

time: 122 us -> 122 us (level)
  no operation moved by 1% of the time
where the time goes in v9:
time: 122 us
  Pallas kernels  116 us (95%)
  waiting for transfers between devices  2.39 us (2%)
  starting transfers between devices  1.87 us (2%)
    pallas_call x3, Pallas kernels, call(): pl.pallas_call(functools.partial(kernel, tuple(scratch)), out_shape=out_s...  71.8 us
    pallas_call x2, Pallas kernels, attention(): pl.pallas_call(functools.partial(attention_kernel, layer, PER_COPY, PER_S...  44.3 us
  transfers between devices with their start and end apart: 2, of which 2 were waited for; matrix products, arithmetic and copies ran while one was open for 0% of the time, Pallas kernels for 36%

profile of v9, /device:TPU:0, one launch (start us, length us, event | category | flops | bytes accessed | tf_op | source)
XLA Modules:
  0.0 121.7 jit_solution(3184608081676912440)
XLA Ops:
  0.6 18.1 %start.1 = (bf16[2,32,1024]{2,1,0:T(8,128)(2,1)}, bf16[9,64,896]{2,1,0:T(8,128)(2,1)}, bf16[10,64,896]{2,1,0:T(8,128)(2,1)}, bf16[2,192,128]{2,1,0:T(8,128)(2,1)}) custom-call(bf16[192,256]{1,0:T(8,128)(2,1)} %bitcast.3, bf16[2,384]{1,0:T(2,128)(2,1)} %refs_2_.3, bf16[2,384,1024]{2,1,0:T(8,128)(2,1)} %refs_7_.1, bf16[2,384,2,4480]{3,2,1,0:T(2,128)(2,1)} %refs_8_.1), custom_call_target="tpu_custom_call" | custom-call | tf_op jit(solution)/shard_map/start/pallas_call | solution.py:694
  18.7 0.6 collective-permute-start
  19.3 22.2 %attention_0.1 = (bf16[2,32,2,1024,128]{4,3,2,1,0:T(8,128)(2,1)}, bf16[2,32,2,1024,128]{4,3,2,1,0:T(8,128)(2,1)}, bf16[2,32,768]{2,1,0:T(8,128)(2,1)}) custom-call(s32[32]{0:T(128)} %len_hbm.3, bf16[2,32,1024]{2,1,0:T(8,128)(2,1)} %get-tuple-element.18.qkv_hbm, bf16[2,32,2,1024,128]{4,3,2,1,0:T(8,128)(2,1)} %k_hbm.3, bf16[2,32,2,1024,128]{4,3,2,1,0:T(8,128)(2,1)} %v_hbm.3), custom_call_target="tpu_custom_call" | custom-call | flops 10000000000 | bytes 67108864 | tf_op jit(solution)/shard_map/attention_0/pallas_call | solution.py:616
  41.5 1.6 %collective-permute-done.refs_4_ = bf16[9,64,896]{2,1,0:T(8,128)(2,1)} collective-permute-done((bf16[9,64,896]{2,1,0:T(8,128)(2,1)}, bf16[9,64,896]{2,1,0:T(8,128)(2,1)}, u32[]{:S(2)}, u32[]{:S(2)}) %collective-permute-start) | collective-permute-done | bytes 1032224 | tf_op jit(solution)/shard_map/ppermute | solution.py:709
  43.1 33.1 %middle.1 = (bf16[2,32,1024]{2,1,0:T(8,128)(2,1)}, bf16[9,64,896]{2,1,0:T(8,128)(2,1)}, bf16[10,64,896]{2,1,0:T(8,128)(2,1)}, bf16[2,192,128]{2,1,0:T(8,128)(2,1)}) custom-call(bf16[2,192,128]{2,1,0:T(8,128)(2,1)} %get-tuple-element.17.refs_0_, bf16[2,32,768]{2,1,0:T(8,128)(2,1)} %get-tuple-element.19.refs_1_, bf16[2,384]{1,0:T(2,128)(2,1)} %refs_2_.3, ...), custom_call_target="tpu_custom_call" | custom-call | tf_op jit(solution)/shard_map/middle/pallas_call | solution.py:694
  76.2 1.2 %collective-permute-start.1 = (bf16[9,64,896]{2,1,0:T(8,128)(2,1)}, bf16[9,64,896]{2,1,0:T(8,128)(2,1)}, u32[]{:S(2)}, u32[]{:S(2)}) collective-permute-start(bf16[9,64,896]{2,1,0:T(8,128)(2,1)} %get-tuple-element.28), channel_id=1, source_target_pairs={{0,2},{2,0},{1,3},{3,1},{4,6},{6,4},{5,7},{7,5}} | collective-permute-start | bytes 3096584 | tf_op jit(solution)/shard_map/ppermute | solution.py:715
  77.4 22.2 %attention_1.1 = (bf16[2,32,2,1024,128]{4,3,2,1,0:T(8,128)(2,1)}, bf16[2,32,2,1024,128]{4,3,2,1,0:T(8,128)(2,1)}, bf16[2,32,768]{2,1,0:T(8,128)(2,1)}) custom-call(s32[32]{0:T(128)} %len_hbm.3, bf16[2,32,1024]{2,1,0:T(8,128)(2,1)} %get-tuple-element.23.qkv_hbm, bf16[2,32,2,1024,128]{4,3,2,1,0:T(8,128)(2,1)} %k_hbm.3, ...), custom_call_target="tpu_custom_call", output_to_operand_aliasing={{0}: (4, {}), {1}: (5, {})} | custom-call | flops 10000000000 | bytes 67108864 | tf_op jit(solution)/shard_map/attention_1/pallas_call | solution.py:616
  99.6 0.8 collective-permute-done.1.zgot_hbm
  100.4 20.6 %end.1 = bf16[192,256]{1,0:T(8,128)(2,1)S(1)} custom-call(bf16[2,192,128]{2,1,0:T(8,128)(2,1)} %get-tuple-element.22.h_hbm, bf16[2,32,768]{2,1,0:T(8,128)(2,1)} %get-tuple-element.26.o_hbm, bf16[10,64,896]{2,1,0:T(8,128)(2,1)} %get-tuple-element.27.zmine_hbm, bf16[9,64,896]{2,1,0:T(8,128)(2,1)} %collective-permute-done.1.zgot_hbm, ...), custom_call_target="tpu_custom_call" | custom-call | tf_op jit(solution)/shard_map/end/pallas_call | solution.py:694
  121.0 0.6 copy.17
Async XLA Ops:
  18.7 24.4 %collective-permute-start = (bf16[9,64,896]{2,1,0:T(8,128)(2,1)}, bf16[9,64,896]{2,1,0:T(8,128)(2,1)}, u32[]{:S(2)}, u32[]{:S(2)}) collective-permute-start(bf16[9,64,896]{2,1,0:T(8,128)(2,1)} %get-tuple-element.21), channel_id=1, source_target_pairs={{0,2},{2,0},{1,3},{3,1},{4,6},{6,4},{5,7},{7,5}} | collective-permute-start | bytes 3096584 | tf_op jit(solution)/shard_map/ppermute | solution.py:709
  76.2 24.2 %collective-permute-start.1 = (bf16[9,64,896]{2,1,0:T(8,128)(2,1)}, bf16[9,64,896]{2,1,0:T(8,128)(2,1)}, u32[]{:S(2)}, u32[]{:S(2)}) collective-permute-start(bf16[9,64,896]{2,1,0:T(8,128)(2,1)} %get-tuple-element.28), channel_id=1, source_target_pairs={{0,2},{2,0},{1,3},{3,1},{4,6},{6,4},{5,7},{7,5}} | collective-permute-start | bytes 3096584 | tf_op jit(solution)/shard_map/ppermute | solution.py:715

commit v10 on v9

--- a/solution.py
+++ b/solution.py
@@ -377,7 +377,7 @@
         for j in range(1, chunks):
             self.mix(0, j)
             self.send(0, j)
-            if j == 2:
+            if j == 2 + self.carry:
                 self.send_o(0)
         self.send_partner(0)
         for j in range(chunks):
@@ -477,7 +477,7 @@
         b.forward(0, j)
         if filler is not None:
             filler(j)
-        if j == 2:
+        if j == 2 + b.carry:
             b.forward_o(0)
         if j >= 1:
             b.down(0, j - 1)

time: 122 us -> 121 us (level)
  transfers between devices with their start and end apart: 2 -> 2, of which waited for: 2 -> 2; matrix products, arithmetic and copies ran while one was open for 0% -> 0% of each run, Pallas kernels for 36% -> 37%
where the time goes in v10:
time: 121 us
  Pallas kernels  115 us (95%)
  waiting for transfers between devices  2.39 us (2%)
  starting transfers between devices  1.87 us (2%)
    pallas_call x3, Pallas kernels, call(): pl.pallas_call(functools.partial(kernel, tuple(scratch)), out_shape=out_s...  70.9 us
    pallas_call x2, Pallas kernels, attention(): pl.pallas_call(functools.partial(attention_kernel, layer, PER_COPY, PER_S...  44.3 us
  transfers between devices with their start and end apart: 2, of which 2 were waited for; matrix products, arithmetic and copies ran while one was open for 0% of the time, Pallas kernels for 37%

profile of v10, /device:TPU:0, one launch (start us, length us, event | category | flops | bytes accessed | tf_op | source)
XLA Modules:
  0.0 120.8 jit_solution(2108739446440474650)
XLA Ops:
  0.6 18.1 %start.1 = (bf16[2,32,1024]{2,1,0:T(8,128)(2,1)}, bf16[9,64,896]{2,1,0:T(8,128)(2,1)}, bf16[10,64,896]{2,1,0:T(8,128)(2,1)}, bf16[2,192,128]{2,1,0:T(8,128)(2,1)}) custom-call(bf16[192,256]{1,0:T(8,128)(2,1)} %bitcast.3, bf16[2,384]{1,0:T(2,128)(2,1)} %refs_2_.3, bf16[2,384,1024]{2,1,0:T(8,128)(2,1)} %refs_7_.1, bf16[2,384,2,4480]{3,2,1,0:T(2,128)(2,1)} %refs_8_.1), custom_call_target="tpu_custom_call" | custom-call | tf_op jit(solution)/shard_map/start/pallas_call | solution.py:694
  18.7 0.6 collective-permute-start
  19.3 22.2 %attention_0.1 = (bf16[2,32,2,1024,128]{4,3,2,1,0:T(8,128)(2,1)}, bf16[2,32,2,1024,128]{4,3,2,1,0:T(8,128)(2,1)}, bf16[2,32,768]{2,1,0:T(8,128)(2,1)}) custom-call(s32[32]{0:T(128)} %len_hbm.3, bf16[2,32,1024]{2,1,0:T(8,128)(2,1)} %get-tuple-element.18.qkv_hbm, bf16[2,32,2,1024,128]{4,3,2,1,0:T(8,128)(2,1)} %k_hbm.3, bf16[2,32,2,1024,128]{4,3,2,1,0:T(8,128)(2,1)} %v_hbm.3), custom_call_target="tpu_custom_call" | custom-call | flops 10000000000 | bytes 67108864 | tf_op jit(solution)/shard_map/attention_0/pallas_call | solution.py:616
  41.5 1.6 %collective-permute-done.refs_4_ = bf16[9,64,896]{2,1,0:T(8,128)(2,1)} collective-permute-done((bf16[9,64,896]{2,1,0:T(8,128)(2,1)}, bf16[9,64,896]{2,1,0:T(8,128)(2,1)}, u32[]{:S(2)}, u32[]{:S(2)}) %collective-permute-start) | collective-permute-done | bytes 1032224 | tf_op jit(solution)/shard_map/ppermute | solution.py:709
  43.1 33.1 %middle.1 = (bf16[2,32,1024]{2,1,0:T(8,128)(2,1)}, bf16[9,64,896]{2,1,0:T(8,128)(2,1)}, bf16[10,64,896]{2,1,0:T(8,128)(2,1)}, bf16[2,192,128]{2,1,0:T(8,128)(2,1)}) custom-call(bf16[2,192,128]{2,1,0:T(8,128)(2,1)} %get-tuple-element.17.refs_0_, bf16[2,32,768]{2,1,0:T(8,128)(2,1)} %get-tuple-element.19.refs_1_, bf16[2,384]{1,0:T(2,128)(2,1)} %refs_2_.3, ...), custom_call_target="tpu_custom_call" | custom-call | tf_op jit(solution)/shard_map/middle/pallas_call | solution.py:694
  76.2 1.2 %collective-permute-start.1 = (bf16[9,64,896]{2,1,0:T(8,128)(2,1)}, bf16[9,64,896]{2,1,0:T(8,128)(2,1)}, u32[]{:S(2)}, u32[]{:S(2)}) collective-permute-start(bf16[9,64,896]{2,1,0:T(8,128)(2,1)} %get-tuple-element.28), channel_id=1, source_target_pairs={{0,2},{2,0},{1,3},{3,1},{4,6},{6,4},{5,7},{7,5}} | collective-permute-start | bytes 3096584 | tf_op jit(solution)/shard_map/ppermute | solution.py:715
  77.4 22.2 %attention_1.1 = (bf16[2,32,2,1024,128]{4,3,2,1,0:T(8,128)(2,1)}, bf16[2,32,2,1024,128]{4,3,2,1,0:T(8,128)(2,1)}, bf16[2,32,768]{2,1,0:T(8,128)(2,1)}) custom-call(s32[32]{0:T(128)} %len_hbm.3, bf16[2,32,1024]{2,1,0:T(8,128)(2,1)} %get-tuple-element.23.qkv_hbm, bf16[2,32,2,1024,128]{4,3,2,1,0:T(8,128)(2,1)} %k_hbm.3, ...), custom_call_target="tpu_custom_call", output_to_operand_aliasing={{0}: (4, {}), {1}: (5, {})} | custom-call | flops 10000000000 | bytes 67108864 | tf_op jit(solution)/shard_map/attention_1/pallas_call | solution.py:616
  99.6 0.8 collective-permute-done.1.zgot_hbm
  100.4 19.7 %end.1 = bf16[192,256]{1,0:T(8,128)(2,1)S(1)} custom-call(bf16[2,192,128]{2,1,0:T(8,128)(2,1)} %get-tuple-element.22.h_hbm, bf16[2,32,768]{2,1,0:T(8,128)(2,1)} %get-tuple-element.26.o_hbm, bf16[10,64,896]{2,1,0:T(8,128)(2,1)} %get-tuple-element.27.zmine_hbm, bf16[9,64,896]{2,1,0:T(8,128)(2,1)} %collective-permute-done.1.zgot_hbm, ...), custom_call_target="tpu_custom_call" | custom-call | tf_op jit(solution)/shard_map/end/pallas_call | solution.py:694
  120.2 0.6 copy.17
Async XLA Ops:
  18.7 24.4 %collective-permute-start = (bf16[9,64,896]{2,1,0:T(8,128)(2,1)}, bf16[9,64,896]{2,1,0:T(8,128)(2,1)}, u32[]{:S(2)}, u32[]{:S(2)}) collective-permute-start(bf16[9,64,896]{2,1,0:T(8,128)(2,1)} %get-tuple-element.21), channel_id=1, source_target_pairs={{0,2},{2,0},{1,3},{3,1},{4,6},{6,4},{5,7},{7,5}} | collective-permute-start | bytes 3096584 | tf_op jit(solution)/shard_map/ppermute | solution.py:709
  76.2 24.2 %collective-permute-start.1 = (bf16[9,64,896]{2,1,0:T(8,128)(2,1)}, bf16[9,64,896]{2,1,0:T(8,128)(2,1)}, u32[]{:S(2)}, u32[]{:S(2)}) collective-permute-start(bf16[9,64,896]{2,1,0:T(8,128)(2,1)} %get-tuple-element.28), channel_id=1, source_target_pairs={{0,2},{2,0},{1,3},{3,1},{4,6},{6,4},{5,7},{7,5}} | collective-permute-start | bytes 3096584 | tf_op jit(solution)/shard_map/ppermute | solution.py:715

commit v11 on v10

--- a/solution.py
+++ b/solution.py
@@ -46,9 +46,15 @@
     def meet(self):
         pl.semaphore_wait(self.barrier, len(self.peers))
 
-    def push(self, src, dst, to, group):
-        k = self.used
+    def slot(self):
         self.used += 1
+        return self.used - 1
+
+    def take(self, k, got):
+        pltpu.make_async_copy(got, got, self.recv_sems.at[k]).wait()
+
+    def push(self, src, dst, to, group, k=None):
+        k = self.slot() if k is None else k
         g = self.groups.setdefault(group, len(self.groups))
         copy = pltpu.make_async_remote_copy(
             src_ref=src, dst_ref=dst, send_sem=self.send_sems.at[g], recv_sem=self.recv_sems.at[k],
@@ -126,14 +132,15 @@
 
     def send_h(self, p):
         s, links = self.s, self.links
-        self.sq[p] = [links.push(s.sq_send.at[p], s.sq_recv.at[p, k], k, 'sq') for k in EVERYONE]
+        self.sq[p] = links.slot()
+        for k in EVERYONE:
+            links.push(s.sq_send.at[p], s.sq_recv.at[p, k], k, 'sq', self.sq[p])
         self.h_yz[p] = links.push(s.h.at[p, self.mine], s.h.at[p, self.mine], YZ, 'h')
         links.copy(s.h.at[p, self.mine], self.h_out.at[p], 'h')
 
     def normalize(self, p):
         s, links = self.s, self.links
-        for c in self.sq[p]:
-            c.wait_recv()
+        links.take(self.sq[p], s.sq_recv.at[p, pl.ds(0, len(EVERYONE))])
         total = s.sq_send[p]
         for k in EVERYONE:
             total = total + s.sq_recv[p, k]
@@ -158,16 +165,15 @@
         shard, seqs = half // 2, s.a_got.shape[2]
         y = self.links.y
         here, there = pl.multiple_of(y * seqs, seqs), pl.multiple_of((1 - y) * seqs, seqs)
-        self.a_got[p] = [
-            self.links.push(s.a_sum.at[p, pl.ds(there, seqs)], s.a_got.at[p, 2], ACROSS_YZ, 'a_got'),
-            self.links.push(s.a_sum.at[p, pl.ds(here, seqs)], s.a_got.at[p, 0], ACROSS, 'a_got'),
-            self.links.push(s.a_sum.at[p, pl.ds(shard + there, seqs)], s.a_got.at[p, 1], YZ, 'a_got')]
+        k = self.a_got[p] = self.links.slot()
+        self.links.push(s.a_sum.at[p, pl.ds(there, seqs)], s.a_got.at[p, 2], ACROSS_YZ, 'a_got', k)
+        self.links.push(s.a_sum.at[p, pl.ds(here, seqs)], s.a_got.at[p, 0], ACROSS, 'a_got', k)
+        self.links.push(s.a_sum.at[p, pl.ds(shard + there, seqs)], s.a_got.at[p, 1], YZ, 'a_got', k)
 
     def attend_ends(self, p):
         s, y = self.s, self.links.y
         shard, seqs = s.a_sum.shape[1] // 2, s.a_got.shape[2]
-        for c in self.a_got[p]:
-            c.wait_recv()
+        self.links.take(self.a_got[p], s.a_got.at[p])
         own = s.a_sum[p, pl.ds(shard + pl.multiple_of(y * seqs, seqs), seqs), :]
         s.a_full[p, 0] = (own.astype(F32) + s.a_got[p, 0].astype(F32)).astype(BF16)
         s.a_full[p, 1] = (s.a_got[p, 1].astype(F32) + s.a_got[p, 2].astype(F32)).astype(BF16)
@@ -370,11 +376,13 @@
 
     def open(self):
         links, chunks = self.links, self.chunks
-        self.mix(0, 0)
+        for j in range(self.carry + 1):
+            self.mix(0, j)
         links.meet()
-        self.send(0, 0)
+        for j in range(self.carry + 1):
+            self.send(0, j)
         self.send_o_yz()
-        for j in range(1, chunks):
+        for j in range(self.carry + 1, chunks):
             self.mix(0, j)
             self.send(0, j)
             if j == 2 + self.carry:
@@ -704,12 +712,12 @@
             middle_kernel(names, model_dim, *refs)
 
         qkv, zsend, zmine, h_block = call(
-            start, 'start', 0, dict(**semaphores(6, 34 + EARLY[0], 8), **front_scratch(0), h_in=pltpu.VMEM((part, rows), BF16)), (HBM,) * 4,
+            start, 'start', 0, dict(**semaphores(6, 18 + EARLY[0], 8), **front_scratch(0), h_in=pltpu.VMEM((part, rows), BF16)), (HBM,) * 4,
             front_shapes(0), front_specs, hidden.T, norm_gain, w_attn, w_mlp)
         zgot = lax.ppermute(zsend, 'x', swap)
         k_new, v_new, o = attention(0, lengths, qkv, k_cache, v_cache, ())
         qkv, zsend, zmine, h_block = call(
-            middle, 'middle', 1, dict(**semaphores(11, 65 + EARLY[1], 17), **front_scratch(1), **back_scratch, **got_scratch(0),
+            middle, 'middle', 1, dict(**semaphores(11, 49 + EARLY[1], 17), **front_scratch(1), **back_scratch, **got_scratch(0),
                        m_early=pltpu.VMEM((half, cols), BF16)), (HBM,) * 9,
             front_shapes(1), front_specs, h_block, o, norm_gain, zmine, zgot, w_down, w_out, w_attn, w_mlp)
         zgot = lax.ppermute(zsend, 'x', swap)

time: 121 us -> 121 us (level)
  no operation moved by 1% of the time
where the time goes in v11:
time: 121 us; the launch traced here: 120 us
  Pallas kernels  115 us (95%)
  waiting for transfers between devices  2.4 us (2%)
  starting transfers between devices  1.87 us (2%)
    pallas_call x3, Pallas kernels, call(): pl.pallas_call(functools.partial(kernel, tuple(scratch)), out_shape=out_s...  70.5 us
    pallas_call x2, Pallas kernels, attention(): pl.pallas_call(functools.partial(attention_kernel, layer, PER_COPY, PER_S...  44.3 us
  transfers between devices with their start and end apart: 2, of which 2 were waited for; matrix products, arithmetic and copies ran while one was open for 0% of the time, Pallas kernels for 37%

profile of v11, /device:TPU:0, one launch (start us, length us, event | category | flops | bytes accessed | tf_op | source)
XLA Modules:
  0.0 120.4 jit_solution(943333768642527674)
XLA Ops:
  0.6 17.9 %start.1 = (bf16[2,32,1024]{2,1,0:T(8,128)(2,1)}, bf16[9,64,896]{2,1,0:T(8,128)(2,1)}, bf16[10,64,896]{2,1,0:T(8,128)(2,1)}, bf16[2,192,128]{2,1,0:T(8,128)(2,1)}) custom-call(bf16[192,256]{1,0:T(8,128)(2,1)} %bitcast.3, bf16[2,384]{1,0:T(2,128)(2,1)} %refs_2_.3, bf16[2,384,1024]{2,1,0:T(8,128)(2,1)} %refs_7_.1, bf16[2,384,2,4480]{3,2,1,0:T(2,128)(2,1)} %refs_8_.1), custom_call_target="tpu_custom_call" | custom-call | tf_op jit(solution)/shard_map/start/pallas_call | solution.py:702
  18.6 0.6 collective-permute-start
  19.2 22.2 %attention_0.1 = (bf16[2,32,2,1024,128]{4,3,2,1,0:T(8,128)(2,1)}, bf16[2,32,2,1024,128]{4,3,2,1,0:T(8,128)(2,1)}, bf16[2,32,768]{2,1,0:T(8,128)(2,1)}) custom-call(s32[32]{0:T(128)} %len_hbm.3, bf16[2,32,1024]{2,1,0:T(8,128)(2,1)} %get-tuple-element.18.qkv_hbm, bf16[2,32,2,1024,128]{4,3,2,1,0:T(8,128)(2,1)} %k_hbm.3, bf16[2,32,2,1024,128]{4,3,2,1,0:T(8,128)(2,1)} %v_hbm.3), custom_call_target="tpu_custom_call" | custom-call | flops 10000000000 | bytes 67108864 | tf_op jit(solution)/shard_map/attention_0/pallas_call | solution.py:624
  41.4 1.6 %collective-permute-done.refs_4_ = bf16[9,64,896]{2,1,0:T(8,128)(2,1)} collective-permute-done((bf16[9,64,896]{2,1,0:T(8,128)(2,1)}, bf16[9,64,896]{2,1,0:T(8,128)(2,1)}, u32[]{:S(2)}, u32[]{:S(2)}) %collective-permute-start) | collective-permute-done | bytes 1032224 | tf_op jit(solution)/shard_map/ppermute | solution.py:717
  42.9 32.9 %middle.1 = (bf16[2,32,1024]{2,1,0:T(8,128)(2,1)}, bf16[9,64,896]{2,1,0:T(8,128)(2,1)}, bf16[10,64,896]{2,1,0:T(8,128)(2,1)}, bf16[2,192,128]{2,1,0:T(8,128)(2,1)}) custom-call(bf16[2,192,128]{2,1,0:T(8,128)(2,1)} %get-tuple-element.17.refs_0_, bf16[2,32,768]{2,1,0:T(8,128)(2,1)} %get-tuple-element.19.refs_1_, bf16[2,384]{1,0:T(2,128)(2,1)} %refs_2_.3, ...), custom_call_target="tpu_custom_call" | custom-call | tf_op jit(solution)/shard_map/middle/pallas_call | solution.py:702
  75.9 1.2 %collective-permute-start.1 = (bf16[9,64,896]{2,1,0:T(8,128)(2,1)}, bf16[9,64,896]{2,1,0:T(8,128)(2,1)}, u32[]{:S(2)}, u32[]{:S(2)}) collective-permute-start(bf16[9,64,896]{2,1,0:T(8,128)(2,1)} %get-tuple-element.28), channel_id=1, source_target_pairs={{0,2},{2,0},{1,3},{3,1},{4,6},{6,4},{5,7},{7,5}} | collective-permute-start | bytes 3096584 | tf_op jit(solution)/shard_map/ppermute | solution.py:723
  77.1 22.2 %attention_1.1 = (bf16[2,32,2,1024,128]{4,3,2,1,0:T(8,128)(2,1)}, bf16[2,32,2,1024,128]{4,3,2,1,0:T(8,128)(2,1)}, bf16[2,32,768]{2,1,0:T(8,128)(2,1)}) custom-call(s32[32]{0:T(128)} %len_hbm.3, bf16[2,32,1024]{2,1,0:T(8,128)(2,1)} %get-tuple-element.23.qkv_hbm, bf16[2,32,2,1024,128]{4,3,2,1,0:T(8,128)(2,1)} %k_hbm.3, ...), custom_call_target="tpu_custom_call", output_to_operand_aliasing={{0}: (4, {}), {1}: (5, {})} | custom-call | flops 10000000000 | bytes 67108864 | tf_op jit(solution)/shard_map/attention_1/pallas_call | solution.py:624
  99.3 0.8 collective-permute-done.1.zgot_hbm
  100.1 19.6 %end.1 = bf16[192,256]{1,0:T(8,128)(2,1)S(1)} custom-call(bf16[2,192,128]{2,1,0:T(8,128)(2,1)} %get-tuple-element.22.h_hbm, bf16[2,32,768]{2,1,0:T(8,128)(2,1)} %get-tuple-element.26.o_hbm, bf16[10,64,896]{2,1,0:T(8,128)(2,1)} %get-tuple-element.27.zmine_hbm, bf16[9,64,896]{2,1,0:T(8,128)(2,1)} %collective-permute-done.1.zgot_hbm, ...), custom_call_target="tpu_custom_call" | custom-call | tf_op jit(solution)/shard_map/end/pallas_call | solution.py:702
  119.8 0.6 copy.17
Async XLA Ops:
  18.6 24.4 %collective-permute-start = (bf16[9,64,896]{2,1,0:T(8,128)(2,1)}, bf16[9,64,896]{2,1,0:T(8,128)(2,1)}, u32[]{:S(2)}, u32[]{:S(2)}) collective-permute-start(bf16[9,64,896]{2,1,0:T(8,128)(2,1)} %get-tuple-element.21), channel_id=1, source_target_pairs={{0,2},{2,0},{1,3},{3,1},{4,6},{6,4},{5,7},{7,5}} | collective-permute-start | bytes 3096584 | tf_op jit(solution)/shard_map/ppermute | solution.py:717
  75.9 24.2 %collective-permute-start.1 = (bf16[9,64,896]{2,1,0:T(8,128)(2,1)}, bf16[9,64,896]{2,1,0:T(8,128)(2,1)}, u32[]{:S(2)}, u32[]{:S(2)}) collective-permute-start(bf16[9,64,896]{2,1,0:T(8,128)(2,1)} %get-tuple-element.28), channel_id=1, source_target_pairs={{0,2},{2,0},{1,3},{3,1},{4,6},{6,4},{5,7},{7,5}} | collective-permute-start | bytes 3096584 | tf_op jit(solution)/shard_map/ppermute | solution.py:723

commit v12 on v11

--- a/solution.py
+++ b/solution.py
@@ -271,7 +271,7 @@
         self.wo = links.copy(wo_hbm.at[layer], s.wo)
         self.wo_ready, self.wd_ready = False, False
         self.across, self.partner, self.diag = {}, {}, {}
-        self.o_across, self.o_partner, self.o_diag = {}, {}, {}
+        self.o_across, self.o_core = {}, {}
         self.up = {}
 
     def mix(self, p, j):
@@ -321,16 +321,16 @@
         s.o[p, pl.ds(OWN * shard + pl.multiple_of(y * seqs, seqs), seqs), :] = s.o_in[y, p * seqs:(p + 1) * seqs]
         s.o[p, pl.ds(OWN * shard + pl.multiple_of((1 - y) * seqs, seqs), seqs), :] = s.o_yz[p * seqs:(p + 1) * seqs]
         self.o_across[p] = self.links.push(self.o_block(p, OWN), self.o_block(p, ACROSS), ACROSS, 'o')
-        self.o_partner[p] = self.links.push(self.o_block(p, OWN), self.o_block(p, PARTNER), PARTNER, 'o')
+        self.o_core[p] = self.links.slot()
+        self.links.push(self.o_block(p, OWN), self.o_block(p, PARTNER), PARTNER, 'o', self.o_core[p])
 
     def forward_o(self, p):
         self.o_across[p].wait_recv()
-        self.o_diag[p] = self.links.push(self.o_block(p, ACROSS), self.o_block(p, DIAG), PARTNER, 'o')
+        self.links.push(self.o_block(p, ACROSS), self.o_block(p, DIAG), PARTNER, 'o', self.o_core[p])
 
     def project_o(self, p):
         s = self.s
-        self.o_partner[p].wait_recv()
-        self.o_diag[p].wait_recv()
+        self.links.take(self.o_core[p], s.o.at[p, pl.ds(0, s.o.shape[1] // 2)])
         if not self.wo_ready:
             self.wo.wait()
             self.wo_ready = True
@@ -463,8 +463,8 @@
     f.normalize(1)
     f.project([1], 0)
     f.combine(0, 4)
+    f.attend_core(1)
     f.project([1], 1)
-    f.attend_core(1)
     f.attend_ends(0)
     f.project([1], 2)
     f.combine(1, 0)
@@ -717,13 +717,13 @@
         zgot = lax.ppermute(zsend, 'x', swap)
         k_new, v_new, o = attention(0, lengths, qkv, k_cache, v_cache, ())
         qkv, zsend, zmine, h_block = call(
-            middle, 'middle', 1, dict(**semaphores(11, 49 + EARLY[1], 17), **front_scratch(1), **back_scratch, **got_scratch(0),
+            middle, 'middle', 1, dict(**semaphores(11, 47 + EARLY[1], 17), **front_scratch(1), **back_scratch, **got_scratch(0),
                        m_early=pltpu.VMEM((half, cols), BF16)), (HBM,) * 9,
             front_shapes(1), front_specs, h_block, o, norm_gain, zmine, zgot, w_down, w_out, w_attn, w_mlp)
         zgot = lax.ppermute(zsend, 'x', swap)
         k_new, v_new, o = attention(1, lengths, qkv, k_cache, v_cache, (k_new, v_new))
         h_out = call(
-            end_kernel, 'end', 2, dict(**semaphores(5, 29, 11), **back_scratch, **got_scratch(1)), (HBM,) * 6,
+            end_kernel, 'end', 2, dict(**semaphores(5, 27, 11), **back_scratch, **got_scratch(1)), (HBM,) * 6,
             jax.ShapeDtypeStruct((part, rows), BF16), VMEM, h_block, o, zmine, zgot, w_down, w_out)
         return h_out.T, k_new, v_new
 

time: 121 us -> 120 us (level)
  no operation moved by 1% of the time
where the time goes in v12:
time: 120 us
  Pallas kernels  114 us (95%)
  waiting for transfers between devices  2.75 us (2%)
  starting transfers between devices  1.87 us (2%)
    pallas_call x3, Pallas kernels, call(): pl.pallas_call(functools.partial(kernel, tuple(scratch)), out_shape=out_s...  70.1 us
    pallas_call x2, Pallas kernels, attention(): pl.pallas_call(functools.partial(attention_kernel, layer, PER_COPY, PER_S...  44.3 us
    ppermute x2, waiting for transfers between devices, device_step(): zgot = lax.ppermute(zsend, 'x', swap)  2.75 us
  transfers between devices with their start and end apart: 2, of which 2 were waited for; matrix products, arithmetic and copies ran while one was open for 0% of the time, Pallas kernels for 37%

profile of v12, /device:TPU:0, one launch (start us, length us, event | category | flops | bytes accessed | tf_op | source)
XLA Modules:
  0.0 120.4 jit_solution(6355030148689212734)
XLA Ops:
  0.6 17.9 %start.1 = (bf16[2,32,1024]{2,1,0:T(8,128)(2,1)}, bf16[9,64,896]{2,1,0:T(8,128)(2,1)}, bf16[10,64,896]{2,1,0:T(8,128)(2,1)}, bf16[2,192,128]{2,1,0:T(8,128)(2,1)}) custom-call(bf16[192,256]{1,0:T(8,128)(2,1)} %bitcast.3, bf16[2,384]{1,0:T(2,128)(2,1)} %refs_2_.3, bf16[2,384,1024]{2,1,0:T(8,128)(2,1)} %refs_7_.1, bf16[2,384,2,4480]{3,2,1,0:T(2,128)(2,1)} %refs_8_.1), custom_call_target="tpu_custom_call" | custom-call | tf_op jit(solution)/shard_map/start/pallas_call | solution.py:702
  18.6 0.6 collective-permute-start
  19.2 22.2 %attention_0.1 = (bf16[2,32,2,1024,128]{4,3,2,1,0:T(8,128)(2,1)}, bf16[2,32,2,1024,128]{4,3,2,1,0:T(8,128)(2,1)}, bf16[2,32,768]{2,1,0:T(8,128)(2,1)}) custom-call(s32[32]{0:T(128)} %len_hbm.3, bf16[2,32,1024]{2,1,0:T(8,128)(2,1)} %get-tuple-element.18.qkv_hbm, bf16[2,32,2,1024,128]{4,3,2,1,0:T(8,128)(2,1)} %k_hbm.3, bf16[2,32,2,1024,128]{4,3,2,1,0:T(8,128)(2,1)} %v_hbm.3), custom_call_target="tpu_custom_call" | custom-call | flops 10000000000 | bytes 67108864 | tf_op jit(solution)/shard_map/attention_0/pallas_call | solution.py:624
  41.4 1.6 %collective-permute-done.refs_4_ = bf16[9,64,896]{2,1,0:T(8,128)(2,1)} collective-permute-done((bf16[9,64,896]{2,1,0:T(8,128)(2,1)}, bf16[9,64,896]{2,1,0:T(8,128)(2,1)}, u32[]{:S(2)}, u32[]{:S(2)}) %collective-permute-start) | collective-permute-done | bytes 1032224 | tf_op jit(solution)/shard_map/ppermute | solution.py:717
  42.9 32.9 %middle.1 = (bf16[2,32,1024]{2,1,0:T(8,128)(2,1)}, bf16[9,64,896]{2,1,0:T(8,128)(2,1)}, bf16[10,64,896]{2,1,0:T(8,128)(2,1)}, bf16[2,192,128]{2,1,0:T(8,128)(2,1)}) custom-call(bf16[2,192,128]{2,1,0:T(8,128)(2,1)} %get-tuple-element.17.refs_0_, bf16[2,32,768]{2,1,0:T(8,128)(2,1)} %get-tuple-element.19.refs_1_, bf16[2,384]{1,0:T(2,128)(2,1)} %refs_2_.3, ...), custom_call_target="tpu_custom_call" | custom-call | tf_op jit(solution)/shard_map/middle/pallas_call | solution.py:702
  75.9 1.2 %collective-permute-start.1 = (bf16[9,64,896]{2,1,0:T(8,128)(2,1)}, bf16[9,64,896]{2,1,0:T(8,128)(2,1)}, u32[]{:S(2)}, u32[]{:S(2)}) collective-permute-start(bf16[9,64,896]{2,1,0:T(8,128)(2,1)} %get-tuple-element.28), channel_id=1, source_target_pairs={{0,2},{2,0},{1,3},{3,1},{4,6},{6,4},{5,7},{7,5}} | collective-permute-start | bytes 3096584 | tf_op jit(solution)/shard_map/ppermute | solution.py:723
  77.1 22.2 %attention_1.1 = (bf16[2,32,2,1024,128]{4,3,2,1,0:T(8,128)(2,1)}, bf16[2,32,2,1024,128]{4,3,2,1,0:T(8,128)(2,1)}, bf16[2,32,768]{2,1,0:T(8,128)(2,1)}) custom-call(s32[32]{0:T(128)} %len_hbm.3, bf16[2,32,1024]{2,1,0:T(8,128)(2,1)} %get-tuple-element.23.qkv_hbm, bf16[2,32,2,1024,128]{4,3,2,1,0:T(8,128)(2,1)} %k_hbm.3, ...), custom_call_target="tpu_custom_call", output_to_operand_aliasing={{0}: (4, {}), {1}: (5, {})} | custom-call | flops 10000000000 | bytes 67108864 | tf_op jit(solution)/shard_map/attention_1/pallas_call | solution.py:624
  99.3 1.2 collective-permute-done.1.zgot_hbm
  100.5 19.3 %end.1 = bf16[192,256]{1,0:T(8,128)(2,1)S(1)} custom-call(bf16[2,192,128]{2,1,0:T(8,128)(2,1)} %get-tuple-element.22.h_hbm, bf16[2,32,768]{2,1,0:T(8,128)(2,1)} %get-tuple-element.26.o_hbm, bf16[10,64,896]{2,1,0:T(8,128)(2,1)} %get-tuple-element.27.zmine_hbm, bf16[9,64,896]{2,1,0:T(8,128)(2,1)} %collective-permute-done.1.zgot_hbm, ...), custom_call_target="tpu_custom_call" | custom-call | tf_op jit(solution)/shard_map/end/pallas_call | solution.py:702
  119.7 0.6 copy.17
Async XLA Ops:
  18.6 24.4 %collective-permute-start = (bf16[9,64,896]{2,1,0:T(8,128)(2,1)}, bf16[9,64,896]{2,1,0:T(8,128)(2,1)}, u32[]{:S(2)}, u32[]{:S(2)}) collective-permute-start(bf16[9,64,896]{2,1,0:T(8,128)(2,1)} %get-tuple-element.21), channel_id=1, source_target_pairs={{0,2},{2,0},{1,3},{3,1},{4,6},{6,4},{5,7},{7,5}} | collective-permute-start | bytes 3096584 | tf_op jit(solution)/shard_map/ppermute | solution.py:717
  75.9 24.6 %collective-permute-start.1 = (bf16[9,64,896]{2,1,0:T(8,128)(2,1)}, bf16[9,64,896]{2,1,0:T(8,128)(2,1)}, u32[]{:S(2)}, u32[]{:S(2)}) collective-permute-start(bf16[9,64,896]{2,1,0:T(8,128)(2,1)} %get-tuple-element.28), channel_id=1, source_target_pairs={{0,2},{2,0},{1,3},{3,1},{4,6},{6,4},{5,7},{7,5}} | collective-permute-start | bytes 3096584 | tf_op jit(solution)/shard_map/ppermute | solution.py:723
